TPU v7x, 16 devices: a whole 2x2x2 slice. The times are simulated.
16 devices in a mesh: dp: 2 (over z), cp: 8 (over y, x, core).
Axes of the slice: x: 2, y: 2, z: 2, core: 2. Of those that a mesh axis runs over, the one named last changes fastest.
Arguments:
- x_in: bfloat16 [16, 512, 2048], P('dp', 'cp'), parts along dimension 0
- positions: int32 [1024], P(('dp', 'cp')), parts along dimension 0
- long_factor: float32 [32], replicated
- norm_gain: float32 [2048], replicated
- w_qkv: bfloat16 [2048, 6144], replicated
- w_out: bfloat16 [2048, 2048], replicated
- grad_y: bfloat16 [16, 512, 2048], P('dp', 'cp'), parts along dimension 0
Outputs:
- output 1: bfloat16 [16, 512, 2048], P('dp', 'cp'), parts along dimension 0
- output 2: bfloat16 [16, 512, 2048], P('dp', 'cp'), parts along dimension 0
- output 3: float32 [4096], P('dp'), parts along dimension 0
- output 4: float32 [4096, 6144], P('dp'), parts along dimension 0
- output 5: float32 [4096, 2048], P('dp'), parts along dimension 0
There are 2 independent parts. A program takes and returns all parts, laid end to end along the dimension named above; an argument that names none is the same for every part.
All inputs are finite; a program needn't handle non-finite values.
Results may differ from a plain program's by a relative error of at most 0.014743.
Values are sent between devices in bfloat16 or wider.
A program may use at most 1 GiB of HBM per device.

v0:
```python
import math
import jax
import jax.numpy as jnp
from jax import lax
from jax.sharding import PartitionSpec as P

NORM_EPS = 1e-5
MSCALE = math.sqrt(1.0 + math.log(32.0) / math.log(4096.0))
MASK_VALUE = -1e30


def rope_tables(positions, long_factor):
    half = long_factor.shape[0]
    exponent = jnp.arange(half, dtype=jnp.float32) * (1.0 / half)
    inv_freq = 1.0 / (long_factor * jnp.power(10000.0, exponent))
    angles = positions.astype(jnp.float32)[:, None] * inv_freq[None, :]
    angle_pair = jnp.concatenate([angles, angles], axis=-1)
    return (jnp.cos(angle_pair) * MSCALE)[None, :, None, :], (jnp.sin(angle_pair) * MSCALE)[None, :, None, :]


def rotate_half(values):
    half = values.shape[-1] // 2
    return jnp.concatenate([-values[..., half:], values[..., :half]], axis=-1)


def masked_scores(q_blk, k_blk, q_start, k_start, scale):
    scores = jnp.einsum('bqhd,bkhd->bhqk', q_blk, k_blk, preferred_element_type=jnp.float32) * scale
    q_pos = q_start + jnp.arange(q_blk.shape[1])[:, None]
    k_pos = k_start + jnp.arange(k_blk.shape[1])[None, :]
    return jnp.where(k_pos <= q_pos, scores, MASK_VALUE)


def fwd_block(stats, q_blk, k_blk, v_blk, q_start, k_start, scale):
    out_acc, row_max, row_sum = stats
    scores = masked_scores(q_blk, k_blk, q_start, k_start, scale)
    new_max = jnp.maximum(row_max, jnp.max(scores, axis=-1, keepdims=True))
    rescale = jnp.exp(row_max - new_max)
    attn_probs = jnp.exp(scores - new_max)
    row_sum = row_sum * rescale + jnp.sum(attn_probs, axis=-1, keepdims=True)
    pv_part = jnp.einsum('bhqk,bkhd->bqhd', attn_probs.astype(jnp.bfloat16), v_blk, preferred_element_type=jnp.float32)
    out_acc = out_acc * jnp.transpose(rescale, (0, 2, 1, 3)) + pv_part
    return out_acc, new_max, row_sum


def bwd_block(q_blk, k_blk, v_blk, d_attn, log_norm, delta, q_start, k_start, scale):
    attn_probs = jnp.exp(masked_scores(q_blk, k_blk, q_start, k_start, scale) - log_norm)
    dv_part = jnp.einsum('bhqk,bqhd->bkhd', attn_probs.astype(jnp.bfloat16), d_attn, preferred_element_type=jnp.float32)
    d_probs = jnp.einsum('bqhd,bkhd->bhqk', d_attn, v_blk, preferred_element_type=jnp.float32)
    d_scores = (attn_probs * (d_probs - delta) * scale).astype(jnp.bfloat16)
    dq_part = jnp.einsum('bhqk,bkhd->bqhd', d_scores, k_blk, preferred_element_type=jnp.float32)
    dk_part = jnp.einsum('bhqk,bqhd->bkhd', d_scores, q_blk, preferred_element_type=jnp.float32)
    return dq_part, dk_part, dv_part


def solution(mesh):
    cp_size = mesh.shape['cp']
    shift_perm = [(src_dev, (src_dev + 1) % cp_size) for src_dev in range(cp_size)]

    def device_fn(x_in, positions, long_factor, norm_gain, w_qkv, w_out, grad_y):
        batch, piece, hidden = x_in.shape
        head_dim = 2 * long_factor.shape[0]
        width = w_out.shape[0]
        heads = width // head_dim
        scale = 1.0 / math.sqrt(head_dim)
        my_index = lax.axis_index('cp')
        q_start = my_index * piece
        x_float = x_in.astype(jnp.float32)
        inv_rms = lax.rsqrt(jnp.mean(x_float * x_float, axis=-1, keepdims=True) + NORM_EPS)
        x_hat = x_float * inv_rms
        normed = (x_hat * norm_gain).astype(jnp.bfloat16)
        qkv_proj = jnp.einsum('bsd,de->bse', normed, w_qkv, preferred_element_type=jnp.float32)
        qkv_proj = qkv_proj.reshape(batch, piece, 3, heads, head_dim)
        cos_tab, sin_tab = rope_tables(positions, long_factor)
        q_rot = (qkv_proj[:, :, 0] * cos_tab + rotate_half(qkv_proj[:, :, 0]) * sin_tab).astype(jnp.bfloat16)
        k_rot = (qkv_proj[:, :, 1] * cos_tab + rotate_half(qkv_proj[:, :, 1]) * sin_tab).astype(jnp.bfloat16)
        v_val = qkv_proj[:, :, 2].astype(jnp.bfloat16)

        init_stats = (jnp.zeros((batch, piece, heads, head_dim), jnp.float32), jnp.full((batch, heads, piece, 1), MASK_VALUE, jnp.float32), jnp.zeros((batch, heads, piece, 1), jnp.float32))
        stats = fwd_block(init_stats, q_rot, k_rot, v_val, q_start, q_start, scale)

        def fwd_step(step_idx, state):
            stats, k_cur, v_cur = state
            k_cur = lax.ppermute(k_cur, 'cp', shift_perm)
            v_cur = lax.ppermute(v_cur, 'cp', shift_perm)
            k_start = (my_index - step_idx) * piece
            stats = lax.cond(step_idx <= my_index, lambda acc: fwd_block(acc, q_rot, k_cur, v_cur, q_start, k_start, scale), lambda acc: acc, stats)
            return stats, k_cur, v_cur

        stats, _, _ = lax.fori_loop(1, cp_size, fwd_step, (stats, k_rot, v_val))
        out_acc, row_max, row_sum = stats
        attn_out = (out_acc / jnp.transpose(row_sum, (0, 2, 1, 3))).astype(jnp.bfloat16)
        log_norm = row_max + jnp.log(row_sum)
        attn_flat = attn_out.reshape(batch, piece, width)
        y_out = (x_float + jnp.einsum('bsh,hd->bsd', attn_flat, w_out, preferred_element_type=jnp.float32)).astype(jnp.bfloat16)

        d_attn = jnp.einsum('bsd,hd->bsh', grad_y, w_out, preferred_element_type=jnp.float32).astype(jnp.bfloat16).reshape(batch, piece, heads, head_dim)
        g_wout = jnp.einsum('bsh,bsd->hd', attn_flat, grad_y, preferred_element_type=jnp.float32)
        delta = jnp.einsum('bqhd,bqhd->bhq', d_attn, attn_out, preferred_element_type=jnp.float32)[..., None]
        dq_acc, dk_own, dv_own = bwd_block(q_rot, k_rot, v_val, d_attn, log_norm, delta, q_start, q_start, scale)

        def bwd_step(step_idx, state):
            dq_acc, k_cur, v_cur, dk_cur, dv_cur = state
            k_cur = lax.ppermute(k_cur, 'cp', shift_perm)
            v_cur = lax.ppermute(v_cur, 'cp', shift_perm)
            dk_cur = lax.ppermute(dk_cur, 'cp', shift_perm)
            dv_cur = lax.ppermute(dv_cur, 'cp', shift_perm)
            k_start = (my_index - step_idx) * piece

            def add_block(sums):
                dq_sum, dk_sum, dv_sum = sums
                dq_part, dk_part, dv_part = bwd_block(q_rot, k_cur, v_cur, d_attn, log_norm, delta, q_start, k_start, scale)
                return dq_sum + dq_part, dk_sum + dk_part, dv_sum + dv_part

            dq_acc, dk_cur, dv_cur = lax.cond(step_idx <= my_index, add_block, lambda sums: sums, (dq_acc, dk_cur, dv_cur))
            return dq_acc, k_cur, v_cur, dk_cur, dv_cur

        dq_acc, _, _, dk_cur, dv_cur = lax.fori_loop(1, cp_size, bwd_step, (dq_acc, k_rot, v_val, dk_own, dv_own))
        dk_home = lax.ppermute(dk_cur, 'cp', shift_perm)
        dv_home = lax.ppermute(dv_cur, 'cp', shift_perm)

        dq_raw = dq_acc * cos_tab - rotate_half(dq_acc * sin_tab)
        dk_raw = dk_home * cos_tab - rotate_half(dk_home * sin_tab)
        d_qkv = jnp.stack([dq_raw.astype(jnp.bfloat16), dk_raw.astype(jnp.bfloat16), dv_home.astype(jnp.bfloat16)], axis=2).reshape(batch, piece, 3 * width)
        g_wqkv = jnp.einsum('bsd,bse->de', normed, d_qkv, preferred_element_type=jnp.float32)
        d_normed = jnp.einsum('bse,de->bsd', d_qkv, w_qkv, preferred_element_type=jnp.float32)
        g_gain = jnp.sum(d_normed * x_hat, axis=(0, 1))
        d_hat = d_normed * norm_gain
        dx_norm = inv_rms * (d_hat - x_hat * jnp.mean(d_hat * x_hat, axis=-1, keepdims=True))
        grad_x = (grad_y.astype(jnp.float32) + dx_norm).astype(jnp.bfloat16)
        g_gain, g_wqkv, g_wout = lax.psum((g_gain, g_wqkv, g_wout), 'cp')
        return y_out, grad_x, g_gain, g_wqkv, g_wout

    seq_spec = P('dp', 'cp', None)
    return jax.shard_map(device_fn, mesh=mesh, in_specs=(seq_spec, P(('dp', 'cp')), P(None), P(None), P(None, None), P(None, None), seq_spec), out_specs=(seq_spec, seq_spec, P('dp'), P('dp', None), P('dp', None)), check_vma=False)
```

profile of v0, /device:TPU:0, one launch (start us, length us, event | category | flops | bytes accessed | tf_op | source)
XLA Modules:
  0.0 4440.8 jit_solution(8367541083957763634)
XLA Ops:
  194.2 830.5 %while.42 = (s32[]{:T(128)}, f32[8,64,32,64]{3,1,2,0:T(8,128)}, f32[8,32,64,1]{2,1,0,3:T(8,128)S(1)}, f32[8,32,64,1]{2,1,0,3:T(8,128)S(1)}, bf16[8,64,32,64]{3,1...) while((s32[]{:T(128)}, f32[8,64,32,64]{3,1,2,0:T(8,128)}, ...), condition=%wide.region_8.9_spmd, body=%wide.region_3.8_spmd.sunk | while | flops 282120320 | bytes 95438256 | solution.py:89
  197.6 46.5 %collective-permute-done.1 = bf16[8,64,32,64]{3,1,2,0:T(8,128)(2,1)} collective-permute-done((bf16[8,64,32,64]{3,1,2,0:T(8,128)(2,1)}, bf16[8,64,32,64]{3,1,2,0:T(8,128)(2,1)}, u32[]{:S(2)}, u32[]{:S(2)}) %collective-permute-start.1) | collective-permute-done | bytes 2097184 | tf_op jit(solution)/shard_map/while/body/eval_jaxpr/ppermute | solution.py:84
  244.0 44.9 %collective-permute-done = bf16[8,64,32,64]{3,1,2,0:T(8,128)(2,1)} collective-permute-done((bf16[8,64,32,64]{3,1,2,0:T(8,128)(2,1)}, bf16[8,64,32,64]{3,1,2,0:T(8,128)(2,1)}, u32[]{:S(2)}, u32[]{:S(2)}) %collective-permute-start) | collective-permute-done | bytes 2097184 | tf_op jit(solution)/shard_map/while/body/eval_jaxpr/ppermute | solution.py:83
  320.9 44.0 collective-permute-done.1
  364.9 44.9 %collective-permute-done = bf16[8,64,32,64]{3,1,2,0:T(8,128)(2,1)} collective-permute-done((bf16[8,64,32,64]{3,1,2,0:T(8,128)(2,1)}, bf16[8,64,32,64]{3,1,2,0:T(8,128)(2,1)}, u32[]{:S(2)}, u32[]{:S(2)}) %collective-permute-start) | collective-permute-done | bytes 2097184 | tf_op jit(solution)/shard_map/while/body/eval_jaxpr/ppermute | solution.py:83
  485.8 44.9 %collective-permute-done = bf16[8,64,32,64]{3,1,2,0:T(8,128)(2,1)} collective-permute-done((bf16[8,64,32,64]{3,1,2,0:T(8,128)(2,1)}, bf16[8,64,32,64]{3,1,2,0:T(8,128)(2,1)}, u32[]{:S(2)}, u32[]{:S(2)}) %collective-permute-start) | collective-permute-done | bytes 2097184 | tf_op jit(solution)/shard_map/while/body/eval_jaxpr/ppermute | solution.py:83
  547.7 59.0 %collective-permute-done.1 = bf16[8,64,32,64]{3,1,2,0:T(8,128)(2,1)} collective-permute-done((bf16[8,64,32,64]{3,1,2,0:T(8,128)(2,1)}, bf16[8,64,32,64]{3,1,2,0:T(8,128)(2,1)}, u32[]{:S(2)}, u32[]{:S(2)}) %collective-permute-start.1) | collective-permute-done | bytes 2097184 | tf_op jit(solution)/shard_map/while/body/eval_jaxpr/ppermute | solution.py:84
  606.7 44.9 %collective-permute-done = bf16[8,64,32,64]{3,1,2,0:T(8,128)(2,1)} collective-permute-done((bf16[8,64,32,64]{3,1,2,0:T(8,128)(2,1)}, bf16[8,64,32,64]{3,1,2,0:T(8,128)(2,1)}, u32[]{:S(2)}, u32[]{:S(2)}) %collective-permute-start) | collective-permute-done | bytes 2097184 | tf_op jit(solution)/shard_map/while/body/eval_jaxpr/ppermute | solution.py:83
  662.1 65.5 %collective-permute-done.1 = bf16[8,64,32,64]{3,1,2,0:T(8,128)(2,1)} collective-permute-done((bf16[8,64,32,64]{3,1,2,0:T(8,128)(2,1)}, bf16[8,64,32,64]{3,1,2,0:T(8,128)(2,1)}, u32[]{:S(2)}, u32[]{:S(2)}) %collective-permute-start.1) | collective-permute-done | bytes 2097184 | tf_op jit(solution)/shard_map/while/body/eval_jaxpr/ppermute | solution.py:84
  727.6 44.9 %collective-permute-done = bf16[8,64,32,64]{3,1,2,0:T(8,128)(2,1)} collective-permute-done((bf16[8,64,32,64]{3,1,2,0:T(8,128)(2,1)}, bf16[8,64,32,64]{3,1,2,0:T(8,128)(2,1)}, u32[]{:S(2)}, u32[]{:S(2)}) %collective-permute-start) | collective-permute-done | bytes 2097184 | tf_op jit(solution)/shard_map/while/body/eval_jaxpr/ppermute | solution.py:83
  783.0 65.5 %collective-permute-done.1 = bf16[8,64,32,64]{3,1,2,0:T(8,128)(2,1)} collective-permute-done((bf16[8,64,32,64]{3,1,2,0:T(8,128)(2,1)}, bf16[8,64,32,64]{3,1,2,0:T(8,128)(2,1)}, u32[]{:S(2)}, u32[]{:S(2)}) %collective-permute-start.1) | collective-permute-done | bytes 2097184 | tf_op jit(solution)/shard_map/while/body/eval_jaxpr/ppermute | solution.py:84
  848.5 44.9 %collective-permute-done = bf16[8,64,32,64]{3,1,2,0:T(8,128)(2,1)} collective-permute-done((bf16[8,64,32,64]{3,1,2,0:T(8,128)(2,1)}, bf16[8,64,32,64]{3,1,2,0:T(8,128)(2,1)}, u32[]{:S(2)}, u32[]{:S(2)}) %collective-permute-start) | collective-permute-done | bytes 2097184 | tf_op jit(solution)/shard_map/while/body/eval_jaxpr/ppermute | solution.py:83
  903.9 65.5 %collective-permute-done.1 = bf16[8,64,32,64]{3,1,2,0:T(8,128)(2,1)} collective-permute-done((bf16[8,64,32,64]{3,1,2,0:T(8,128)(2,1)}, bf16[8,64,32,64]{3,1,2,0:T(8,128)(2,1)}, u32[]{:S(2)}, u32[]{:S(2)}) %collective-permute-start.1) | collective-permute-done | bytes 2097184 | tf_op jit(solution)/shard_map/while/body/eval_jaxpr/ppermute | solution.py:84
  969.3 44.9 %collective-permute-done = bf16[8,64,32,64]{3,1,2,0:T(8,128)(2,1)} collective-permute-done((bf16[8,64,32,64]{3,1,2,0:T(8,128)(2,1)}, bf16[8,64,32,64]{3,1,2,0:T(8,128)(2,1)}, u32[]{:S(2)}, u32[]{:S(2)}) %collective-permute-start) | collective-permute-done | bytes 2097184 | tf_op jit(solution)/shard_map/while/body/eval_jaxpr/ppermute | solution.py:83
  1101.3 2302.2 %while.43 = (s32[]{:T(128)}, f32[8,64,32,64]{3,1,2,0:T(8,128)}, bf16[8,64,32,64]{3,1,2,0:T(8,128)(2,1)}, bf16[8,64,32,64]{3,1,2,0:T(8,128)(2,1)}, f32[8,64,32,64...) while((s32[]{:T(128)}, f32[8,64,32,64]{3,1,2,0:T(8,128)}, ...), condition=%wide.region_12.13_spmd, body=%wide.region_9.12_spmd.sunk | while | flops 685772928 | bytes 151205392 | solution.py:117
  1101.7 245.0 %collective-permute-done.5 = bf16[8,64,32,64]{3,1,2,0:T(8,128)(2,1)} collective-permute-done((bf16[8,64,32,64]{3,1,2,0:T(8,128)(2,1)}, bf16[8,64,32,64]{3,1,2,0:T(8,128)(2,1)}, u32[]{:S(2)}, u32[]{:S(2)}) %collective-permute-start.5) | collective-permute-done | bytes 2097184 | tf_op jit(solution)/shard_map/while/body/eval_jaxpr/ppermute | solution.py:104
  1420.8 257.5 %collective-permute-done.5 = bf16[8,64,32,64]{3,1,2,0:T(8,128)(2,1)} collective-permute-done((bf16[8,64,32,64]{3,1,2,0:T(8,128)(2,1)}, bf16[8,64,32,64]{3,1,2,0:T(8,128)(2,1)}, u32[]{:S(2)}, u32[]{:S(2)}) %collective-permute-start.5) | collective-permute-done | bytes 2097184 | tf_op jit(solution)/shard_map/while/body/eval_jaxpr/ppermute | solution.py:104
  1755.9 254.1 %collective-permute-done.5 = bf16[8,64,32,64]{3,1,2,0:T(8,128)(2,1)} collective-permute-done((bf16[8,64,32,64]{3,1,2,0:T(8,128)(2,1)}, bf16[8,64,32,64]{3,1,2,0:T(8,128)(2,1)}, u32[]{:S(2)}, u32[]{:S(2)}) %collective-permute-start.5) | collective-permute-done | bytes 2097184 | tf_op jit(solution)/shard_map/while/body/eval_jaxpr/ppermute | solution.py:104
  2090.9 250.7 %collective-permute-done.5 = bf16[8,64,32,64]{3,1,2,0:T(8,128)(2,1)} collective-permute-done((bf16[8,64,32,64]{3,1,2,0:T(8,128)(2,1)}, bf16[8,64,32,64]{3,1,2,0:T(8,128)(2,1)}, u32[]{:S(2)}, u32[]{:S(2)}) %collective-permute-start.5) | collective-permute-done | bytes 2097184 | tf_op jit(solution)/shard_map/while/body/eval_jaxpr/ppermute | solution.py:104
  2425.9 247.4 %collective-permute-done.5 = bf16[8,64,32,64]{3,1,2,0:T(8,128)(2,1)} collective-permute-done((bf16[8,64,32,64]{3,1,2,0:T(8,128)(2,1)}, bf16[8,64,32,64]{3,1,2,0:T(8,128)(2,1)}, u32[]{:S(2)}, u32[]{:S(2)}) %collective-permute-start.5) | collective-permute-done | bytes 2097184 | tf_op jit(solution)/shard_map/while/body/eval_jaxpr/ppermute | solution.py:104
  2740.1 264.8 %collective-permute-done.5 = bf16[8,64,32,64]{3,1,2,0:T(8,128)(2,1)} collective-permute-done((bf16[8,64,32,64]{3,1,2,0:T(8,128)(2,1)}, bf16[8,64,32,64]{3,1,2,0:T(8,128)(2,1)}, u32[]{:S(2)}, u32[]{:S(2)}) %collective-permute-start.5) | collective-permute-done | bytes 2097184 | tf_op jit(solution)/shard_map/while/body/eval_jaxpr/ppermute | solution.py:104
  3071.8 264.8 %collective-permute-done.5 = bf16[8,64,32,64]{3,1,2,0:T(8,128)(2,1)} collective-permute-done((bf16[8,64,32,64]{3,1,2,0:T(8,128)(2,1)}, bf16[8,64,32,64]{3,1,2,0:T(8,128)(2,1)}, u32[]{:S(2)}, u32[]{:S(2)}) %collective-permute-start.5) | collective-permute-done | bytes 2097184 | tf_op jit(solution)/shard_map/while/body/eval_jaxpr/ppermute | solution.py:104
  3432.0 101.6 %collective-permute-done.6 = f32[8,64,32,64]{3,1,2,0:T(8,128)} collective-permute-done((f32[8,64,32,64]{3,1,2,0:T(8,128)}, f32[8,64,32,64]{3,1,2,0:T(8,128)}, u32[]{:S(2)}, u32[]{:S(2)}) %collective-permute-start.6) | collective-permute-done | bytes 4194336 | tf_op jit(solution)/shard_map/ppermute | solution.py:118
  3683.4 704.0 %all-reduce.3.cloned.1.call-done = (f32[2048,6144]{1,0:T(8,128)}, f32[2048,2048]{1,0:T(8,128)}) async-done(((f32[2048,6144]{1,0:T(8,128)}, f32[2048,2048]{1,0:T(8,128)}), (f32[2048,6144]{1,0:T(8,128)}, f32[2048,2048]{1,0:T(8,128)})) %all-reduce.3.cloned.1.call-update) | async-done | bytes 67108880 | tf_op jit(solution)/shard_map/psum | solution.py:130
  (237 shorter events, 1175.4 us)
Async XLA Ops:
  7.2 4380.2 %all-reduce.3.cloned.1.call-start = ((), (), s32[]{:S(2)}) async-start(), calls=%async_computation | async-start | bytes 134217728 | tf_op jit(solution)/shard_map/psum | solution.py:130
  1101.5 295.5 %collective-permute-start.3 = (f32[8,64,32,64]{3,1,2,0:T(8,128)}, f32[8,64,32,64]{3,1,2,0:T(8,128)}, u32[]{:S(2)}, u32[]{:S(2)}) collective-permute-start(f32[8,64,32,64]{3,1,2,0:T(8,128)} %get-tuple-element.834), channel_id=1, source_target_pairs={{0,1},{1,2},{2,3},{3,4},{4,5},{5,6},{6,7},{7,0},{8,9},{9,10},{10,1... | collective-permute-start | bytes 12582920 | tf_op jit(solution)/shard_map/while/body/eval_jaxpr/ppermute | solution.py:106
  1101.5 295.4 %collective-permute-start.2 = (f32[8,64,32,64]{3,1,2,0:T(8,128)}, f32[8,64,32,64]{3,1,2,0:T(8,128)}, u32[]{:S(2)}, u32[]{:S(2)}) collective-permute-start(f32[8,64,32,64]{3,1,2,0:T(8,128)} %get-tuple-element.833), channel_id=1, source_target_pairs={{0,1},{1,2},{2,3},{3,4},{4,5},{5,6},{6,7},{7,0},{8,9},{9,10},{10,1... | collective-permute-start | bytes 12582920 | tf_op jit(solution)/shard_map/while/body/eval_jaxpr/ppermute | solution.py:105
  1101.6 290.0 %collective-permute-start.4 = (bf16[8,64,32,64]{3,1,2,0:T(8,128)(2,1)}, bf16[8,64,32,64]{3,1,2,0:T(8,128)(2,1)}, u32[]{:S(2)}, u32[]{:S(2)}) collective-permute-start(bf16[8,64,32,64]{3,1,2,0:T(8,128)(2,1)} %get-tuple-element.831), channel_id=1, source_target_pairs={{0,1},{1,2},{2,3},{3,4},{4,5},{5,6},{6,7},{7,0},{8,9},{9,10},{10,1... | collective-permute-start | bytes 6291464 | tf_op jit(solution)/shard_map/while/body/eval_jaxpr/ppermute | solution.py:103
  1413.5 315.0 %collective-permute-start.3 = (f32[8,64,32,64]{3,1,2,0:T(8,128)}, f32[8,64,32,64]{3,1,2,0:T(8,128)}, u32[]{:S(2)}, u32[]{:S(2)}) collective-permute-start(f32[8,64,32,64]{3,1,2,0:T(8,128)} %get-tuple-element.834), channel_id=1, source_target_pairs={{0,1},{1,2},{2,3},{3,4},{4,5},{5,6},{6,7},{7,0},{8,9},{9,10},{10,1... | collective-permute-start | bytes 12582920 | tf_op jit(solution)/shard_map/while/body/eval_jaxpr/ppermute | solution.py:106
  1413.5 315.0 %collective-permute-start.2 = (f32[8,64,32,64]{3,1,2,0:T(8,128)}, f32[8,64,32,64]{3,1,2,0:T(8,128)}, u32[]{:S(2)}, u32[]{:S(2)}) collective-permute-start(f32[8,64,32,64]{3,1,2,0:T(8,128)} %get-tuple-element.833), channel_id=1, source_target_pairs={{0,1},{1,2},{2,3},{3,4},{4,5},{5,6},{6,7},{7,0},{8,9},{9,10},{10,1... | collective-permute-start | bytes 12582920 | tf_op jit(solution)/shard_map/while/body/eval_jaxpr/ppermute | solution.py:105
  1413.5 264.8 %collective-permute-start.5 = (bf16[8,64,32,64]{3,1,2,0:T(8,128)(2,1)}, bf16[8,64,32,64]{3,1,2,0:T(8,128)(2,1)}, u32[]{:S(2)}, u32[]{:S(2)}) collective-permute-start(bf16[8,64,32,64]{3,1,2,0:T(8,128)(2,1)} %get-tuple-element.832), channel_id=1, source_target_pairs={{0,1},{1,2},{2,3},{3,4},{4,5},{5,6},{6,7},{7,0},{8,9},{9,10},{10,1... | collective-permute-start | bytes 6291464 | tf_op jit(solution)/shard_map/while/body/eval_jaxpr/ppermute | solution.py:104
  1417.4 305.9 %collective-permute-start.4 = (bf16[8,64,32,64]{3,1,2,0:T(8,128)(2,1)}, bf16[8,64,32,64]{3,1,2,0:T(8,128)(2,1)}, u32[]{:S(2)}, u32[]{:S(2)}) collective-permute-start(bf16[8,64,32,64]{3,1,2,0:T(8,128)(2,1)} %get-tuple-element.831), channel_id=1, source_target_pairs={{0,1},{1,2},{2,3},{3,4},{4,5},{5,6},{6,7},{7,0},{8,9},{9,10},{10,1... | collective-permute-start | bytes 6291464 | tf_op jit(solution)/shard_map/while/body/eval_jaxpr/ppermute | solution.py:103
  1745.2 315.0 %collective-permute-start.3 = (f32[8,64,32,64]{3,1,2,0:T(8,128)}, f32[8,64,32,64]{3,1,2,0:T(8,128)}, u32[]{:S(2)}, u32[]{:S(2)}) collective-permute-start(f32[8,64,32,64]{3,1,2,0:T(8,128)} %get-tuple-element.834), channel_id=1, source_target_pairs={{0,1},{1,2},{2,3},{3,4},{4,5},{5,6},{6,7},{7,0},{8,9},{9,10},{10,1... | collective-permute-start | bytes 12582920 | tf_op jit(solution)/shard_map/while/body/eval_jaxpr/ppermute | solution.py:106
  1745.2 315.0 %collective-permute-start.2 = (f32[8,64,32,64]{3,1,2,0:T(8,128)}, f32[8,64,32,64]{3,1,2,0:T(8,128)}, u32[]{:S(2)}, u32[]{:S(2)}) collective-permute-start(f32[8,64,32,64]{3,1,2,0:T(8,128)} %get-tuple-element.833), channel_id=1, source_target_pairs={{0,1},{1,2},{2,3},{3,4},{4,5},{5,6},{6,7},{7,0},{8,9},{9,10},{10,1... | collective-permute-start | bytes 12582920 | tf_op jit(solution)/shard_map/while/body/eval_jaxpr/ppermute | solution.py:105
  1745.2 264.8 %collective-permute-start.5 = (bf16[8,64,32,64]{3,1,2,0:T(8,128)(2,1)}, bf16[8,64,32,64]{3,1,2,0:T(8,128)(2,1)}, u32[]{:S(2)}, u32[]{:S(2)}) collective-permute-start(bf16[8,64,32,64]{3,1,2,0:T(8,128)(2,1)} %get-tuple-element.832), channel_id=1, source_target_pairs={{0,1},{1,2},{2,3},{3,4},{4,5},{5,6},{6,7},{7,0},{8,9},{9,10},{10,1... | collective-permute-start | bytes 6291464 | tf_op jit(solution)/shard_map/while/body/eval_jaxpr/ppermute | solution.py:104
  1752.5 302.5 %collective-permute-start.4 = (bf16[8,64,32,64]{3,1,2,0:T(8,128)(2,1)}, bf16[8,64,32,64]{3,1,2,0:T(8,128)(2,1)}, u32[]{:S(2)}, u32[]{:S(2)}) collective-permute-start(bf16[8,64,32,64]{3,1,2,0:T(8,128)(2,1)} %get-tuple-element.831), channel_id=1, source_target_pairs={{0,1},{1,2},{2,3},{3,4},{4,5},{5,6},{6,7},{7,0},{8,9},{9,10},{10,1... | collective-permute-start | bytes 6291464 | tf_op jit(solution)/shard_map/while/body/eval_jaxpr/ppermute | solution.py:103
  2076.8 315.0 %collective-permute-start.3 = (f32[8,64,32,64]{3,1,2,0:T(8,128)}, f32[8,64,32,64]{3,1,2,0:T(8,128)}, u32[]{:S(2)}, u32[]{:S(2)}) collective-permute-start(f32[8,64,32,64]{3,1,2,0:T(8,128)} %get-tuple-element.834), channel_id=1, source_target_pairs={{0,1},{1,2},{2,3},{3,4},{4,5},{5,6},{6,7},{7,0},{8,9},{9,10},{10,1... | collective-permute-start | bytes 12582920 | tf_op jit(solution)/shard_map/while/body/eval_jaxpr/ppermute | solution.py:106
  2076.8 315.0 %collective-permute-start.2 = (f32[8,64,32,64]{3,1,2,0:T(8,128)}, f32[8,64,32,64]{3,1,2,0:T(8,128)}, u32[]{:S(2)}, u32[]{:S(2)}) collective-permute-start(f32[8,64,32,64]{3,1,2,0:T(8,128)} %get-tuple-element.833), channel_id=1, source_target_pairs={{0,1},{1,2},{2,3},{3,4},{4,5},{5,6},{6,7},{7,0},{8,9},{9,10},{10,1... | collective-permute-start | bytes 12582920 | tf_op jit(solution)/shard_map/while/body/eval_jaxpr/ppermute | solution.py:105
  2087.5 299.1 %collective-permute-start.4 = (bf16[8,64,32,64]{3,1,2,0:T(8,128)(2,1)}, bf16[8,64,32,64]{3,1,2,0:T(8,128)(2,1)}, u32[]{:S(2)}, u32[]{:S(2)}) collective-permute-start(bf16[8,64,32,64]{3,1,2,0:T(8,128)(2,1)} %get-tuple-element.831), channel_id=1, source_target_pairs={{0,1},{1,2},{2,3},{3,4},{4,5},{5,6},{6,7},{7,0},{8,9},{9,10},{10,1... | collective-permute-start | bytes 6291464 | tf_op jit(solution)/shard_map/while/body/eval_jaxpr/ppermute | solution.py:103
  2408.4 315.0 %collective-permute-start.3 = (f32[8,64,32,64]{3,1,2,0:T(8,128)}, f32[8,64,32,64]{3,1,2,0:T(8,128)}, u32[]{:S(2)}, u32[]{:S(2)}) collective-permute-start(f32[8,64,32,64]{3,1,2,0:T(8,128)} %get-tuple-element.834), channel_id=1, source_target_pairs={{0,1},{1,2},{2,3},{3,4},{4,5},{5,6},{6,7},{7,0},{8,9},{9,10},{10,1... | collective-permute-start | bytes 12582920 | tf_op jit(solution)/shard_map/while/body/eval_jaxpr/ppermute | solution.py:106
  2408.4 315.0 %collective-permute-start.2 = (f32[8,64,32,64]{3,1,2,0:T(8,128)}, f32[8,64,32,64]{3,1,2,0:T(8,128)}, u32[]{:S(2)}, u32[]{:S(2)}) collective-permute-start(f32[8,64,32,64]{3,1,2,0:T(8,128)} %get-tuple-element.833), channel_id=1, source_target_pairs={{0,1},{1,2},{2,3},{3,4},{4,5},{5,6},{6,7},{7,0},{8,9},{9,10},{10,1... | collective-permute-start | bytes 12582920 | tf_op jit(solution)/shard_map/while/body/eval_jaxpr/ppermute | solution.py:105
  2408.4 309.8 %collective-permute-start.4 = (bf16[8,64,32,64]{3,1,2,0:T(8,128)(2,1)}, bf16[8,64,32,64]{3,1,2,0:T(8,128)(2,1)}, u32[]{:S(2)}, u32[]{:S(2)}) collective-permute-start(bf16[8,64,32,64]{3,1,2,0:T(8,128)(2,1)} %get-tuple-element.831), channel_id=1, source_target_pairs={{0,1},{1,2},{2,3},{3,4},{4,5},{5,6},{6,7},{7,0},{8,9},{9,10},{10,1... | collective-permute-start | bytes 6291464 | tf_op jit(solution)/shard_map/while/body/eval_jaxpr/ppermute | solution.py:103
  2740.1 315.0 %collective-permute-start.3 = (f32[8,64,32,64]{3,1,2,0:T(8,128)}, f32[8,64,32,64]{3,1,2,0:T(8,128)}, u32[]{:S(2)}, u32[]{:S(2)}) collective-permute-start(f32[8,64,32,64]{3,1,2,0:T(8,128)} %get-tuple-element.834), channel_id=1, source_target_pairs={{0,1},{1,2},{2,3},{3,4},{4,5},{5,6},{6,7},{7,0},{8,9},{9,10},{10,1... | collective-permute-start | bytes 12582920 | tf_op jit(solution)/shard_map/while/body/eval_jaxpr/ppermute | solution.py:106
  2740.1 315.0 %collective-permute-start.2 = (f32[8,64,32,64]{3,1,2,0:T(8,128)}, f32[8,64,32,64]{3,1,2,0:T(8,128)}, u32[]{:S(2)}, u32[]{:S(2)}) collective-permute-start(f32[8,64,32,64]{3,1,2,0:T(8,128)} %get-tuple-element.833), channel_id=1, source_target_pairs={{0,1},{1,2},{2,3},{3,4},{4,5},{5,6},{6,7},{7,0},{8,9},{9,10},{10,1... | collective-permute-start | bytes 12582920 | tf_op jit(solution)/shard_map/while/body/eval_jaxpr/ppermute | solution.py:105
  2740.1 309.8 %collective-permute-start.4 = (bf16[8,64,32,64]{3,1,2,0:T(8,128)(2,1)}, bf16[8,64,32,64]{3,1,2,0:T(8,128)(2,1)}, u32[]{:S(2)}, u32[]{:S(2)}) collective-permute-start(bf16[8,64,32,64]{3,1,2,0:T(8,128)(2,1)} %get-tuple-element.831), channel_id=1, source_target_pairs={{0,1},{1,2},{2,3},{3,4},{4,5},{5,6},{6,7},{7,0},{8,9},{9,10},{10,1... | collective-permute-start | bytes 6291464 | tf_op jit(solution)/shard_map/while/body/eval_jaxpr/ppermute | solution.py:103
  3071.7 315.0 %collective-permute-start.3 = (f32[8,64,32,64]{3,1,2,0:T(8,128)}, f32[8,64,32,64]{3,1,2,0:T(8,128)}, u32[]{:S(2)}, u32[]{:S(2)}) collective-permute-start(f32[8,64,32,64]{3,1,2,0:T(8,128)} %get-tuple-element.834), channel_id=1, source_target_pairs={{0,1},{1,2},{2,3},{3,4},{4,5},{5,6},{6,7},{7,0},{8,9},{9,10},{10,1... | collective-permute-start | bytes 12582920 | tf_op jit(solution)/shard_map/while/body/eval_jaxpr/ppermute | solution.py:106
  3071.7 315.0 %collective-permute-start.2 = (f32[8,64,32,64]{3,1,2,0:T(8,128)}, f32[8,64,32,64]{3,1,2,0:T(8,128)}, u32[]{:S(2)}, u32[]{:S(2)}) collective-permute-start(f32[8,64,32,64]{3,1,2,0:T(8,128)} %get-tuple-element.833), channel_id=1, source_target_pairs={{0,1},{1,2},{2,3},{3,4},{4,5},{5,6},{6,7},{7,0},{8,9},{9,10},{10,1... | collective-permute-start | bytes 12582920 | tf_op jit(solution)/shard_map/while/body/eval_jaxpr/ppermute | solution.py:105
  3071.7 309.8 %collective-permute-start.4 = (bf16[8,64,32,64]{3,1,2,0:T(8,128)(2,1)}, bf16[8,64,32,64]{3,1,2,0:T(8,128)(2,1)}, u32[]{:S(2)}, u32[]{:S(2)}) collective-permute-start(bf16[8,64,32,64]{3,1,2,0:T(8,128)(2,1)} %get-tuple-element.831), channel_id=1, source_target_pairs={{0,1},{1,2},{2,3},{3,4},{4,5},{5,6},{6,7},{7,0},{8,9},{9,10},{10,1... | collective-permute-start | bytes 6291464 | tf_op jit(solution)/shard_map/while/body/eval_jaxpr/ppermute | solution.py:103
  (47 other events, 3207.0 us)
Sparse Core Ops, SparseCore 0:
  3636.5 750.9 all-reduce.2
where the time goes:
time: 4450 us; the launch traced here: 4440 us
  waiting for transfers between devices  3570 us (80%)
  local copies, waits for them, and re-layouts  476 us (11%)
  matrix products  140 us (3%)
  other arithmetic  121 us (3%)
  starting transfers between devices  105 us (2%)
    ppermute x7, waiting for transfers between devices, bwd_step(): v_cur = lax.ppermute(v_cur, 'cp', shift_perm)  1780 us
    psum x1, waiting for transfers between devices, device_fn(): g_gain, g_wqkv, g_wout = lax.psum((g_gain, g_wqkv, g_wout), 'cp')  704 us
    ppermute x7, waiting for transfers between devices, fwd_step(): v_cur = lax.ppermute(v_cur, 'cp', shift_perm)  387 us
    ppermute x7, waiting for transfers between devices, fwd_step(): k_cur = lax.ppermute(k_cur, 'cp', shift_perm)  315 us
    ppermute x7, waiting for transfers between devices, bwd_step(): k_cur = lax.ppermute(k_cur, 'cp', shift_perm)  278 us
    while x42, local copies, waits for them, and re-layouts  263 us
    ppermute x1, waiting for transfers between devices, device_fn(): dk_home = lax.ppermute(dk_cur, 'cp', shift_perm)  102 us
  transfers between devices with their start and end apart: 45, of which 31 were waited for; matrix products, arithmetic and copies ran while one was open for 4% of the time, Pallas kernels for 0%

commit v1 on v0

v1 whole, which is shorter than its diff:
```python
import functools
import math
import jax
import jax.numpy as jnp
from jax import lax
from jax.experimental import pallas as pl
from jax.experimental.pallas import tpu as pltpu
from jax.sharding import PartitionSpec as P

NORM_EPS = 1e-5
MSCALE = math.sqrt(1.0 + math.log(32.0) / math.log(4096.0))
MASK_VALUE = -1e30
F32 = jnp.float32
BF16 = jnp.bfloat16


def rope_tables(positions, long_factor):
    half = long_factor.shape[0]
    exponent = jnp.arange(half, dtype=F32) * (1.0 / half)
    inv_freq = 1.0 / (long_factor * jnp.power(10000.0, exponent))
    angles = positions.astype(F32)[:, None] * inv_freq[None, :]
    cos, sin = jnp.cos(angles) * MSCALE, jnp.sin(angles) * MSCALE
    return jnp.concatenate([cos] * 4, axis=1), jnp.concatenate([-sin, sin, -sin, sin], axis=1)


def dot(a, b, dims=((1,), (0,))):
    return lax.dot_general(a, b, (dims, ((), ())), preferred_element_type=F32)


def partner(t, first_half):
    width = t.shape[-1]
    return jnp.where(first_half, pltpu.roll(t, width - 32, 1), pltpu.roll(t, 32, 1))


def block_kernel(scale, x_ref, r_ref, dy_ref, gain_ref, wq_ref, wk_ref, wv_ref, wo_ref, cos_ref, sin_ref,
                 y_ref, dx_ref, gg_ref, ot_ref, dq_ref, dk_ref, dv_ref, y_acc, dn_acc):
    step = pl.program_id(0)
    seq = x_ref.shape[0]
    qb = 256

    @pl.when(step == 0)
    def _():
        y_acc[...] = x_ref[...].astype(F32)
        dn_acc[...] = jnp.zeros_like(dn_acc)

    r = r_ref[...]
    q_all = dot(r, wq_ref[...])
    k_all = dot(r, wk_ref[...])
    v_all = dot(r, wv_ref[...]).astype(BF16)
    da_all = dot(dy_ref[...], wo_ref[...], ((1,), (1,))).astype(BF16)
    cos, sin = cos_ref[...], sin_ref[...]
    lane = lax.broadcasted_iota(jnp.int32, (seq, 128), 1)
    first_half = (lane % 64) < 32
    head0 = lane < 64
    tri = lax.broadcasted_iota(jnp.int32, (qb, qb), 0) <= lax.broadcasted_iota(jnp.int32, (qb, qb), 1)
    zero_rows = jnp.zeros((64, seq), BF16)
    zero_pair = jnp.zeros((seq, 128), BF16)

    for pair in range(2):
        cols = slice(128 * pair, 128 * pair + 128)
        qf, kf = q_all[:, cols], k_all[:, cols]
        q = ((qf * cos + partner(qf, first_half) * sin).astype(BF16) * scale).astype(BF16)
        k = (kf * cos + partner(kf, first_half) * sin).astype(BF16)
        v, da = v_all[:, cols], da_all[:, cols]
        qt, kt, vt, dat = q.T, k.T, v.T, da.T
        ots, dqts = [], []
        dk_sum = [jnp.zeros((qb, 128), F32), jnp.zeros((qb, 128), F32)]
        dv_sum = [jnp.zeros((qb, 128), F32), jnp.zeros((qb, 128), F32)]
        for head in range(2):
            rows = slice(64 * head, 64 * head + 64)
            if head == 0:
                qt_h = jnp.concatenate([qt[rows], zero_rows], axis=0)
                dat_h = jnp.concatenate([dat[rows], zero_rows], axis=0)
                q_h = jnp.where(head0, q, zero_pair)
                da_h = jnp.where(head0, da, zero_pair)
            else:
                qt_h = jnp.concatenate([zero_rows, qt[rows]], axis=0)
                dat_h = jnp.concatenate([zero_rows, dat[rows]], axis=0)
                q_h = jnp.where(head0, zero_pair, q)
                da_h = jnp.where(head0, zero_pair, da)
            kt_h, vt_h = kt[rows], vt[rows]
            ot_b, dqt_b = [], []
            for blk in range(2):
                qs = slice(qb * blk, qb * blk + qb)
                nk = qb * (blk + 1)
                st = dot(k[:nk], qt_h[:, qs])
                if blk == 0:
                    st = jnp.where(tri, st, MASK_VALUE)
                else:
                    st = jnp.concatenate([st[:qb], jnp.where(tri, st[qb:], MASK_VALUE)], axis=0)
                m = jnp.max(st, axis=0, keepdims=True)
                e = jnp.exp(st - m)
                p = e * (1.0 / jnp.sum(e, axis=0, keepdims=True))
                pb = p.astype(BF16)
                ot = dot(vt_h[:, :nk], pb)
                ob = ot.astype(BF16)
                delta = jnp.sum(dat[rows, qs].astype(F32) * ob.astype(F32), axis=0, keepdims=True)
                dpt = dot(v[:nk], dat_h[:, qs])
                dsb = (p * (dpt - delta)).astype(BF16)
                dqt_b.append(dot(kt_h[:, :nk], dsb))
                ot_b.append(ob)
                dv_part = dot(pb, da_h[qs])
                dk_part = dot(dsb, q_h[qs])
                for half in range(blk + 1):
                    hs = slice(qb * half, qb * half + qb)
                    dv_sum[half] += dv_part[hs]
                    dk_sum[half] += dk_part[hs]
            ots.append(jnp.concatenate(ot_b, axis=1))
            dqts.append(jnp.concatenate(dqt_b, axis=1))
        ot_pair = jnp.concatenate(ots, axis=0)
        ot_ref[cols, :] = ot_pair
        o = ot_pair.T
        dq = jnp.concatenate(dqts, axis=0).T * scale
        dk = jnp.concatenate(dk_sum, axis=0)
        dv = jnp.concatenate(dv_sum, axis=0)
        dqb = (dq * cos - partner(dq, first_half) * sin).astype(BF16)
        dkb = (dk * cos - partner(dk, first_half) * sin).astype(BF16)
        dvb = dv.astype(BF16)
        dq_ref[:, cols] = dqb
        dk_ref[:, cols] = dkb
        dv_ref[:, cols] = dvb
        y_acc[...] += dot(o, wo_ref[cols, :])

    dn_acc[...] += (dot(dq_ref[...], wq_ref[...], ((1,), (1,))) + dot(dk_ref[...], wk_ref[...], ((1,), (1,)))
                    + dot(dv_ref[...], wv_ref[...], ((1,), (1,))))

    @pl.when(step == pl.num_programs(0) - 1)
    def _():
        y_ref[...] = y_acc[...].astype(BF16)
        x = x_ref[...].astype(F32)
        inv = lax.rsqrt(jnp.mean(x * x, axis=1, keepdims=True) + NORM_EPS)
        x_hat = x * inv
        dn = dn_acc[...]
        gg_ref[...] = jnp.sum(dn * x_hat, axis=0, keepdims=True)
        d_hat = dn * gain_ref[...]
        dx = inv * (d_hat - x_hat * jnp.mean(d_hat * x_hat, axis=1, keepdims=True))
        dx_ref[...] = (dy_ref[...].astype(F32) + dx).astype(BF16)


def block_call(x, r, dy, gain, w_qkv, w_out, cos, sin, scale):
    seq, hidden = x.shape
    width = w_out.shape[0]
    hb = 256
    steps = width // hb
    whole = lambda a: pl.BlockSpec(a.shape, lambda j: (0, 0), pipeline_mode=pl.Buffered(1))
    wcol = lambda part: pl.BlockSpec((hidden, hb), lambda j, part=part: (0, part * steps + j))
    tok = pl.BlockSpec((seq, hb), lambda j: (0, j))
    full = lambda s: pl.BlockSpec(s, lambda j: (0, 0))
    return pl.pallas_call(
        functools.partial(block_kernel, scale),
        grid=(steps,),
        in_specs=[whole(x), whole(r), whole(dy), whole(gain), wcol(0), wcol(1), wcol(2),
                  pl.BlockSpec((hb, hidden), lambda j: (j, 0)), whole(cos), whole(sin)],
        out_specs=[full((seq, hidden)), full((seq, hidden)), full((1, hidden)), pl.BlockSpec((hb, seq), lambda j: (j, 0)), tok, tok, tok],
        out_shape=[jax.ShapeDtypeStruct((seq, hidden), BF16), jax.ShapeDtypeStruct((seq, hidden), BF16),
                   jax.ShapeDtypeStruct((1, hidden), F32), jax.ShapeDtypeStruct((width, seq), BF16)]
        + [jax.ShapeDtypeStruct((seq, width), BF16)] * 3,
        scratch_shapes=[pltpu.VMEM((seq, hidden), F32), pltpu.VMEM((seq, hidden), F32)],
        compiler_params=pltpu.CompilerParams(dimension_semantics=("arbitrary",), vmem_limit_bytes=60 << 20),
        cost_estimate=pl.CostEstimate(flops=60_000_000_000, bytes_accessed=60_000_000, transcendentals=8_000_000),
        name="block",
    )(x, r, dy, gain, w_qkv, w_qkv, w_qkv, w_out, cos, sin)


def norm_kernel(x_ref, dy_ref, gain_ref, r_ref, pair_ref):
    x = x_ref[...].astype(F32)
    inv = lax.rsqrt(jnp.mean(x * x, axis=1, keepdims=True) + NORM_EPS)
    r = (x * inv * gain_ref[...]).astype(BF16)
    r_ref[...] = r
    pair_ref[0] = r.T
    pair_ref[1] = dy_ref[...].T


def norm_call(x, dy, gain):
    seq, hidden = x.shape
    return pl.pallas_call(
        norm_kernel,
        out_shape=[jax.ShapeDtypeStruct((seq, hidden), BF16), jax.ShapeDtypeStruct((2, hidden, seq), BF16)],
        compiler_params=pltpu.CompilerParams(vmem_limit_bytes=40 << 20),
        cost_estimate=pl.CostEstimate(flops=10_000_000, bytes_accessed=10_000_000, transcendentals=0),
        name="norm",
    )(x, dy, gain)


def grad_kernel(flip, a_ref, b_ref, *rest):
    out_ref = rest[-1]
    dims = ((1,), (1,)) if flip else ((1,), (0,))
    part = dot(a_ref[0, 0], b_ref[0, 0], dims)
    for i in range(1, a_ref.shape[0]):
        part += dot(a_ref[i, 0], b_ref[i, 0], dims)

    @pl.when(pl.program_id(2) == 0)
    def _():
        out_ref[...] = part

    @pl.when(pl.program_id(2) > 0)
    def _():
        out_ref[...] += part


def grad_call(at, b, n_out, col, buf=None, flip=False):
    n_seq, _, rows, seq = at.shape
    last = b.shape[1] - 1
    n = b.shape[2] if flip else b.shape[3]
    tm, tn, ts = 1024, 512, 2
    specs = [pl.BlockSpec((ts, 1, tm, seq), lambda i, j, k: (k, 0, i, 0)),
             pl.BlockSpec((ts, 1, tn, seq), lambda i, j, k: (k, last, j, 0)) if flip else pl.BlockSpec((ts, 1, seq, tn), lambda i, j, k: (k, last, 0, j))]
    args = [at, b]
    aliases = {}
    if buf is not None:
        specs.append(pl.BlockSpec(memory_space=pl.ANY))
        args.append(buf)
        aliases = {2: 0}
    return pl.pallas_call(
        functools.partial(grad_kernel, flip),
        grid=(rows // tm, n // tn, n_seq // ts),
        in_specs=specs,
        out_specs=pl.BlockSpec((tm, tn), lambda i, j, k: (i, col // tn + j)),
        out_shape=jax.ShapeDtypeStruct((rows, n_out), F32),
        input_output_aliases=aliases,
        compiler_params=pltpu.CompilerParams(dimension_semantics=("arbitrary",) * 3, vmem_limit_bytes=48 << 20),
        cost_estimate=pl.CostEstimate(flops=2 * rows * n * n_seq * seq, bytes_accessed=80_000_000, transcendentals=0),
        name="wgrad",
    )(*args)


def solution(mesh):
    def device_fn(x_in, positions, long_factor, norm_gain, w_qkv, w_out, grad_y):
        _, piece, hidden = x_in.shape
        n_dev = mesh.shape['cp']
        seq = piece * n_dev
        width = w_out.shape[0]
        scale = 1.0 / math.sqrt(2 * long_factor.shape[0])
        swap = lambda t: lax.all_to_all(t, 'cp', split_axis=0, concat_axis=0)
        x = swap(x_in).reshape(seq, hidden)
        dy = swap(grad_y).reshape(seq, hidden)
        pos = lax.all_gather(positions, 'cp', tiled=True)
        cos, sin = rope_tables(pos, long_factor)
        r, pair = norm_call(x, dy, norm_gain[None, :])
        gather = lambda t: lax.all_gather(t[None] if t.ndim == 2 else t, 'cp')
        pair_all = gather(pair)
        y, dx, gg, ot, dq, dk, dv = block_call(x, r, dy, norm_gain[None, :], w_qkv, w_out, cos, sin, scale)
        ot_all, dq_all, dk_all, dv_all = gather(ot), gather(dq), gather(dk), gather(dv)
        y_out = swap(y.reshape(n_dev, piece, hidden))
        grad_x = swap(dx.reshape(n_dev, piece, hidden))
        g_gain = lax.psum(gg[0], 'cp')
        g_wout = grad_call(ot_all, pair_all, hidden, 0, flip=True)
        g_wqkv = grad_call(pair_all, dq_all, 3 * width, 0)
        g_wqkv = grad_call(pair_all, dk_all, 3 * width, width, g_wqkv)
        g_wqkv = grad_call(pair_all, dv_all, 3 * width, 2 * width, g_wqkv)
        return y_out, grad_x, g_gain, g_wqkv, g_wout

    seq_spec = P('dp', 'cp', None)
    return jax.shard_map(device_fn, mesh=mesh, in_specs=(seq_spec, P(('dp', 'cp')), P(None), P(None), P(None, None), P(None, None), seq_spec), out_specs=(seq_spec, seq_spec, P('dp'), P('dp', None), P('dp', None)), check_vma=False)
```

time: 4450 us -> 802 us (0.18)
  waiting for transfers between devices: 3570 us -> 249 us
  local copies, waits for them, and re-layouts: 476 us -> 8.33 us
  Pallas kernels: 0 us -> 350 us
  blocking collectives: 13.3 us -> 169 us
  matrix products: 140 us -> 0 us
  other arithmetic: 121 us -> 2.32 us
  starting transfers between devices: 105 us -> 8.5 us
    ppermute x44 -> x0, waiting for transfers between devices: 2870 us -> none  [the longest x7 1780 us: bwd_step(): v_cur = lax.ppermute(v_cur, 'cp', shift_perm)]
    psum x1 -> x0, waiting for transfers between devices: 704 us -> none  [device_fn(): g_gain, g_wqkv, g_wout = lax.psum((g_gain, g_wqkv, g_wout), 'cp')]
    pallas_call x0 -> x6, Pallas kernels: none -> 350 us  [the longest x4 252 us: grad_call(): pl.pallas_call(functools.partial(grad_kernel, flip), grid=(rows // tm, n...]
    while x47 -> x0, local copies, waits for them, and re-layouts: 306 us -> none
    all_gather x0 -> x5, waiting for transfers between devices: none -> 246 us  [device_fn(): gather = lambda t: lax.all_gather(t[None] if t.ndim == 2 else t, 'cp')]
    dot_general x12 -> x0, matrix products: 140 us -> none  [the longest x1 23.8 us: device_fn(): jnp.einsum('bsd,bse->de', normed, d_qkv, preferred_element_type=jnp.float32)]
    ppermute x44 -> x0, starting transfers between devices: 105 us -> none  [the longest x7 30.1 us: fwd_step(): k_cur = lax.ppermute(k_cur, 'cp', shift_perm)]
    all_to_all x0 -> x2, blocking collectives: none -> 84.1 us  [device_fn(): swap = lambda t: lax.all_to_all(t, 'cp', split_axis=0, concat_axis=0)]
  transfers between devices with their start and end apart: 45 -> 7, of which waited for: 31 -> 5; matrix products, arithmetic and copies ran while one was open for 4% -> 0% of each run, Pallas kernels for 0% -> 24%
where the time goes in v1:
time: 802 us
  Pallas kernels  350 us (44%)
  waiting for transfers between devices  249 us (31%)
  blocking collectives  169 us (21%)
  between operations  14.5 us (2%)
  starting transfers between devices  8.5 us (1%)
  local copies, waits for them, and re-layouts  8.33 us (1%)
    pallas_call x4, Pallas kernels, grad_call(): pl.pallas_call(functools.partial(grad_kernel, flip), grid=(rows // tm, n...  252 us
    all_gather x5, waiting for transfers between devices, device_fn(): gather = lambda t: lax.all_gather(t[None] if t.ndim == 2 else t, 'cp')  246 us
    pallas_call x1, Pallas kernels, block_call(): pl.pallas_call(functools.partial(block_kernel, scale), grid=(steps,), in_...  95.4 us
    all_to_all x2, blocking collectives, device_fn(): swap = lambda t: lax.all_to_all(t, 'cp', split_axis=0, concat_axis=0)  84.1 us
    psum x1, blocking collectives, device_fn(): g_gain = lax.psum(gg[0], 'cp')  57.6 us
    unnamed x1, blocking collectives  27.2 us
  transfers between devices with their start and end apart: 7, of which 5 were waited for; matrix products, arithmetic and copies ran while one was open for 0% of the time, Pallas kernels for 24%

profile of v1, /device:TPU:0, one launch (start us, length us, event | category | flops | bytes accessed | tf_op | source)
XLA Modules:
  0.0 801.7 jit_solution(4638041190038101430)
XLA Ops:
  7.2 32.0 %all_to_all.20 = bf16[8,64,2048]{2,1,0:T(8,128)(2,1)S(1)} all-to-all(bf16[8,64,2048]{2,1,0:T(8,128)(2,1)} %param.7), channel_id=1, replica_groups=mesh['dp'=2,'cp'=8] {'cp'}, dimensions={0} | all-to-all | bytes 4194304 | tf_op jit(solution)/shard_map/all_to_all | solution.py:234
  39.2 4.5 all-to-all-start.1
  45.3 27.2 %all-reduce = s32[512]{0:T(512)S(1)} all-reduce(s32[512]{0:T(512)S(1)} %dynamic-update-slice), channel_id=1, replica_groups=mesh['dp'=2,'cp'=8] {'cp'}, use_global_device_ids=true, to_apply=%add | all-reduce | flops 512 | bytes 4096
  72.5 1.0 fusion.2
  73.5 1.3 pad_maximum_fusion
  74.8 3.3 norm.1
  78.1 2.0 copy-done.1
  80.1 1.3 copy-done.3
  81.4 95.4 %block.1 = (bf16[512,2048]{1,0:T(8,128)(2,1)}, bf16[512,2048]{1,0:T(8,128)(2,1)}, f32[1,2048]{1,0:T(1,128)}, bf16[2048,512]{1,0:T(8,128)(2,1)}, bf16[512,2048]{1...) custom-call(bf16[512,2048]{1,0:T(8,128)(2,1)} %bitcast.13, bf16[512,2048]{1,0:T(8,128)(2,1)} %copy-done.3, ...), custom_call_target="tpu_custom_call" | custom-call | flops 60000002048 | bytes 60000000 | tf_op jit(solution)/shard_map/block/pallas_call | solution.py:149
  180.0 52.1 %all_to_all.21 = bf16[8,64,2048]{2,1,0:T(8,128)(2,1)} all-to-all(bf16[8,64,2048]{2,1,0:T(8,128)(2,1)S(1)} %bitcast.23), channel_id=1, replica_groups=mesh['dp'=2,'cp'=8] {'cp'}, dimensions={0} | all-to-all | bytes 4194304 | tf_op jit(solution)/shard_map/all_to_all | solution.py:234
  232.1 3.8 all-to-all-start.3
  235.9 57.6 %psum.7 = f32[2048]{0:T(1024)} all-reduce(f32[2048]{0:T(1024)S(1)} %bitcast.24), channel_id=1, replica_groups=mesh['dp'=2,'cp'=8] {'cp'}, use_global_device_ids=true, to_apply=%region_0.0 | all-reduce | flops 2048 | bytes 16384 | tf_op jit(solution)/shard_map/psum | solution.py:246
  293.5 13.7 %all-gather.17.cloned.1.call-done = bf16[4096,2048]{1,0:T(8,128)(2,1)} async-done(((bf16[512,2048]{1,0:T(8,128)(2,1)}), bf16[4096,2048]{1,0:T(8,128)(2,1)}) %all-gather.17.cloned.1.call-update) | async-done | bytes 16777232 | tf_op jit(solution)/shard_map/all_gather | solution.py:240
  307.3 159.3 %all-gather.11.cloned.1.call-done = bf16[16,2048,512]{2,1,0:T(8,128)(2,1)} async-done(((bf16[2,2048,512]{2,1,0:T(8,128)(2,1)}), bf16[16,2048,512]{2,1,0:T(8,128)(2,1)}) %all-gather.11.cloned.1.call-update) | async-done | bytes 33554448 | tf_op jit(solution)/shard_map/all_gather | solution.py:240
  466.5 63.0 %wgrad.4.rest_0_ = f32[2048,6144]{1,0:T(8,128)} custom-call(bf16[8,2,2048,512]{3,2,1,0:T(8,128)(2,1)} %bitcast.16, bf16[8,1,512,2048]{3,2,1,0:T(8,128)(2,1)} %bitcast.25), custom_call_target="tpu_custom_call" | custom-call | flops 34359738368 | bytes 80000000 | tf_op jit(solution)/shard_map/wgrad/pallas_call | solution.py:214
  529.5 24.9 %all-gather.19.cloned.1.call-done = bf16[16384,512]{1,0:T(8,128)(2,1)} async-done(((bf16[2048,512]{1,0:T(8,128)(2,1)}), bf16[16384,512]{1,0:T(8,128)(2,1)}) %all-gather.19.cloned.1.call-update) | async-done | bytes 16777232 | tf_op jit(solution)/shard_map/all_gather | solution.py:240
  554.4 63.9 %wgrad.7 = f32[2048,2048]{1,0:T(8,128)} custom-call(bf16[8,1,2048,512]{3,2,1,0:T(8,128)(2,1)} %bitcast.26, bf16[8,2,2048,512]{3,2,1,0:T(8,128)(2,1)} %bitcast.17), custom_call_target="tpu_custom_call" | custom-call | flops 34359738368 | bytes 80000000 | tf_op jit(solution)/shard_map/wgrad/pallas_call | solution.py:214
  618.4 23.8 %all-gather.15.cloned.1.call-done = bf16[4096,2048]{1,0:T(8,128)(2,1)} async-done(((bf16[512,2048]{1,0:T(8,128)(2,1)}), bf16[4096,2048]{1,0:T(8,128)(2,1)}) %all-gather.15.cloned.1.call-update) | async-done | bytes 16777232 | tf_op jit(solution)/shard_map/all_gather | solution.py:240
  642.1 63.1 %wgrad.5.rest_0_ = f32[2048,6144]{1,0:T(8,128)} custom-call(bf16[8,2,2048,512]{3,2,1,0:T(8,128)(2,1)} %bitcast.18, bf16[8,1,512,2048]{3,2,1,0:T(8,128)(2,1)} %bitcast.20, f32[2048,6144]{1,0:T(8,128)} %wgrad.4.rest_0_), custom_call_target="tpu_custom_call", output_to_operand_aliasing={{}: (2, {})} | custom-call | flops 34359738368 | bytes 80000000 | tf_op jit(solution)/shard_map/wgrad/pallas_call | solution.py:214
  705.2 24.6 %all-gather.13.cloned.1.call-done = bf16[4096,2048]{1,0:T(8,128)(2,1)} async-done(((bf16[512,2048]{1,0:T(8,128)(2,1)}), bf16[4096,2048]{1,0:T(8,128)(2,1)}) %all-gather.13.cloned.1.call-update) | async-done | bytes 16777232 | tf_op jit(solution)/shard_map/all_gather | solution.py:240
  729.8 61.7 %wgrad.6 = f32[2048,6144]{1,0:T(8,128)} custom-call(bf16[8,2,2048,512]{3,2,1,0:T(8,128)(2,1)} %bitcast.19, bf16[8,1,512,2048]{3,2,1,0:T(8,128)(2,1)} %bitcast.21, f32[2048,6144]{1,0:T(8,128)} %wgrad.5.rest_0_), custom_call_target="tpu_custom_call", output_to_operand_aliasing={{}: (2, {})} | custom-call | flops 34359738368 | bytes 80000000 | tf_op jit(solution)/shard_map/wgrad/pallas_call | solution.py:214
  791.5 1.3 copy.20
  792.8 1.0 copy-done.6
  793.9 1.3 copy.21
  (38 shorter events, 4.0 us)
Async XLA Ops:
  39.2 35.6 %copy-start = (bf16[8,64,2048]{2,1,0:T(8,128)(2,1)}, bf16[8,64,2048]{2,1,0:T(8,128)(2,1)S(1)}, u32[]{:S(2)}) copy-start(bf16[8,64,2048]{2,1,0:T(8,128)(2,1)S(1)} %all_to_all.20) | copy-start | bytes 6291460
  39.2 4.6 copy-start.11
  39.2 5.8 copy-start.9
  39.2 33.3 %copy-start.10 = (f32[32]{0:T(128)S(1)}, f32[32]{0:T(128)}, u32[]{:S(2)}) copy-start(f32[32]{0:T(128)} %param.9) | copy-start | bytes 388
  39.2 35.6 %all-to-all-start.1 = ((bf16[8,64,2048]{2,1,0:T(8,128)(2,1)}), bf16[8,64,2048]{2,1,0:T(8,128)(2,1)}, u32[]{:S(2)}, u32[]{:S(2)}) async-start(bf16[8,64,2048]{2,1,0:T(8,128)(2,1)} %param.13), calls=%async_computation.1 | async-start | bytes 4194304 | tf_op jit(solution)/shard_map/all_to_all | solution.py:234
  43.7 31.1 %copy-start.2 = (f32[2048]{0:T(1024)S(1)}, f32[2048]{0:T(1024)}, u32[]{:S(2)}) copy-start(f32[2048]{0:T(1024)} %param.10) | copy-start | bytes 24580
  43.7 263.6 %all-gather.17.cloned.1.call-start = ((), (), s32[]{:S(2)}) async-start(), calls=%async_computation.7 | async-start | bytes 18874368 | tf_op jit(solution)/shard_map/all_gather | solution.py:240
  78.1 2.0 copy-start.1
  80.1 1.3 copy-start.3
  176.8 289.7 %all-gather.11.cloned.1.call-start = ((), (), s32[]{:S(2)}) async-start(), calls=%async_computation.4 | async-start | bytes 37748736 | tf_op jit(solution)/shard_map/all_gather | solution.py:240
  177.6 376.8 %all-gather.19.cloned.1.call-start = ((), (), s32[]{:S(2)}) async-start(), calls=%async_computation.8 | async-start | bytes 18874368 | tf_op jit(solution)/shard_map/all_gather | solution.py:240
  178.3 463.8 %all-gather.15.cloned.1.call-start = ((), (), s32[]{:S(2)}) async-start(), calls=%async_computation.6 | async-start | bytes 18874368 | tf_op jit(solution)/shard_map/all_gather | solution.py:240
  178.4 1.6 copy-start.7
  178.9 550.9 %all-gather.13.cloned.1.call-start = ((), (), s32[]{:S(2)}) async-start(), calls=%async_computation.5 | async-start | bytes 18874368 | tf_op jit(solution)/shard_map/all_gather | solution.py:240
  232.1 3.8 copy-start.8
  232.1 61.5 %all-to-all-start.3 = ((bf16[8,64,2048]{2,1,0:T(8,128)(2,1)}), bf16[8,64,2048]{2,1,0:T(8,128)(2,1)S(1)}, u32[]{:S(2)}, u32[]{:S(2)}) async-start(bf16[8,64,2048]{2,1,0:T(8,128)(2,1)} %bitcast.22), calls=%async_computation.3 | async-start | bytes 4194304 | tf_op jit(solution)/shard_map/all_to_all | solution.py:234
  293.5 236.0 %copy-start.5 = (bf16[8,64,2048]{2,1,0:T(8,128)(2,1)}, bf16[8,64,2048]{2,1,0:T(8,128)(2,1)S(1)}, u32[]{:S(2)}) copy-start(bf16[8,64,2048]{2,1,0:T(8,128)(2,1)S(1)} %all-to-all-done.3) | copy-start | bytes 6291460
  729.8 61.7 %copy-start.4 = (bf16[8,64,2048]{2,1,0:T(8,128)(2,1)S(1)}, bf16[8,64,2048]{2,1,0:T(8,128)(2,1)}, u32[]{:S(2)}) copy-start(bf16[8,64,2048]{2,1,0:T(8,128)(2,1)} %all_to_all.21) | copy-start | bytes 6291460
  791.5 2.3 copy-start.6
Sparse Core Ops, SparseCore 0:
  177.0 130.2 all-gather.16
  309.7 156.8 all-gather.10
  468.4 85.9 all-gather.18
  556.1 85.9 all-gather.14
  643.8 85.9 all-gather.12

commit v2 on v1

--- a/solution.py
+++ b/solution.py
@@ -33,7 +33,7 @@
 
 
 def block_kernel(scale, x_ref, r_ref, dy_ref, gain_ref, wq_ref, wk_ref, wv_ref, wo_ref, cos_ref, sin_ref,
-                 y_ref, dx_ref, gg_ref, ot_ref, dq_ref, dk_ref, dv_ref, y_acc, dn_acc):
+                 y_ref, dx_ref, gg_ref, oa_ref, ob_ref, qa_ref, qb_ref, ka_ref, kb_ref, va_ref, vb_ref, y_acc, dn_acc):
     step = pl.program_id(0)
     seq = x_ref.shape[0]
     qb = 256
@@ -108,7 +108,6 @@
             ots.append(jnp.concatenate(ot_b, axis=1))
             dqts.append(jnp.concatenate(dqt_b, axis=1))
         ot_pair = jnp.concatenate(ots, axis=0)
-        ot_ref[cols, :] = ot_pair
         o = ot_pair.T
         dq = jnp.concatenate(dqts, axis=0).T * scale
         dk = jnp.concatenate(dk_sum, axis=0)
@@ -116,13 +115,14 @@
         dqb = (dq * cos - partner(dq, first_half) * sin).astype(BF16)
         dkb = (dk * cos - partner(dk, first_half) * sin).astype(BF16)
         dvb = dv.astype(BF16)
-        dq_ref[:, cols] = dqb
-        dk_ref[:, cols] = dkb
-        dv_ref[:, cols] = dvb
+        for value, a_ref, b_ref in ((o, oa_ref, ob_ref), (dqb, qa_ref, qb_ref), (dkb, ka_ref, kb_ref), (dvb, va_ref, vb_ref)):
+            a_ref[:, cols] = value[:qb]
+            b_ref[:, cols] = value[qb:]
         y_acc[...] += dot(o, wo_ref[cols, :])
 
-    dn_acc[...] += (dot(dq_ref[...], wq_ref[...], ((1,), (1,))) + dot(dk_ref[...], wk_ref[...], ((1,), (1,)))
-                    + dot(dv_ref[...], wv_ref[...], ((1,), (1,))))
+    for rows, dq_ref, dk_ref, dv_ref in ((slice(0, qb), qa_ref, ka_ref, va_ref), (slice(qb, 2 * qb), qb_ref, kb_ref, vb_ref)):
+        dn_acc[rows, :] += (dot(dq_ref[...], wq_ref[...], ((1,), (1,))) + dot(dk_ref[...], wk_ref[...], ((1,), (1,)))
+                            + dot(dv_ref[...], wv_ref[...], ((1,), (1,))))
 
     @pl.when(step == pl.num_programs(0) - 1)
     def _():
@@ -144,17 +144,16 @@
     steps = width // hb
     whole = lambda a: pl.BlockSpec(a.shape, lambda j: (0, 0), pipeline_mode=pl.Buffered(1))
     wcol = lambda part: pl.BlockSpec((hidden, hb), lambda j, part=part: (0, part * steps + j))
-    tok = pl.BlockSpec((seq, hb), lambda j: (0, j))
+    tok = pl.BlockSpec((seq // 2, hb), lambda j: (0, j))
     full = lambda s: pl.BlockSpec(s, lambda j: (0, 0))
     return pl.pallas_call(
         functools.partial(block_kernel, scale),
         grid=(steps,),
         in_specs=[whole(x), whole(r), whole(dy), whole(gain), wcol(0), wcol(1), wcol(2),
                   pl.BlockSpec((hb, hidden), lambda j: (j, 0)), whole(cos), whole(sin)],
-        out_specs=[full((seq, hidden)), full((seq, hidden)), full((1, hidden)), pl.BlockSpec((hb, seq), lambda j: (j, 0)), tok, tok, tok],
+        out_specs=[full((seq, hidden)), full((seq, hidden)), full((1, hidden))] + [tok] * 8,
         out_shape=[jax.ShapeDtypeStruct((seq, hidden), BF16), jax.ShapeDtypeStruct((seq, hidden), BF16),
-                   jax.ShapeDtypeStruct((1, hidden), F32), jax.ShapeDtypeStruct((width, seq), BF16)]
-        + [jax.ShapeDtypeStruct((seq, width), BF16)] * 3,
+                   jax.ShapeDtypeStruct((1, hidden), F32)] + [jax.ShapeDtypeStruct((seq // 2, width), BF16)] * 8,
         scratch_shapes=[pltpu.VMEM((seq, hidden), F32), pltpu.VMEM((seq, hidden), F32)],
         compiler_params=pltpu.CompilerParams(dimension_semantics=("arbitrary",), vmem_limit_bytes=60 << 20),
         cost_estimate=pl.CostEstimate(flops=60_000_000_000, bytes_accessed=60_000_000, transcendentals=8_000_000),
@@ -162,64 +161,85 @@
     )(x, r, dy, gain, w_qkv, w_qkv, w_qkv, w_out, cos, sin)
 
 
-def norm_kernel(x_ref, dy_ref, gain_ref, r_ref, pair_ref):
+def norm_kernel(x_ref, dy_ref, gain_ref, r_ref, *pair_refs):
     x = x_ref[...].astype(F32)
     inv = lax.rsqrt(jnp.mean(x * x, axis=1, keepdims=True) + NORM_EPS)
     r = (x * inv * gain_ref[...]).astype(BF16)
     r_ref[...] = r
-    pair_ref[0] = r.T
-    pair_ref[1] = dy_ref[...].T
+    part = pair_refs[0].shape[2]
+    for i, ref in enumerate(pair_refs):
+        ref[0] = r[part * i:part * i + part].T
+        ref[1] = dy_ref[part * i:part * i + part, :].T
 
 
 def norm_call(x, dy, gain):
     seq, hidden = x.shape
     return pl.pallas_call(
         norm_kernel,
-        out_shape=[jax.ShapeDtypeStruct((seq, hidden), BF16), jax.ShapeDtypeStruct((2, hidden, seq), BF16)],
+        out_shape=[jax.ShapeDtypeStruct((seq, hidden), BF16)] + [jax.ShapeDtypeStruct((2, hidden, seq // 2), BF16)] * 2,
         compiler_params=pltpu.CompilerParams(vmem_limit_bytes=40 << 20),
         cost_estimate=pl.CostEstimate(flops=10_000_000, bytes_accessed=10_000_000, transcendentals=0),
         name="norm",
     )(x, dy, gain)
 
 
-def grad_kernel(flip, a_ref, b_ref, *rest):
-    out_ref = rest[-1]
-    dims = ((1,), (1,)) if flip else ((1,), (0,))
-    part = dot(a_ref[0, 0], b_ref[0, 0], dims)
-    for i in range(1, a_ref.shape[0]):
-        part += dot(a_ref[i, 0], b_ref[i, 0], dims)
-
-    @pl.when(pl.program_id(2) == 0)
+def grad_kernel(count, flip, add, *refs):
+    lefts, rights = refs[:count], refs[count:2 * count]
+    out_ref, l_buf, r_buf = refs[-3:]
+    part = lefts[0].shape[2]
+
+    @pl.when(pl.program_id(1) == 0)
     def _():
-        out_ref[...] = part
-
-    @pl.when(pl.program_id(2) > 0)
-    def _():
-        out_ref[...] += part
-
-
-def grad_call(at, b, n_out, col, buf=None, flip=False):
-    n_seq, _, rows, seq = at.shape
-    last = b.shape[1] - 1
-    n = b.shape[2] if flip else b.shape[3]
-    tm, tn, ts = 1024, 512, 2
-    specs = [pl.BlockSpec((ts, 1, tm, seq), lambda i, j, k: (k, 0, i, 0)),
-             pl.BlockSpec((ts, 1, tn, seq), lambda i, j, k: (k, last, j, 0)) if flip else pl.BlockSpec((ts, 1, seq, tn), lambda i, j, k: (k, last, 0, j))]
-    args = [at, b]
+        for i, ref in enumerate(lefts):
+            l_buf[:, part * i:part * i + part] = ref[0]
+
+    for i, ref in enumerate(rights):
+        r_buf[part * i:part * i + part, :] = ref[...]
+
+    sub = 512
+
+    def body(i, carry):
+        rows = pl.ds(pl.multiple_of(i * sub, sub), sub)
+        tile = dot(l_buf[rows, :], r_buf[...])
+        if flip:
+            out_ref[:, rows] = tile.T
+        elif add:
+            out_ref[rows, :] = refs[2 * count][rows, :] + tile
+        else:
+            out_ref[rows, :] = tile
+        return carry
+
+    lax.fori_loop(0, l_buf.shape[0] // sub, body, 0)
+
+
+def grad_call(lefts, rights, which, n_out, col, buf=None, flip=False, add=False):
+    count = len(lefts)
+    _, rows, part = lefts[0].shape
+    n = rights[0].shape[1]
+    tm, tn = 1024, 512
+    specs = [pl.BlockSpec((1, tm, part), lambda i, j: (which, i, 0))] * count + [pl.BlockSpec((part, tn), lambda i, j: (0, j))] * count
+    args = list(lefts) + list(rights)
+    if flip:
+        out_spec = pl.BlockSpec((tn, tm), lambda i, j: (j, i))
+        out_shape = jax.ShapeDtypeStruct((n, rows), F32)
+    else:
+        out_spec = pl.BlockSpec((tm, tn), lambda i, j: (i, col // tn + j))
+        out_shape = jax.ShapeDtypeStruct((rows, n_out), F32)
     aliases = {}
     if buf is not None:
-        specs.append(pl.BlockSpec(memory_space=pl.ANY))
+        specs.append(out_spec if add else pl.BlockSpec(memory_space=pl.ANY))
         args.append(buf)
-        aliases = {2: 0}
+        aliases = {2 * count: 0}
     return pl.pallas_call(
-        functools.partial(grad_kernel, flip),
-        grid=(rows // tm, n // tn, n_seq // ts),
+        functools.partial(grad_kernel, count, flip, add),
+        grid=(rows // tm, n // tn),
         in_specs=specs,
-        out_specs=pl.BlockSpec((tm, tn), lambda i, j, k: (i, col // tn + j)),
-        out_shape=jax.ShapeDtypeStruct((rows, n_out), F32),
+        out_specs=out_spec,
+        out_shape=out_shape,
+        scratch_shapes=[pltpu.VMEM((tm, part * count), BF16), pltpu.VMEM((part * count, tn), BF16)],
         input_output_aliases=aliases,
-        compiler_params=pltpu.CompilerParams(dimension_semantics=("arbitrary",) * 3, vmem_limit_bytes=48 << 20),
-        cost_estimate=pl.CostEstimate(flops=2 * rows * n * n_seq * seq, bytes_accessed=80_000_000, transcendentals=0),
+        compiler_params=pltpu.CompilerParams(dimension_semantics=("arbitrary",) * 2, vmem_limit_bytes=56 << 20),
+        cost_estimate=pl.CostEstimate(flops=2 * rows * n * part * count, bytes_accessed=80_000_000, transcendentals=0),
         name="wgrad",
     )(*args)
 
@@ -231,23 +251,54 @@
         seq = piece * n_dev
         width = w_out.shape[0]
         scale = 1.0 / math.sqrt(2 * long_factor.shape[0])
-        swap = lambda t: lax.all_to_all(t, 'cp', split_axis=0, concat_axis=0)
+        me = lax.axis_index('cp')
+        mine = jnp.bitwise_xor(me, jnp.arange(n_dev))
+
+        def shift(t, bit):
+            return lax.ppermute(t, 'cp', [(i, i ^ bit) for i in range(n_dev)])
+
+        def swap(t):
+            sent = t[mine]
+            return jnp.stack([sent[0]] + [shift(sent[m], m) for m in range(1, n_dev)])[mine]
+
+        def after(values, deps):
+            return lax.optimization_barrier((values, deps))[0]
+
         x = swap(x_in).reshape(seq, hidden)
         dy = swap(grad_y).reshape(seq, hidden)
         pos = lax.all_gather(positions, 'cp', tiled=True)
         cos, sin = rope_tables(pos, long_factor)
-        r, pair = norm_call(x, dy, norm_gain[None, :])
-        gather = lambda t: lax.all_gather(t[None] if t.ndim == 2 else t, 'cp')
-        pair_all = gather(pair)
-        y, dx, gg, ot, dq, dk, dv = block_call(x, r, dy, norm_gain[None, :], w_qkv, w_out, cos, sin, scale)
-        ot_all, dq_all, dk_all, dv_all = gather(ot), gather(dq), gather(dk), gather(dv)
+        r, pair_a, pair_b = norm_call(x, dy, norm_gain[None, :])
+
+        def near(ab):
+            a, b = ab
+            return [a, b, shift(a, 2), shift(b, 2), shift(a, 4), shift(b, 4)]
+
+        def far(pieces, deps=()):
+            pieces = after(pieces, deps)
+            diag = [shift(pieces[2], 4), shift(pieces[5], 2)]
+            return pieces + [shift(t, 1) for t in pieces], diag + [shift(t, 1) for t in diag]
+
+        pair_part = near((pair_a, pair_b))
+        out = block_call(x, r, dy, norm_gain[None, :], w_qkv, w_out, cos, sin, scale)
+        y, dx, gg = out[:3]
+        pair_near, pair_far = far(pair_part, (gg,))
+        o_part = near(out[3:5])
+        q_part = near(out[5:7])
+        k_part = near(after(out[7:9], o_part))
+        o_near, o_far = far(o_part)
         y_out = swap(y.reshape(n_dev, piece, hidden))
         grad_x = swap(dx.reshape(n_dev, piece, hidden))
         g_gain = lax.psum(gg[0], 'cp')
-        g_wout = grad_call(ot_all, pair_all, hidden, 0, flip=True)
-        g_wqkv = grad_call(pair_all, dq_all, 3 * width, 0)
-        g_wqkv = grad_call(pair_all, dk_all, 3 * width, width, g_wqkv)
-        g_wqkv = grad_call(pair_all, dv_all, 3 * width, 2 * width, g_wqkv)
+        g_wout = grad_call(pair_near + pair_far, o_near + o_far, 1, hidden, 0, flip=True)
+        v_part = near(after(out[9:11], q_part))
+        q_near, q_far = far(q_part, (g_wout,))
+        g_wqkv = grad_call(pair_near + pair_far, q_near + q_far, 0, 3 * width, 0)
+        k_near, k_far = far(k_part, (g_wqkv,))
+        g_wqkv = grad_call(pair_near + pair_far, k_near + k_far, 0, 3 * width, width, g_wqkv)
+        v_near, v_far = far(v_part, (g_wqkv,))
+        g_wqkv = grad_call(pair_near, v_near, 0, 3 * width, 2 * width, g_wqkv)
+        g_wqkv = grad_call(pair_far, v_far, 0, 3 * width, 2 * width, g_wqkv, add=True)
         return y_out, grad_x, g_gain, g_wqkv, g_wout
 
     seq_spec = P('dp', 'cp', None)

time: 802 us -> 847 us (1.056)
  blocking collectives: 169 us -> 34.5 us
  waiting for transfers between devices: 249 us -> 361 us
  local copies, waits for them, and re-layouts: 8.33 us -> 70.2 us
  starting transfers between devices: 8.5 us -> 68.4 us
  Pallas kernels: 350 us -> 308 us
  between operations: 14.5 us -> 2.29 us
    ppermute x0 -> x98, waiting for transfers between devices: none -> 361 us  [shift(): return lax.ppermute(t, 'cp', [(i, i ^ bit) for i in range(n_dev)])]
    all_gather x5 -> x0, waiting for transfers between devices: 246 us -> none  [device_fn(): gather = lambda t: lax.all_gather(t[None] if t.ndim == 2 else t, 'cp')]
    all_to_all x2 -> x0, blocking collectives: 84.1 us -> none  [device_fn(): swap = lambda t: lax.all_to_all(t, 'cp', split_axis=0, concat_axis=0)]
    ppermute x0 -> x98, starting transfers between devices: none -> 68.4 us  [shift(): return lax.ppermute(t, 'cp', [(i, i ^ bit) for i in range(n_dev)])]
    psum x1, blocking collectives: 57.6 us -> 14.6 us  [device_fn(): g_gain = lax.psum(gg[0], 'cp')]
    pallas_call x4 -> x5, Pallas kernels: 252 us -> 210 us  [grad_call(): pl.pallas_call(functools.partial(grad_kernel, count, flip, add), grid=(ro...]
    unnamed x29 -> x193, local copies, waits for them, and re-layouts: 8.33 us -> 37.4 us
    gather x0 -> x8, local copies, waits for them, and re-layouts: none -> 21.4 us  [the longest x4 11.3 us: swap(): jnp.stack([sent[0]] + [shift(sent[m], m) for m in range(1, n_dev)])[mine]]
  transfers between devices with their start and end apart: 7 -> 98, of which waited for: 5 -> 33; matrix products, arithmetic and copies ran while one was open for 0% -> 6% of each run, Pallas kernels for 24% -> 22%
where the time goes in v2:
time: 847 us; the launch traced here: 846 us
  waiting for transfers between devices  361 us (43%)
  Pallas kernels  308 us (36%)
  local copies, waits for them, and re-layouts  70.2 us (8%)
  starting transfers between devices  68.4 us (8%)
  blocking collectives  34.5 us (4%)
    ppermute x98, waiting for transfers between devices, shift(): return lax.ppermute(t, 'cp', [(i, i ^ bit) for i in range(n_dev)])  361 us
    pallas_call x5, Pallas kernels, grad_call(): pl.pallas_call(functools.partial(grad_kernel, count, flip, add), grid=(ro...  210 us
    pallas_call x1, Pallas kernels, block_call(): pl.pallas_call(functools.partial(block_kernel, scale), grid=(steps,), in_...  95.9 us
    ppermute x98, starting transfers between devices, shift(): return lax.ppermute(t, 'cp', [(i, i ^ bit) for i in range(n_dev)])  68.4 us
    unnamed x193, local copies, waits for them, and re-layouts  37.4 us
    unnamed x1, blocking collectives  19.9 us
  transfers between devices with their start and end apart: 98, of which 33 were waited for; matrix products, arithmetic and copies ran while one was open for 6% of the time, Pallas kernels for 22%

profile of v2, /device:TPU:0, one launch (start us, length us, event | category | flops | bytes accessed | tf_op | source)
XLA Modules:
  0.0 846.2 jit_solution(7596555729321371531)
XLA Ops:
  14.6 19.9 %all-reduce = s32[512]{0:T(512)S(1)} all-reduce(s32[512]{0:T(512)S(1)} %dynamic-update-slice), channel_id=1, replica_groups=mesh['dp'=2,'cp'=8] {'cp'}, use_global_device_ids=true, to_apply=%add | all-reduce | flops 512 | bytes 4096
  50.3 7.0 collective-permute-done.9
  75.3 6.8 collective-permute-done.1
  82.6 7.9 collective-permute-done.2
  104.0 95.9 %block.1 = (bf16[512,2048]{1,0:T(8,128)(2,1)}, bf16[512,2048]{1,0:T(8,128)(2,1)}, f32[1,2048]{1,0:T(1,128)}, bf16[256,2048]{1,0:T(8,128)(2,1)}, bf16[256,2048]{1...) custom-call(bf16[512,2048]{1,0:T(8,128)(2,1)} %bitcast.123, ...), custom_call_target="tpu_custom_call" | custom-call | flops 60000002048 | bytes 60000000 | tf_op jit(solution)/shard_map/block/pallas_call | solution.py:149
  223.2 8.7 %collective-permute-done.38.refs_20_ = bf16[256,2048]{1,0:T(8,128)(2,1)} collective-permute-done((bf16[256,2048]{1,0:T(8,128)(2,1)}, bf16[256,2048]{1,0:T(8,128)(2,1)}, u32[]{:S(2)}, u32[]{:S(2)}) %collective-permute-start.38) | collective-permute-done | bytes 1048608 | tf_op jit(solution)/shard_map/ppermute | solution.py:258
  233.6 10.6 %collective-permute-done.36.refs_18_ = bf16[256,2048]{1,0:T(8,128)(2,1)S(1)} collective-permute-done((bf16[256,2048]{1,0:T(8,128)(2,1)S(1)}, bf16[256,2048]{1,0:T(8,128)(2,1)S(1)}, u32[]{:S(2)}, u32[]{:S(2)}) %collective-permute-start.36) | collective-permute-done | bytes 1048608 | tf_op jit(solution)/shard_map/ppermute | solution.py:258
  245.7 8.6 %collective-permute-done.39.refs_21_ = bf16[256,2048]{1,0:T(8,128)(2,1)S(1)} collective-permute-done((bf16[256,2048]{1,0:T(8,128)(2,1)}, bf16[256,2048]{1,0:T(8,128)(2,1)S(1)}, u32[]{:S(2)}, u32[]{:S(2)}) %collective-permute-start.39) | collective-permute-done | bytes 1048608 | tf_op jit(solution)/shard_map/ppermute | solution.py:258
  256.1 20.7 %collective-permute-done.52.refs_20_ = bf16[256,2048]{1,0:T(8,128)(2,1)S(1)} collective-permute-done((bf16[256,2048]{1,0:T(8,128)(2,1)}, bf16[256,2048]{1,0:T(8,128)(2,1)S(1)}, u32[]{:S(2)}, u32[]{:S(2)}) %collective-permute-start.52) | collective-permute-done | bytes 1048608 | tf_op jit(solution)/shard_map/ppermute | solution.py:258
  279.6 19.6 %collective-permute-done.53.refs_21_ = bf16[256,2048]{1,0:T(8,128)(2,1)S(1)} collective-permute-done((bf16[256,2048]{1,0:T(8,128)(2,1)}, bf16[256,2048]{1,0:T(8,128)(2,1)S(1)}, u32[]{:S(2)}, u32[]{:S(2)}) %collective-permute-start.53) | collective-permute-done | bytes 1048608 | tf_op jit(solution)/shard_map/ppermute | solution.py:258
  301.2 100.3 %collective-permute-done.37.refs_19_ = bf16[256,2048]{1,0:T(8,128)(2,1)S(1)} collective-permute-done((bf16[256,2048]{1,0:T(8,128)(2,1)}, bf16[256,2048]{1,0:T(8,128)(2,1)S(1)}, u32[]{:S(2)}, u32[]{:S(2)}) %collective-permute-start.37) | collective-permute-done | bytes 1048608 | tf_op jit(solution)/shard_map/ppermute | solution.py:258
  407.6 20.1 %collective-permute-done.64.refs_28_ = bf16[256,2048]{1,0:T(8,128)(2,1)S(1)} collective-permute-done((bf16[256,2048]{1,0:T(8,128)(2,1)S(1)}, bf16[256,2048]{1,0:T(8,128)(2,1)S(1)}, u32[]{:S(2)}, u32[]{:S(2)}) %collective-permute-start.64) | collective-permute-done | bytes 1048608 | tf_op jit(solution)/shard_map/ppermute | solution.py:258
  441.0 37.8 %collective-permute-done.32.refs_12_.refs_0_ = bf16[2,2048,256]{2,1,0:T(8,128)(2,1)S(1)} collective-permute-done((bf16[2,2048,256]{2,1,0:T(8,128)(2,1)S(1)}, bf16[2,2048,256]{2,1,0:T(8,128)(2,1)S(1)}, u32[]{:S(2)}, u32[]{:S(2)}) %collective-permute-start.32) | collective-permute-done | bytes 2097184 | tf_op jit(solution)/shard_map/ppermute | solution.py:258
  487.4 51.8 %wgrad.5 = f32[2048,2048]{1,0:T(8,128)} custom-call(bf16[2,2048,256]{2,1,0:T(8,128)(2,1)} %copy-done.2, bf16[2,2048,256]{2,1,0:T(8,128)(2,1)} %copy-done.3, bf16[2,2048,256]{2,1,0:T(8,128)(2,1)} %copy-done.10, bf16[2,2048,256]{2,1,0:T(8,128)(2,1)} %copy-done.12, bf16[2,2048,256]{2,1,0:T(8,128)(2,1)} %copy-done.9, bf16[2,2048,256]{2,1,0:T(8,128)(2,1)} %copy-done.11, ...), custom_call_target="tpu_custom_call" | custom-call | flops 34359738368 | bytes 80000000 | tf_op jit(solution)/shard_map/wgrad/pallas_call | solution.py:233
  545.4 20.3 %collective-permute-done.74.refs_28_ = bf16[256,2048]{1,0:T(8,128)(2,1)} collective-permute-done((bf16[256,2048]{1,0:T(8,128)(2,1)}, bf16[256,2048]{1,0:T(8,128)(2,1)}, u32[]{:S(2)}, u32[]{:S(2)}) %collective-permute-start.74) | collective-permute-done | bytes 1048608 | tf_op jit(solution)/shard_map/ppermute | solution.py:258
  567.5 14.6 %psum.7 = f32[2048]{0:T(1024)} all-reduce(f32[2048]{0:T(1024)S(1)} %bitcast.129), channel_id=1, replica_groups=mesh['dp'=2,'cp'=8] {'cp'}, use_global_device_ids=true, to_apply=%region_0.0 | all-reduce | flops 2048 | bytes 16384 | tf_op jit(solution)/shard_map/psum | solution.py:292
  587.4 48.8 %wgrad.6.refs_32_ = f32[2048,6144]{1,0:T(8,128)} custom-call(bf16[2,2048,256]{2,1,0:T(8,128)(2,1)} %copy-done.2, bf16[2,2048,256]{2,1,0:T(8,128)(2,1)} %copy-done.3, bf16[2,2048,256]{2,1,0:T(8,128)(2,1)} %copy-done.10, bf16[2,2048,256]{2,1,0:T(8,128)(2,1)} %copy-done.12, bf16[2,2048,256]{2,1,0:T(8,128)(2,1)} %copy-done.9, bf16[2,2048,256]{2,1,0:T(8,128)(2,1)} %copy-done.11, ...), custom_call_target="tpu_custom_call" | custom-call | flops 34359738368 | bytes 80000000 | tf_op jit(solution)/shard_map/wgrad/pallas_call | solution.py:233
  642.6 20.2 %collective-permute-done.84.refs_28_ = bf16[256,2048]{1,0:T(8,128)(2,1)S(1)} collective-permute-done((bf16[256,2048]{1,0:T(8,128)(2,1)}, bf16[256,2048]{1,0:T(8,128)(2,1)S(1)}, u32[]{:S(2)}, u32[]{:S(2)}) %collective-permute-start.84) | collective-permute-done | bytes 1048608 | tf_op jit(solution)/shard_map/ppermute | solution.py:258
  671.0 48.6 %wgrad.7.refs_24_ = f32[2048,6144]{1,0:T(8,128)} custom-call(bf16[2,2048,256]{2,1,0:T(8,128)(2,1)} %copy-done.2, bf16[2,2048,256]{2,1,0:T(8,128)(2,1)} %copy-done.3, bf16[2,2048,256]{2,1,0:T(8,128)(2,1)} %copy-done.10, bf16[2,2048,256]{2,1,0:T(8,128)(2,1)} %copy-done.12, bf16[2,2048,256]{2,1,0:T(8,128)(2,1)} %copy-done.9, ...), custom_call_target="tpu_custom_call", output_to_operand_aliasing={{}: (32, {})} | custom-call | flops 34359738368 | bytes 80000000 | tf_op jit(solution)/shard_map/wgrad/pallas_call | solution.py:233
  724.2 10.2 %collective-permute-done.16 = bf16[64,2048]{1,0:T(8,128)(2,1)S(1)} collective-permute-done((bf16[64,2048]{1,0:T(8,128)(2,1)}, bf16[64,2048]{1,0:T(8,128)(2,1)S(1)}, u32[]{:S(2)}, u32[]{:S(2)}) %collective-permute-start.16) | collective-permute-done | bytes 262176 | tf_op jit(solution)/shard_map/ppermute | solution.py:258
  737.8 10.4 %collective-permute-done.17 = bf16[64,2048]{1,0:T(8,128)(2,1)S(1)} collective-permute-done((bf16[64,2048]{1,0:T(8,128)(2,1)S(1)}, bf16[64,2048]{1,0:T(8,128)(2,1)S(1)}, u32[]{:S(2)}, u32[]{:S(2)}) %collective-permute-start.17) | collective-permute-done | bytes 262176 | tf_op jit(solution)/shard_map/ppermute | solution.py:258
  768.0 13.4 %collective-permute-done.88.refs_4_ = bf16[256,2048]{1,0:T(8,128)(2,1)} collective-permute-done((bf16[256,2048]{1,0:T(8,128)(2,1)}, bf16[256,2048]{1,0:T(8,128)(2,1)}, u32[]{:S(2)}, u32[]{:S(2)}) %collective-permute-start.88) | collective-permute-done | bytes 1048608 | tf_op jit(solution)/shard_map/ppermute | solution.py:258
  783.2 38.5 %wgrad.8.refs_8_ = f32[2048,6144]{1,0:T(8,128)} custom-call(bf16[2,2048,256]{2,1,0:T(8,128)(2,1)} %copy-done.2, bf16[2,2048,256]{2,1,0:T(8,128)(2,1)} %copy-done.3, bf16[2,2048,256]{2,1,0:T(8,128)(2,1)} %copy-done.10, bf16[2,2048,256]{2,1,0:T(8,128)(2,1)} %copy-done.12, bf16[2,2048,256]{2,1,0:T(8,128)(2,1)} %copy-done.9, ...), custom_call_target="tpu_custom_call", output_to_operand_aliasing={{}: (24, {})} | custom-call | flops 25769803776 | bytes 80000000 | tf_op jit(solution)/shard_map/wgrad/pallas_call | solution.py:233
  823.7 22.4 %wgrad.9 = f32[2048,6144]{1,0:T(8,128)} custom-call(bf16[2,2048,256]{2,1,0:T(8,128)(2,1)} %copy-done.13, bf16[2,2048,256]{2,1,0:T(8,128)(2,1)} %copy-done.15, bf16[2,2048,256]{2,1,0:T(8,128)(2,1)} %copy-done.18, bf16[2,2048,256]{2,1,0:T(8,128)(2,1)} %copy-done.20, bf16[256,2048]{1,0:T(8,128)(2,1)} %collective-permute-done.88.refs_4_, ...), custom_call_target="tpu_custom_call", output_to_operand_aliasing={{}: (8, {})} | custom-call | flops 8589934592 | bytes 80000000 | tf_op jit(solution)/shard_map/wgrad/pallas_call | solution.py:233
  (396 shorter events, 181.0 us)
Async XLA Ops:
  7.0 60.7 %collective-permute-start.13 = (bf16[64,2048]{1,0:T(8,128)(2,1)S(1)}, bf16[64,2048]{1,0:T(8,128)(2,1)}, u32[]{:S(2)}, u32[]{:S(2)}) collective-permute-start(bf16[64,2048]{1,0:T(8,128)(2,1)S(1)} %get-tuple-element.117), channel_id=1, source_target_pairs={{0,7},{1,6},{2,5},{3,4},{4,3},{5,2},{6,1},{7,0},{8,15},{9,14},{10,... | collective-permute-start | bytes 786440 | tf_op jit(solution)/shard_map/ppermute | solution.py:258
  10.6 55.1 %collective-permute-start.12 = (bf16[64,2048]{1,0:T(8,128)(2,1)}, bf16[64,2048]{1,0:T(8,128)(2,1)}, u32[]{:S(2)}, u32[]{:S(2)}) collective-permute-start(bf16[64,2048]{1,0:T(8,128)(2,1)} %get-tuple-element.118), channel_id=1, source_target_pairs={{0,6},{1,7},{2,4},{3,5},{4,2},{5,3},{6,0},{7,1},{8,14},{9,15},{10,... | collective-permute-start | bytes 786440 | tf_op jit(solution)/shard_map/ppermute | solution.py:258
  217.6 59.2 %collective-permute-start.52 = (bf16[256,2048]{1,0:T(8,128)(2,1)}, bf16[256,2048]{1,0:T(8,128)(2,1)S(1)}, u32[]{:S(2)}, u32[]{:S(2)}) collective-permute-start(bf16[256,2048]{1,0:T(8,128)(2,1)} %get-tuple-element.77.refs_16_), channel_id=1, source_target_pairs={{0,4},{1,5},{2,6},{3,7},{4,0},{5,1},{6,2},{7,3},{8,12},{9,13},{10,... | collective-permute-start | bytes 3145736 | tf_op jit(solution)/shard_map/ppermute | solution.py:258
  221.8 56.2 %collective-permute-start.50 = (bf16[256,2048]{1,0:T(8,128)(2,1)}, bf16[256,2048]{1,0:T(8,128)(2,1)S(1)}, u32[]{:S(2)}, u32[]{:S(2)}) collective-permute-start(bf16[256,2048]{1,0:T(8,128)(2,1)} %get-tuple-element.77.refs_16_), channel_id=1, source_target_pairs={{0,2},{1,3},{2,0},{3,1},{4,6},{5,7},{6,4},{7,5},{8,10},{9,11},{10,... | collective-permute-start | bytes 3145736 | tf_op jit(solution)/shard_map/ppermute | solution.py:258
  231.9 67.3 %collective-permute-start.53 = (bf16[256,2048]{1,0:T(8,128)(2,1)}, bf16[256,2048]{1,0:T(8,128)(2,1)S(1)}, u32[]{:S(2)}, u32[]{:S(2)}) collective-permute-start(bf16[256,2048]{1,0:T(8,128)(2,1)} %get-tuple-element.78.refs_17_), channel_id=1, source_target_pairs={{0,4},{1,5},{2,6},{3,7},{4,0},{5,1},{6,2},{7,3},{8,12},{9,13},{10,... | collective-permute-start | bytes 3145736 | tf_op jit(solution)/shard_map/ppermute | solution.py:258
  244.3 56.2 %collective-permute-start.51 = (bf16[256,2048]{1,0:T(8,128)(2,1)}, bf16[256,2048]{1,0:T(8,128)(2,1)S(1)}, u32[]{:S(2)}, u32[]{:S(2)}) collective-permute-start(bf16[256,2048]{1,0:T(8,128)(2,1)} %get-tuple-element.78.refs_17_), channel_id=1, source_target_pairs={{0,2},{1,3},{2,0},{3,1},{4,6},{5,7},{6,4},{7,5},{8,10},{9,11},{10,... | collective-permute-start | bytes 3145736 | tf_op jit(solution)/shard_map/ppermute | solution.py:258
  254.3 147.4 %collective-permute-start.30 = (bf16[2,2048,256]{2,1,0:T(8,128)(2,1)S(1)}, bf16[2,2048,256]{2,1,0:T(8,128)(2,1)S(1)}, u32[]{:S(2)}, u32[]{:S(2)}) collective-permute-start(bf16[2,2048,256]{2,1,0:T(8,128)(2,1)S(1)} %get-tuple-element.67.refs_0_), channel_id=1, source_target_pairs={{0,4},{1,5},{2,6},{3,7},{4,0},{5,1},{6,2},{7,3},{8,12},{9,13},{10,... | collective-permute-start | bytes 6291464 | tf_op jit(solution)/shard_map/ppermute | solution.py:258
  276.7 125.4 %collective-permute-start.28 = (bf16[2,2048,256]{2,1,0:T(8,128)(2,1)S(1)}, bf16[2,2048,256]{2,1,0:T(8,128)(2,1)S(1)}, u32[]{:S(2)}, u32[]{:S(2)}) collective-permute-start(bf16[2,2048,256]{2,1,0:T(8,128)(2,1)S(1)} %get-tuple-element.67.refs_0_), channel_id=1, source_target_pairs={{0,2},{1,3},{2,0},{3,1},{4,6},{5,7},{6,4},{7,5},{8,10},{9,11},{10,... | collective-permute-start | bytes 6291464 | tf_op jit(solution)/shard_map/ppermute | solution.py:258
  278.0 124.2 %collective-permute-start.31 = (bf16[2,2048,256]{2,1,0:T(8,128)(2,1)S(1)}, bf16[2,2048,256]{2,1,0:T(8,128)(2,1)S(1)}, u32[]{:S(2)}, u32[]{:S(2)}) collective-permute-start(bf16[2,2048,256]{2,1,0:T(8,128)(2,1)S(1)} %copy-done.4), channel_id=1, source_target_pairs={{0,4},{1,5},{2,6},{3,7},{4,0},{5,1},{6,2},{7,3},{8,12},{9,13},{10,... | collective-permute-start | bytes 6291464 | tf_op jit(solution)/shard_map/ppermute | solution.py:258
  299.2 104.6 %collective-permute-start.29 = (bf16[2,2048,256]{2,1,0:T(8,128)(2,1)S(1)}, bf16[2,2048,256]{2,1,0:T(8,128)(2,1)S(1)}, u32[]{:S(2)}, u32[]{:S(2)}) collective-permute-start(bf16[2,2048,256]{2,1,0:T(8,128)(2,1)S(1)} %copy-done.4), channel_id=1, source_target_pairs={{0,2},{1,3},{2,0},{3,1},{4,6},{5,7},{6,4},{7,5},{8,10},{9,11},{10,... | collective-permute-start | bytes 6291464 | tf_op jit(solution)/shard_map/ppermute | solution.py:258
  300.5 101.1 %collective-permute-start.37 = (bf16[256,2048]{1,0:T(8,128)(2,1)}, bf16[256,2048]{1,0:T(8,128)(2,1)S(1)}, u32[]{:S(2)}, u32[]{:S(2)}) collective-permute-start(bf16[256,2048]{1,0:T(8,128)(2,1)} %get-tuple-element.84.refs_17_), channel_id=1, source_target_pairs={{0,2},{1,3},{2,0},{3,1},{4,6},{5,7},{6,4},{7,5},{8,10},{9,11},{10,... | collective-permute-start | bytes 3145736 | tf_op jit(solution)/shard_map/ppermute | solution.py:258
  479.6 59.6 %collective-permute-start.21 = (bf16[64,2048]{1,0:T(8,128)(2,1)S(1)}, bf16[64,2048]{1,0:T(8,128)(2,1)S(1)}, u32[]{:S(2)}, u32[]{:S(2)}) collective-permute-start(bf16[64,2048]{1,0:T(8,128)(2,1)S(1)} %get-tuple-element.107), channel_id=1, source_target_pairs={{0,1},{1,0},{2,3},{3,2},{4,5},{5,4},{6,7},{7,6},{8,9},{9,8},{10,11... | collective-permute-start | bytes 786440 | tf_op jit(solution)/shard_map/ppermute | solution.py:258
  480.1 59.2 %collective-permute-start.56 = (bf16[256,2048]{1,0:T(8,128)(2,1)S(1)}, bf16[256,2048]{1,0:T(8,128)(2,1)}, u32[]{:S(2)}, u32[]{:S(2)}) collective-permute-start(bf16[256,2048]{1,0:T(8,128)(2,1)S(1)} %copy-done.27), channel_id=1, source_target_pairs={{0,4},{1,5},{2,6},{3,7},{4,0},{5,1},{6,2},{7,3},{8,12},{9,13},{10,... | collective-permute-start | bytes 3145736 | tf_op jit(solution)/shard_map/ppermute | solution.py:258
  481.8 58.0 %collective-permute-start.54 = (bf16[256,2048]{1,0:T(8,128)(2,1)S(1)}, bf16[256,2048]{1,0:T(8,128)(2,1)}, u32[]{:S(2)}, u32[]{:S(2)}) collective-permute-start(bf16[256,2048]{1,0:T(8,128)(2,1)S(1)} %copy-done.27), channel_id=1, source_target_pairs={{0,2},{1,3},{2,0},{3,1},{4,6},{5,7},{6,4},{7,5},{8,10},{9,11},{10,... | collective-permute-start | bytes 3145736 | tf_op jit(solution)/shard_map/ppermute | solution.py:258
  483.1 56.8 %collective-permute-start.57 = (bf16[256,2048]{1,0:T(8,128)(2,1)}, bf16[256,2048]{1,0:T(8,128)(2,1)}, u32[]{:S(2)}, u32[]{:S(2)}) collective-permute-start(bf16[256,2048]{1,0:T(8,128)(2,1)} %get-tuple-element.90.refs_17_), channel_id=1, source_target_pairs={{0,4},{1,5},{2,6},{3,7},{4,0},{5,1},{6,2},{7,3},{8,12},{9,13},{10,... | collective-permute-start | bytes 3145736 | tf_op jit(solution)/shard_map/ppermute | solution.py:258
  486.0 54.7 %collective-permute-start.55 = (bf16[256,2048]{1,0:T(8,128)(2,1)}, bf16[256,2048]{1,0:T(8,128)(2,1)}, u32[]{:S(2)}, u32[]{:S(2)}) collective-permute-start(bf16[256,2048]{1,0:T(8,128)(2,1)} %get-tuple-element.90.refs_17_), channel_id=1, source_target_pairs={{0,2},{1,3},{2,0},{3,1},{4,6},{5,7},{6,4},{7,5},{8,10},{9,11},{10,... | collective-permute-start | bytes 3145736 | tf_op jit(solution)/shard_map/ppermute | solution.py:258
  583.6 52.7 %collective-permute-start.26 = (bf16[64,2048]{1,0:T(8,128)(2,1)}, bf16[64,2048]{1,0:T(8,128)(2,1)S(1)}, u32[]{:S(2)}, u32[]{:S(2)}) collective-permute-start(bf16[64,2048]{1,0:T(8,128)(2,1)} %get-tuple-element.102), channel_id=1, source_target_pairs={{0,6},{1,7},{2,4},{3,5},{4,2},{5,3},{6,0},{7,1},{8,14},{9,15},{10,... | collective-permute-start | bytes 786440 | tf_op jit(solution)/shard_map/ppermute | solution.py:258
  583.6 53.3 %collective-permute-start.25 = (bf16[64,2048]{1,0:T(8,128)(2,1)}, bf16[64,2048]{1,0:T(8,128)(2,1)}, u32[]{:S(2)}, u32[]{:S(2)}) collective-permute-start(bf16[64,2048]{1,0:T(8,128)(2,1)} %get-tuple-element.103), channel_id=1, source_target_pairs={{0,5},{1,4},{2,7},{3,6},{4,1},{5,0},{6,3},{7,2},{8,13},{9,12},{10,... | collective-permute-start | bytes 786440 | tf_op jit(solution)/shard_map/ppermute | solution.py:258
  583.7 53.3 %collective-permute-start.24 = (bf16[64,2048]{1,0:T(8,128)(2,1)}, bf16[64,2048]{1,0:T(8,128)(2,1)}, u32[]{:S(2)}, u32[]{:S(2)}) collective-permute-start(bf16[64,2048]{1,0:T(8,128)(2,1)} %get-tuple-element.104), channel_id=1, source_target_pairs={{0,4},{1,5},{2,6},{3,7},{4,0},{5,1},{6,2},{7,3},{8,12},{9,13},{10,... | collective-permute-start | bytes 786440 | tf_op jit(solution)/shard_map/ppermute | solution.py:258
  584.8 52.6 %collective-permute-start.23 = (bf16[64,2048]{1,0:T(8,128)(2,1)S(1)}, bf16[64,2048]{1,0:T(8,128)(2,1)}, u32[]{:S(2)}, u32[]{:S(2)}) collective-permute-start(bf16[64,2048]{1,0:T(8,128)(2,1)S(1)} %get-tuple-element.105), channel_id=1, source_target_pairs={{0,3},{1,2},{2,1},{3,0},{4,7},{5,6},{6,5},{7,4},{8,11},{9,10},{10,... | collective-permute-start | bytes 786440 | tf_op jit(solution)/shard_map/ppermute | solution.py:258
  665.5 57.0 %collective-permute-start.15 = (bf16[64,2048]{1,0:T(8,128)(2,1)}, bf16[64,2048]{1,0:T(8,128)(2,1)}, u32[]{:S(2)}, u32[]{:S(2)}) collective-permute-start(bf16[64,2048]{1,0:T(8,128)(2,1)} %get-tuple-element.114), channel_id=1, source_target_pairs={{0,2},{1,3},{2,0},{3,1},{4,6},{5,7},{6,4},{7,5},{8,10},{9,11},{10,... | collective-permute-start | bytes 786440 | tf_op jit(solution)/shard_map/ppermute | solution.py:258
  665.9 53.8 %collective-permute-start.42 = (bf16[256,2048]{1,0:T(8,128)(2,1)S(1)}, bf16[256,2048]{1,0:T(8,128)(2,1)}, u32[]{:S(2)}, u32[]{:S(2)}) collective-permute-start(bf16[256,2048]{1,0:T(8,128)(2,1)S(1)} %copy-done.25), channel_id=1, source_target_pairs={{0,4},{1,5},{2,6},{3,7},{4,0},{5,1},{6,2},{7,3},{8,12},{9,13},{10,... | collective-permute-start | bytes 3145736 | tf_op jit(solution)/shard_map/ppermute | solution.py:258
  666.9 53.7 %collective-permute-start.40 = (bf16[256,2048]{1,0:T(8,128)(2,1)S(1)}, bf16[256,2048]{1,0:T(8,128)(2,1)}, u32[]{:S(2)}, u32[]{:S(2)}) collective-permute-start(bf16[256,2048]{1,0:T(8,128)(2,1)S(1)} %copy-done.25), channel_id=1, source_target_pairs={{0,2},{1,3},{2,0},{3,1},{4,6},{5,7},{6,4},{7,5},{8,10},{9,11},{10,... | collective-permute-start | bytes 3145736 | tf_op jit(solution)/shard_map/ppermute | solution.py:258
  668.6 53.3 %collective-permute-start.43 = (bf16[256,2048]{1,0:T(8,128)(2,1)S(1)}, bf16[256,2048]{1,0:T(8,128)(2,1)}, u32[]{:S(2)}, u32[]{:S(2)}) collective-permute-start(bf16[256,2048]{1,0:T(8,128)(2,1)S(1)} %copy-done.26), channel_id=1, source_target_pairs={{0,4},{1,5},{2,6},{3,7},{4,0},{5,1},{6,2},{7,3},{8,12},{9,13},{10,... | collective-permute-start | bytes 3145736 | tf_op jit(solution)/shard_map/ppermute | solution.py:258
  (157 other events, 4509.8 us)

commit v3 on v2

--- a/solution.py
+++ b/solution.py
@@ -161,26 +161,33 @@
     )(x, r, dy, gain, w_qkv, w_qkv, w_qkv, w_out, cos, sin)
 
 
-def norm_kernel(x_ref, dy_ref, gain_ref, r_ref, *pair_refs):
-    x = x_ref[...].astype(F32)
+def norm_kernel(both_ref, gain_ref, x_ref, dy_ref, r_ref, *pair_refs):
+    n, rows, hidden = both_ref.shape
+    piece = rows // 2
+    xb = both_ref[:, :piece, :].reshape(n * piece, hidden)
+    dy = both_ref[:, piece:, :].reshape(n * piece, hidden)
+    x_ref[...] = xb
+    dy_ref[...] = dy
+    x = xb.astype(F32)
     inv = lax.rsqrt(jnp.mean(x * x, axis=1, keepdims=True) + NORM_EPS)
     r = (x * inv * gain_ref[...]).astype(BF16)
     r_ref[...] = r
     part = pair_refs[0].shape[2]
     for i, ref in enumerate(pair_refs):
         ref[0] = r[part * i:part * i + part].T
-        ref[1] = dy_ref[part * i:part * i + part, :].T
-
-
-def norm_call(x, dy, gain):
-    seq, hidden = x.shape
+        ref[1] = dy[part * i:part * i + part].T
+
+
+def norm_call(both, gain):
+    n, rows, hidden = both.shape
+    seq = n * rows // 2
     return pl.pallas_call(
         norm_kernel,
-        out_shape=[jax.ShapeDtypeStruct((seq, hidden), BF16)] + [jax.ShapeDtypeStruct((2, hidden, seq // 2), BF16)] * 2,
-        compiler_params=pltpu.CompilerParams(vmem_limit_bytes=40 << 20),
-        cost_estimate=pl.CostEstimate(flops=10_000_000, bytes_accessed=10_000_000, transcendentals=0),
+        out_shape=[jax.ShapeDtypeStruct((seq, hidden), BF16)] * 3 + [jax.ShapeDtypeStruct((2, hidden, seq // 2), BF16)] * 2,
+        compiler_params=pltpu.CompilerParams(vmem_limit_bytes=48 << 20),
+        cost_estimate=pl.CostEstimate(flops=10_000_000, bytes_accessed=14_000_000, transcendentals=0),
         name="norm",
-    )(x, dy, gain)
+    )(both, gain)
 
 
 def grad_kernel(count, flip, add, *refs):
@@ -248,7 +255,6 @@
     def device_fn(x_in, positions, long_factor, norm_gain, w_qkv, w_out, grad_y):
         _, piece, hidden = x_in.shape
         n_dev = mesh.shape['cp']
-        seq = piece * n_dev
         width = w_out.shape[0]
         scale = 1.0 / math.sqrt(2 * long_factor.shape[0])
         me = lax.axis_index('cp')
@@ -264,11 +270,10 @@
         def after(values, deps):
             return lax.optimization_barrier((values, deps))[0]
 
-        x = swap(x_in).reshape(seq, hidden)
-        dy = swap(grad_y).reshape(seq, hidden)
+        both = lax.all_to_all(jnp.concatenate([x_in, grad_y], axis=1), 'cp', split_axis=0, concat_axis=0)
         pos = lax.all_gather(positions, 'cp', tiled=True)
         cos, sin = rope_tables(pos, long_factor)
-        r, pair_a, pair_b = norm_call(x, dy, norm_gain[None, :])
+        x, dy, r, pair_a, pair_b = norm_call(both, norm_gain[None, :])
 
         def near(ab):
             a, b = ab
@@ -287,15 +292,23 @@
         q_part = near(out[5:7])
         k_part = near(after(out[7:9], o_part))
         o_near, o_far = far(o_part)
-        y_out = swap(y.reshape(n_dev, piece, hidden))
-        grad_x = swap(dx.reshape(n_dev, piece, hidden))
-        g_gain = lax.psum(gg[0], 'cp')
+        gg1 = shift(gg, 1)
         g_wout = grad_call(pair_near + pair_far, o_near + o_far, 1, hidden, 0, flip=True)
+        y_out = swap(after(y, g_wout).reshape(n_dev, piece, hidden))
+        gg, gg1 = after((gg, gg1), g_wout)
+        gg = gg + gg1
+        gg2 = shift(gg, 2)
         v_part = near(after(out[9:11], q_part))
         q_near, q_far = far(q_part, (g_wout,))
         g_wqkv = grad_call(pair_near + pair_far, q_near + q_far, 0, 3 * width, 0)
+        grad_x = swap(after(dx, g_wqkv).reshape(n_dev, piece, hidden))
+        gg, gg2 = after((gg, gg2), g_wqkv)
+        gg = gg + gg2
+        gg4 = shift(gg, 4)
         k_near, k_far = far(k_part, (g_wqkv,))
         g_wqkv = grad_call(pair_near + pair_far, k_near + k_far, 0, 3 * width, width, g_wqkv)
+        gg, gg4 = after((gg, gg4), g_wqkv)
+        g_gain = (gg + gg4)[0]
         v_near, v_far = far(v_part, (g_wqkv,))
         g_wqkv = grad_call(pair_near, v_near, 0, 3 * width, 2 * width, g_wqkv)
         g_wqkv = grad_call(pair_far, v_far, 0, 3 * width, 2 * width, g_wqkv, add=True)

time: 847 us -> 769 us (0.908)
  waiting for transfers between devices: 361 us -> 314 us
  local copies, waits for them, and re-layouts: 70.2 us -> 27.5 us
  blocking collectives: 34.5 us -> 49.8 us
  starting transfers between devices: 68.4 us -> 56.2 us
    ppermute x98 -> x87, waiting for transfers between devices: 361 us -> 314 us  [shift(): return lax.ppermute(t, 'cp', [(i, i ^ bit) for i in range(n_dev)])]
    unnamed x1, blocking collectives: 19.9 us -> 49.8 us
    unnamed x193 -> x135, local copies, waits for them, and re-layouts: 37.4 us -> 14 us
    ppermute x98 -> x87, starting transfers between devices: 68.4 us -> 50.7 us  [shift(): return lax.ppermute(t, 'cp', [(i, i ^ bit) for i in range(n_dev)])]
    psum x1 -> x0, blocking collectives: 14.6 us -> none  [device_fn(): g_gain = lax.psum(gg[0], 'cp')]
  transfers between devices with their start and end apart: 98 -> 88, of which waited for: 33 -> 33; matrix products, arithmetic and copies ran while one was open for 6% -> 3% of each run, Pallas kernels for 22% -> 24%
where the time goes in v3:
time: 769 us
  waiting for transfers between devices  314 us (41%)
  Pallas kernels  311 us (40%)
  starting transfers between devices  56.2 us (7%)
  blocking collectives  49.8 us (6%)
  local copies, waits for them, and re-layouts  27.5 us (4%)
  other arithmetic  7.79 us (1%)
    ppermute x87, waiting for transfers between devices, shift(): return lax.ppermute(t, 'cp', [(i, i ^ bit) for i in range(n_dev)])  314 us
    pallas_call x5, Pallas kernels, grad_call(): pl.pallas_call(functools.partial(grad_kernel, count, flip, add), grid=(ro...  210 us
    pallas_call x1, Pallas kernels, block_call(): pl.pallas_call(functools.partial(block_kernel, scale), grid=(steps,), in_...  95.4 us
    ppermute x87, starting transfers between devices, shift(): return lax.ppermute(t, 'cp', [(i, i ^ bit) for i in range(n_dev)])  50.7 us
    unnamed x1, blocking collectives  49.8 us
  transfers between devices with their start and end apart: 88, of which 33 were waited for; matrix products, arithmetic and copies ran while one was open for 3% of the time, Pallas kernels for 24%

profile of v3, /device:TPU:0, one launch (start us, length us, event | category | flops | bytes accessed | tf_op | source)
XLA Modules:
  0.0 768.7 jit_solution(8488660898119752446)
XLA Ops:
  0.6 4.8 pad_maximum_fusion
  5.5 5.6 all-to-all-start
  12.6 49.8 %all-reduce = s32[512]{0:T(512)S(1)} all-reduce(s32[512]{0:T(512)S(1)} %dynamic-update-slice), channel_id=1, replica_groups=mesh['dp'=2,'cp'=8] {'cp'}, use_global_device_ids=true, to_apply=%add | all-reduce | flops 512 | bytes 4096
  64.7 6.2 norm.1
  73.5 95.4 %block.1 = (bf16[512,2048]{1,0:T(8,128)(2,1)}, bf16[512,2048]{1,0:T(8,128)(2,1)}, f32[1,2048]{1,0:T(1,128)}, bf16[256,2048]{1,0:T(8,128)(2,1)}, bf16[256,2048]{1...) custom-call(bf16[512,2048]{1,0:T(8,128)(2,1)} %copy-done.1, ...), custom_call_target="tpu_custom_call" | custom-call | flops 60000002048 | bytes 60000000 | tf_op jit(solution)/shard_map/block/pallas_call | solution.py:149
  173.6 21.6 %collective-permute-done.16.refs_20_ = bf16[256,2048]{1,0:T(8,128)(2,1)S(1)} collective-permute-done((bf16[256,2048]{1,0:T(8,128)(2,1)}, bf16[256,2048]{1,0:T(8,128)(2,1)S(1)}, u32[]{:S(2)}, u32[]{:S(2)}) %collective-permute-start.16) | collective-permute-done | bytes 1048608 | tf_op jit(solution)/shard_map/ppermute | solution.py:264
  196.3 21.4 %collective-permute-done.17.refs_21_ = bf16[256,2048]{1,0:T(8,128)(2,1)S(1)} collective-permute-done((bf16[256,2048]{1,0:T(8,128)(2,1)}, bf16[256,2048]{1,0:T(8,128)(2,1)S(1)}, u32[]{:S(2)}, u32[]{:S(2)}) %collective-permute-start.17) | collective-permute-done | bytes 1048608 | tf_op jit(solution)/shard_map/ppermute | solution.py:264
  218.4 87.1 %collective-permute-done.15.refs_19_ = bf16[256,2048]{1,0:T(8,128)(2,1)S(1)} collective-permute-done((bf16[256,2048]{1,0:T(8,128)(2,1)}, bf16[256,2048]{1,0:T(8,128)(2,1)S(1)}, u32[]{:S(2)}, u32[]{:S(2)}) %collective-permute-start.15) | collective-permute-done | bytes 1048608 | tf_op jit(solution)/shard_map/ppermute | solution.py:264
  311.5 20.1 %collective-permute-done.24.refs_28_ = bf16[256,2048]{1,0:T(8,128)(2,1)S(1)} collective-permute-done((bf16[256,2048]{1,0:T(8,128)(2,1)S(1)}, bf16[256,2048]{1,0:T(8,128)(2,1)S(1)}, u32[]{:S(2)}, u32[]{:S(2)}) %collective-permute-start.24) | collective-permute-done | bytes 1048608 | tf_op jit(solution)/shard_map/ppermute | solution.py:264
  344.9 37.3 %collective-permute-done.10.refs_12_.refs_0_ = bf16[2,2048,256]{2,1,0:T(8,128)(2,1)} collective-permute-done((bf16[2,2048,256]{2,1,0:T(8,128)(2,1)}, bf16[2,2048,256]{2,1,0:T(8,128)(2,1)}, u32[]{:S(2)}, u32[]{:S(2)}) %collective-permute-start.10) | collective-permute-done | bytes 2097184 | tf_op jit(solution)/shard_map/ppermute | solution.py:264
  389.8 51.8 %wgrad.5 = f32[2048,2048]{1,0:T(8,128)} custom-call(bf16[2,2048,256]{2,1,0:T(8,128)(2,1)} %get-tuple-element.70.refs_0_, bf16[2,2048,256]{2,1,0:T(8,128)(2,1)} %get-tuple-element.71.refs_1_, bf16[2,2048,256]{2,1,0:T(8,128)(2,1)} %collective-permute-done.refs_2_, bf16[2,2048,256]{2,1,0:T(8,128)(2,1)} %copy-done.4, ...), custom_call_target="tpu_custom_call" | custom-call | flops 34359738368 | bytes 80000000 | tf_op jit(solution)/shard_map/wgrad/pallas_call | solution.py:240
  451.5 20.6 %collective-permute-done.45.refs_28_ = bf16[256,2048]{1,0:T(8,128)(2,1)S(1)} collective-permute-done((bf16[256,2048]{1,0:T(8,128)(2,1)}, bf16[256,2048]{1,0:T(8,128)(2,1)S(1)}, u32[]{:S(2)}, u32[]{:S(2)}) %collective-permute-start.45) | collective-permute-done | bytes 1048608 | tf_op jit(solution)/shard_map/ppermute | solution.py:264
  480.1 48.7 %wgrad.6.refs_32_ = f32[2048,6144]{1,0:T(8,128)} custom-call(bf16[2,2048,256]{2,1,0:T(8,128)(2,1)} %get-tuple-element.70.refs_0_, bf16[2,2048,256]{2,1,0:T(8,128)(2,1)} %get-tuple-element.71.refs_1_, bf16[2,2048,256]{2,1,0:T(8,128)(2,1)} %collective-permute-done.refs_2_, bf16[2,2048,256]{2,1,0:T(8,128)(2,1)} %copy-done.4, ...), custom_call_target="tpu_custom_call" | custom-call | flops 34359738368 | bytes 80000000 | tf_op jit(solution)/shard_map/wgrad/pallas_call | solution.py:240
  546.7 4.5 collective-permute-done.33
  552.0 5.2 collective-permute-done.31
  561.7 21.5 %collective-permute-done.69.refs_28_ = bf16[256,2048]{1,0:T(8,128)(2,1)} collective-permute-done((bf16[256,2048]{1,0:T(8,128)(2,1)}, bf16[256,2048]{1,0:T(8,128)(2,1)}, u32[]{:S(2)}, u32[]{:S(2)}) %collective-permute-start.69) | collective-permute-done | bytes 1048608 | tf_op jit(solution)/shard_map/ppermute | solution.py:264
  594.9 48.6 %wgrad.7.refs_24_ = f32[2048,6144]{1,0:T(8,128)} custom-call(bf16[2,2048,256]{2,1,0:T(8,128)(2,1)} %get-tuple-element.70.refs_0_, bf16[2,2048,256]{2,1,0:T(8,128)(2,1)} %get-tuple-element.71.refs_1_, bf16[2,2048,256]{2,1,0:T(8,128)(2,1)} %collective-permute-done.refs_2_, bf16[2,2048,256]{2,1,0:T(8,128)(2,1)} %copy-done.4, ...), custom_call_target="tpu_custom_call", output_to_operand_aliasing={{}: (32, {})} | custom-call | flops 34359738368 | bytes 80000000 | tf_op jit(solution)/shard_map/wgrad/pallas_call | solution.py:240
  648.4 5.1 collective-permute-done.51
  654.4 4.9 collective-permute-done.55
  660.7 9.7 %collective-permute-done.52 = bf16[64,2048]{1,0:T(8,128)(2,1)S(1)} collective-permute-done((bf16[64,2048]{1,0:T(8,128)(2,1)S(1)}, bf16[64,2048]{1,0:T(8,128)(2,1)S(1)}, u32[]{:S(2)}, u32[]{:S(2)}) %collective-permute-start.52) | collective-permute-done | bytes 262176 | tf_op jit(solution)/shard_map/ppermute | solution.py:264
  671.8 7.0 collective-permute-done.53
  684.5 19.8 %collective-permute-done.77.refs_4_ = bf16[256,2048]{1,0:T(8,128)(2,1)} collective-permute-done((bf16[256,2048]{1,0:T(8,128)(2,1)}, bf16[256,2048]{1,0:T(8,128)(2,1)}, u32[]{:S(2)}, u32[]{:S(2)}) %collective-permute-start.77) | collective-permute-done | bytes 1048608 | tf_op jit(solution)/shard_map/ppermute | solution.py:264
  705.9 38.5 %wgrad.8.refs_8_ = f32[2048,6144]{1,0:T(8,128)} custom-call(bf16[2,2048,256]{2,1,0:T(8,128)(2,1)} %get-tuple-element.70.refs_0_, bf16[2,2048,256]{2,1,0:T(8,128)(2,1)} %get-tuple-element.71.refs_1_, bf16[2,2048,256]{2,1,0:T(8,128)(2,1)} %collective-permute-done.refs_2_, bf16[2,2048,256]{2,1,0:T(8,128)(2,1)} %copy-done.4, ...), custom_call_target="tpu_custom_call", output_to_operand_aliasing={{}: (24, {})} | custom-call | flops 25769803776 | bytes 80000000 | tf_op jit(solution)/shard_map/wgrad/pallas_call | solution.py:240
  746.4 22.2 %wgrad.9 = f32[2048,6144]{1,0:T(8,128)} custom-call(bf16[2,2048,256]{2,1,0:T(8,128)(2,1)} %collective-permute-done.10.refs_12_.refs_0_, bf16[2,2048,256]{2,1,0:T(8,128)(2,1)} %collective-permute-done.11.refs_13_.refs_1_, bf16[2,2048,256]{2,1,0:T(8,128)(2,1)} %copy-done.8, ...), custom_call_target="tpu_custom_call", output_to_operand_aliasing={{}: (8, {})} | custom-call | flops 8589934592 | bytes 80000000 | tf_op jit(solution)/shard_map/wgrad/pallas_call | solution.py:240
  (313 shorter events, 109.3 us)
Async XLA Ops:
  5.5 59.2 %all-to-all-start = ((bf16[8,128,2048]{2,1,0:T(8,128)(2,1)}), bf16[8,128,2048]{2,1,0:T(8,128)(2,1)}, u32[]{:S(2)}, u32[]{:S(2)}) async-start(bf16[8,128,2048]{2,1,0:T(8,128)(2,1)} %pad_maximum_fusion), calls=%async_computation | async-start | bytes 8388608 | tf_op jit(solution)/shard_map/all_to_all | solution.py:273
  170.1 47.7 %collective-permute-start.17 = (bf16[256,2048]{1,0:T(8,128)(2,1)}, bf16[256,2048]{1,0:T(8,128)(2,1)S(1)}, u32[]{:S(2)}, u32[]{:S(2)}) collective-permute-start(bf16[256,2048]{1,0:T(8,128)(2,1)} %get-tuple-element.79.refs_17_), channel_id=1, source_target_pairs={{0,4},{1,5},{2,6},{3,7},{4,0},{5,1},{6,2},{7,3},{8,12},{9,13},{10,... | collective-permute-start | bytes 3145736 | tf_op jit(solution)/shard_map/ppermute | solution.py:264
  171.7 133.8 %collective-permute-start.2 = (bf16[2,2048,256]{2,1,0:T(8,128)(2,1)S(1)}, bf16[2,2048,256]{2,1,0:T(8,128)(2,1)}, u32[]{:S(2)}, u32[]{:S(2)}) collective-permute-start(bf16[2,2048,256]{2,1,0:T(8,128)(2,1)S(1)} %copy-done.3), channel_id=1, source_target_pairs={{0,4},{1,5},{2,6},{3,7},{4,0},{5,1},{6,2},{7,3},{8,12},{9,13},{10,... | collective-permute-start | bytes 6291464 | tf_op jit(solution)/shard_map/ppermute | solution.py:264
  172.1 133.9 %collective-permute-start = (bf16[2,2048,256]{2,1,0:T(8,128)(2,1)S(1)}, bf16[2,2048,256]{2,1,0:T(8,128)(2,1)}, u32[]{:S(2)}, u32[]{:S(2)}) collective-permute-start(bf16[2,2048,256]{2,1,0:T(8,128)(2,1)S(1)} %copy-done.3), channel_id=1, source_target_pairs={{0,2},{1,3},{2,0},{3,1},{4,6},{5,7},{6,4},{7,5},{8,10},{9,11},{10,... | collective-permute-start | bytes 6291464 | tf_op jit(solution)/shard_map/ppermute | solution.py:264
  195.2 110.8 %collective-permute-start.3 = (bf16[2,2048,256]{2,1,0:T(8,128)(2,1)}, bf16[2,2048,256]{2,1,0:T(8,128)(2,1)}, u32[]{:S(2)}, u32[]{:S(2)}) collective-permute-start(bf16[2,2048,256]{2,1,0:T(8,128)(2,1)} %get-tuple-element.71.refs_1_), channel_id=1, source_target_pairs={{0,4},{1,5},{2,6},{3,7},{4,0},{5,1},{6,2},{7,3},{8,12},{9,13},{10,... | collective-permute-start | bytes 6291464 | tf_op jit(solution)/shard_map/ppermute | solution.py:264
  195.8 111.7 %collective-permute-start.1 = (bf16[2,2048,256]{2,1,0:T(8,128)(2,1)}, bf16[2,2048,256]{2,1,0:T(8,128)(2,1)S(1)}, u32[]{:S(2)}, u32[]{:S(2)}) collective-permute-start(bf16[2,2048,256]{2,1,0:T(8,128)(2,1)} %get-tuple-element.71.refs_1_), channel_id=1, source_target_pairs={{0,2},{1,3},{2,0},{3,1},{4,6},{5,7},{6,4},{7,5},{8,10},{9,11},{10,... | collective-permute-start | bytes 6291464 | tf_op jit(solution)/shard_map/ppermute | solution.py:264
  217.7 87.8 %collective-permute-start.15 = (bf16[256,2048]{1,0:T(8,128)(2,1)}, bf16[256,2048]{1,0:T(8,128)(2,1)S(1)}, u32[]{:S(2)}, u32[]{:S(2)}) collective-permute-start(bf16[256,2048]{1,0:T(8,128)(2,1)} %get-tuple-element.79.refs_17_), channel_id=1, source_target_pairs={{0,2},{1,3},{2,0},{3,1},{4,6},{5,7},{6,4},{7,5},{8,10},{9,11},{10,... | collective-permute-start | bytes 3145736 | tf_op jit(solution)/shard_map/ppermute | solution.py:264
  334.3 48.0 %collective-permute-start.10 = (bf16[2,2048,256]{2,1,0:T(8,128)(2,1)}, bf16[2,2048,256]{2,1,0:T(8,128)(2,1)}, u32[]{:S(2)}, u32[]{:S(2)}) collective-permute-start(bf16[2,2048,256]{2,1,0:T(8,128)(2,1)} %collective-permute-done.refs_2_), channel_id=1, source_target_pairs={{0,4},{1,5},{2,6},{3,7},{4,0},{5,1},{6,2},{7,3},{8,12},{9,13},{10,... | collective-permute-start | bytes 6291464 | tf_op jit(solution)/shard_map/ppermute | solution.py:264
  335.8 48.0 %collective-permute-start.11 = (bf16[2,2048,256]{2,1,0:T(8,128)(2,1)}, bf16[2,2048,256]{2,1,0:T(8,128)(2,1)}, u32[]{:S(2)}, u32[]{:S(2)}) collective-permute-start(bf16[2,2048,256]{2,1,0:T(8,128)(2,1)} %collective-permute-done.3.refs_5_), channel_id=1, source_target_pairs={{0,2},{1,3},{2,0},{3,1},{4,6},{5,7},{6,4},{7,5},{8,10},{9,11},{10,... | collective-permute-start | bytes 6291464 | tf_op jit(solution)/shard_map/ppermute | solution.py:264
  338.8 45.1 %collective-permute-start.8 = (bf16[2,2048,256]{2,1,0:T(8,128)(2,1)}, bf16[2,2048,256]{2,1,0:T(8,128)(2,1)}, u32[]{:S(2)}, u32[]{:S(2)}) collective-permute-start(bf16[2,2048,256]{2,1,0:T(8,128)(2,1)} %collective-permute-done.2.refs_4_), channel_id=1, source_target_pairs={{0,1},{1,0},{2,3},{3,2},{4,5},{5,4},{6,7},{7,6},{8,9},{9,8},{10,11... | collective-permute-start | bytes 6291464 | tf_op jit(solution)/shard_map/ppermute | solution.py:264
  383.9 61.4 %collective-permute-start.37 = (bf16[256,2048]{1,0:T(8,128)(2,1)}, bf16[256,2048]{1,0:T(8,128)(2,1)}, u32[]{:S(2)}, u32[]{:S(2)}) collective-permute-start(bf16[256,2048]{1,0:T(8,128)(2,1)} %get-tuple-element.88.refs_16_), channel_id=1, source_target_pairs={{0,4},{1,5},{2,6},{3,7},{4,0},{5,1},{6,2},{7,3},{8,12},{9,13},{10,... | collective-permute-start | bytes 3145736 | tf_op jit(solution)/shard_map/ppermute | solution.py:264
  385.3 60.3 %collective-permute-start.35 = (bf16[256,2048]{1,0:T(8,128)(2,1)}, bf16[256,2048]{1,0:T(8,128)(2,1)}, u32[]{:S(2)}, u32[]{:S(2)}) collective-permute-start(bf16[256,2048]{1,0:T(8,128)(2,1)} %get-tuple-element.88.refs_16_), channel_id=1, source_target_pairs={{0,2},{1,3},{2,0},{3,1},{4,6},{5,7},{6,4},{7,5},{8,10},{9,11},{10,... | collective-permute-start | bytes 3145736 | tf_op jit(solution)/shard_map/ppermute | solution.py:264
  386.0 59.7 %collective-permute-start.38 = (bf16[256,2048]{1,0:T(8,128)(2,1)}, bf16[256,2048]{1,0:T(8,128)(2,1)}, u32[]{:S(2)}, u32[]{:S(2)}) collective-permute-start(bf16[256,2048]{1,0:T(8,128)(2,1)} %get-tuple-element.89.refs_17_), channel_id=1, source_target_pairs={{0,4},{1,5},{2,6},{3,7},{4,0},{5,1},{6,2},{7,3},{8,12},{9,13},{10,... | collective-permute-start | bytes 3145736 | tf_op jit(solution)/shard_map/ppermute | solution.py:264
  387.0 58.7 %collective-permute-start.36 = (bf16[256,2048]{1,0:T(8,128)(2,1)}, bf16[256,2048]{1,0:T(8,128)(2,1)}, u32[]{:S(2)}, u32[]{:S(2)}) collective-permute-start(bf16[256,2048]{1,0:T(8,128)(2,1)} %get-tuple-element.89.refs_17_), channel_id=1, source_target_pairs={{0,2},{1,3},{2,0},{3,1},{4,6},{5,7},{6,4},{7,5},{8,10},{9,11},{10,... | collective-permute-start | bytes 3145736 | tf_op jit(solution)/shard_map/ppermute | solution.py:264
  474.0 57.1 %collective-permute-start.61 = (bf16[256,2048]{1,0:T(8,128)(2,1)S(1)}, bf16[256,2048]{1,0:T(8,128)(2,1)}, u32[]{:S(2)}, u32[]{:S(2)}) collective-permute-start(bf16[256,2048]{1,0:T(8,128)(2,1)S(1)} %copy-done.12), channel_id=1, source_target_pairs={{0,4},{1,5},{2,6},{3,7},{4,0},{5,1},{6,2},{7,3},{8,12},{9,13},{10,... | collective-permute-start | bytes 3145736 | tf_op jit(solution)/shard_map/ppermute | solution.py:264
  474.9 56.3 %collective-permute-start.59 = (bf16[256,2048]{1,0:T(8,128)(2,1)S(1)}, bf16[256,2048]{1,0:T(8,128)(2,1)}, u32[]{:S(2)}, u32[]{:S(2)}) collective-permute-start(bf16[256,2048]{1,0:T(8,128)(2,1)S(1)} %copy-done.12), channel_id=1, source_target_pairs={{0,2},{1,3},{2,0},{3,1},{4,6},{5,7},{6,4},{7,5},{8,10},{9,11},{10,... | collective-permute-start | bytes 3145736 | tf_op jit(solution)/shard_map/ppermute | solution.py:264
  475.7 57.9 %collective-permute-start.62 = (bf16[256,2048]{1,0:T(8,128)(2,1)}, bf16[256,2048]{1,0:T(8,128)(2,1)}, u32[]{:S(2)}, u32[]{:S(2)}) collective-permute-start(bf16[256,2048]{1,0:T(8,128)(2,1)} %get-tuple-element.104.refs_17_), channel_id=1, source_target_pairs={{0,4},{1,5},{2,6},{3,7},{4,0},{5,1},{6,2},{7,3},{8,12},{9,13},{10,... | collective-permute-start | bytes 3145736 | tf_op jit(solution)/shard_map/ppermute | solution.py:264
  476.7 58.4 %collective-permute-start.60 = (bf16[256,2048]{1,0:T(8,128)(2,1)}, bf16[256,2048]{1,0:T(8,128)(2,1)}, u32[]{:S(2)}, u32[]{:S(2)}) collective-permute-start(bf16[256,2048]{1,0:T(8,128)(2,1)} %get-tuple-element.104.refs_17_), channel_id=1, source_target_pairs={{0,2},{1,3},{2,0},{3,1},{4,6},{5,7},{6,4},{7,5},{8,10},{9,11},{10,... | collective-permute-start | bytes 3145736 | tf_op jit(solution)/shard_map/ppermute | solution.py:264
  479.1 57.4 %collective-permute-start.57 = (f32[1,2048]{1,0:T(1,128)S(1)}, f32[1,2048]{1,0:T(1,128)S(1)}, u32[]{:S(2)}, u32[]{:S(2)}) collective-permute-start(f32[1,2048]{1,0:T(1,128)S(1)} %add.23), channel_id=1, source_target_pairs={{0,2},{1,3},{2,0},{3,1},{4,6},{5,7},{6,4},{7,5},{8,10},{9,11},{10,... | collective-permute-start | bytes 24584 | tf_op jit(solution)/shard_map/ppermute | solution.py:264
  589.9 53.7 %collective-permute-start.75 = (bf16[256,2048]{1,0:T(8,128)(2,1)S(1)}, bf16[256,2048]{1,0:T(8,128)(2,1)}, u32[]{:S(2)}, u32[]{:S(2)}) collective-permute-start(bf16[256,2048]{1,0:T(8,128)(2,1)S(1)} %copy-done.10), channel_id=1, source_target_pairs={{0,4},{1,5},{2,6},{3,7},{4,0},{5,1},{6,2},{7,3},{8,12},{9,13},{10,... | collective-permute-start | bytes 3145736 | tf_op jit(solution)/shard_map/ppermute | solution.py:264
  591.1 53.6 %collective-permute-start.73 = (bf16[256,2048]{1,0:T(8,128)(2,1)S(1)}, bf16[256,2048]{1,0:T(8,128)(2,1)}, u32[]{:S(2)}, u32[]{:S(2)}) collective-permute-start(bf16[256,2048]{1,0:T(8,128)(2,1)S(1)} %copy-done.10), channel_id=1, source_target_pairs={{0,2},{1,3},{2,0},{3,1},{4,6},{5,7},{6,4},{7,5},{8,10},{9,11},{10,... | collective-permute-start | bytes 3145736 | tf_op jit(solution)/shard_map/ppermute | solution.py:264
  591.9 52.8 %collective-permute-start.76 = (bf16[256,2048]{1,0:T(8,128)(2,1)}, bf16[256,2048]{1,0:T(8,128)(2,1)}, u32[]{:S(2)}, u32[]{:S(2)}) collective-permute-start(bf16[256,2048]{1,0:T(8,128)(2,1)} %get-tuple-element.118.refs_13_), channel_id=1, source_target_pairs={{0,4},{1,5},{2,6},{3,7},{4,0},{5,1},{6,2},{7,3},{8,12},{9,13},{10,... | collective-permute-start | bytes 3145736 | tf_op jit(solution)/shard_map/ppermute | solution.py:264
  592.8 51.9 %collective-permute-start.74 = (bf16[256,2048]{1,0:T(8,128)(2,1)}, bf16[256,2048]{1,0:T(8,128)(2,1)S(1)}, u32[]{:S(2)}, u32[]{:S(2)}) collective-permute-start(bf16[256,2048]{1,0:T(8,128)(2,1)} %get-tuple-element.118.refs_13_), channel_id=1, source_target_pairs={{0,2},{1,3},{2,0},{3,1},{4,6},{5,7},{6,4},{7,5},{8,10},{9,11},{10,... | collective-permute-start | bytes 3145736 | tf_op jit(solution)/shard_map/ppermute | solution.py:264
  594.0 52.2 %collective-permute-start.50 = (bf16[64,2048]{1,0:T(8,128)(2,1)}, bf16[64,2048]{1,0:T(8,128)(2,1)}, u32[]{:S(2)}, u32[]{:S(2)}) collective-permute-start(bf16[64,2048]{1,0:T(8,128)(2,1)} %get-tuple-element.126), channel_id=1, source_target_pairs={{0,2},{1,3},{2,0},{3,1},{4,6},{5,7},{6,4},{7,5},{8,10},{9,11},{10,... | collective-permute-start | bytes 786440 | tf_op jit(solution)/shard_map/ppermute | solution.py:264
  (124 other events, 2875.3 us)

commit v4 on v3

--- a/solution.py
+++ b/solution.py
@@ -32,8 +32,9 @@
     return jnp.where(first_half, pltpu.roll(t, width - 32, 1), pltpu.roll(t, 32, 1))
 
 
-def block_kernel(scale, x_ref, r_ref, dy_ref, gain_ref, wq_ref, wk_ref, wv_ref, wo_ref, cos_ref, sin_ref,
-                 y_ref, dx_ref, gg_ref, oa_ref, ob_ref, qa_ref, qb_ref, ka_ref, kb_ref, va_ref, vb_ref, y_acc, dn_acc):
+def block_kernel(scale, me_ref, x_ref, r_ref, dy_ref, gain_ref, wq_ref, wk_ref, wv_ref, wo_ref, cos_ref, sin_ref,
+                 gg_ref, oa_ref, ob_ref, qa_ref, qb_ref, ka_ref, kb_ref, va_ref, vb_ref, *rest):
+    back_refs, (y_acc, dn_acc) = rest[:-2], rest[-2:]
     step = pl.program_id(0)
     seq = x_ref.shape[0]
     qb = 256
@@ -126,7 +127,6 @@
 
     @pl.when(step == pl.num_programs(0) - 1)
     def _():
-        y_ref[...] = y_acc[...].astype(BF16)
         x = x_ref[...].astype(F32)
         inv = lax.rsqrt(jnp.mean(x * x, axis=1, keepdims=True) + NORM_EPS)
         x_hat = x * inv
@@ -134,10 +134,15 @@
         gg_ref[...] = jnp.sum(dn * x_hat, axis=0, keepdims=True)
         d_hat = dn * gain_ref[...]
         dx = inv * (d_hat - x_hat * jnp.mean(d_hat * x_hat, axis=1, keepdims=True))
-        dx_ref[...] = (dy_ref[...].astype(F32) + dx).astype(BF16)
-
-
-def block_call(x, r, dy, gain, w_qkv, w_out, cos, sin, scale):
+        dn_acc[...] = dy_ref[...].astype(F32) + dx
+        piece = back_refs[0].shape[1]
+        for m, ref in enumerate(back_refs):
+            rows = pl.ds(pl.multiple_of(jnp.bitwise_xor(me_ref[0], m) * piece, piece), piece)
+            ref[0] = y_acc[rows, :].astype(BF16)
+            ref[1] = dn_acc[rows, :].astype(BF16)
+
+
+def block_call(me, x, r, dy, gain, w_qkv, w_out, cos, sin, scale, n_dev):
     seq, hidden = x.shape
     width = w_out.shape[0]
     hb = 256
@@ -146,19 +151,41 @@
     wcol = lambda part: pl.BlockSpec((hidden, hb), lambda j, part=part: (0, part * steps + j))
     tok = pl.BlockSpec((seq // 2, hb), lambda j: (0, j))
     full = lambda s: pl.BlockSpec(s, lambda j: (0, 0))
+    back = (2, seq // n_dev, hidden)
     return pl.pallas_call(
         functools.partial(block_kernel, scale),
         grid=(steps,),
-        in_specs=[whole(x), whole(r), whole(dy), whole(gain), wcol(0), wcol(1), wcol(2),
+        in_specs=[pl.BlockSpec(memory_space=pltpu.SMEM), whole(x), whole(r), whole(dy), whole(gain), wcol(0), wcol(1), wcol(2),
                   pl.BlockSpec((hb, hidden), lambda j: (j, 0)), whole(cos), whole(sin)],
-        out_specs=[full((seq, hidden)), full((seq, hidden)), full((1, hidden))] + [tok] * 8,
-        out_shape=[jax.ShapeDtypeStruct((seq, hidden), BF16), jax.ShapeDtypeStruct((seq, hidden), BF16),
-                   jax.ShapeDtypeStruct((1, hidden), F32)] + [jax.ShapeDtypeStruct((seq // 2, width), BF16)] * 8,
+        out_specs=[full((1, hidden))] + [tok] * 8 + [pl.BlockSpec(back, lambda j: (0, 0, 0))] * n_dev,
+        out_shape=[jax.ShapeDtypeStruct((1, hidden), F32)] + [jax.ShapeDtypeStruct((seq // 2, width), BF16)] * 8
+        + [jax.ShapeDtypeStruct(back, BF16)] * n_dev,
         scratch_shapes=[pltpu.VMEM((seq, hidden), F32), pltpu.VMEM((seq, hidden), F32)],
         compiler_params=pltpu.CompilerParams(dimension_semantics=("arbitrary",), vmem_limit_bytes=60 << 20),
         cost_estimate=pl.CostEstimate(flops=60_000_000_000, bytes_accessed=60_000_000, transcendentals=8_000_000),
         name="block",
-    )(x, r, dy, gain, w_qkv, w_qkv, w_qkv, w_out, cos, sin)
+    )(me, x, r, dy, gain, w_qkv, w_qkv, w_qkv, w_out, cos, sin)
+
+
+def join_kernel(me_ref, *refs):
+    y_ref, dx_ref = refs[-2:]
+    for m, ref in enumerate(refs[:-2]):
+        owner = jnp.bitwise_xor(me_ref[0], m)
+        y_ref[owner] = ref[0]
+        dx_ref[owner] = ref[1]
+
+
+def join_call(me, parts):
+    n_dev = len(parts)
+    _, piece, hidden = parts[0].shape
+    return pl.pallas_call(
+        join_kernel,
+        in_specs=[pl.BlockSpec(memory_space=pltpu.SMEM)] + [pl.BlockSpec(memory_space=pltpu.VMEM)] * n_dev,
+        out_shape=[jax.ShapeDtypeStruct((n_dev, piece, hidden), BF16)] * 2,
+        compiler_params=pltpu.CompilerParams(vmem_limit_bytes=32 << 20),
+        cost_estimate=pl.CostEstimate(flops=1_000_000, bytes_accessed=8_000_000, transcendentals=0),
+        name="join",
+    )(me, *parts)
 
 
 def norm_kernel(both_ref, gain_ref, x_ref, dy_ref, r_ref, *pair_refs):
@@ -208,7 +235,9 @@
     def body(i, carry):
         rows = pl.ds(pl.multiple_of(i * sub, sub), sub)
         tile = dot(l_buf[rows, :], r_buf[...])
-        if flip:
+        if flip and add:
+            out_ref[:, rows] = refs[2 * count][:, rows] + tile.T
+        elif flip:
             out_ref[:, rows] = tile.T
         elif add:
             out_ref[rows, :] = refs[2 * count][rows, :] + tile
@@ -253,19 +282,14 @@
 
 def solution(mesh):
     def device_fn(x_in, positions, long_factor, norm_gain, w_qkv, w_out, grad_y):
-        _, piece, hidden = x_in.shape
+        _, _, hidden = x_in.shape
         n_dev = mesh.shape['cp']
         width = w_out.shape[0]
         scale = 1.0 / math.sqrt(2 * long_factor.shape[0])
-        me = lax.axis_index('cp')
-        mine = jnp.bitwise_xor(me, jnp.arange(n_dev))
+        me = lax.axis_index('cp').astype(jnp.int32)[None]
 
         def shift(t, bit):
             return lax.ppermute(t, 'cp', [(i, i ^ bit) for i in range(n_dev)])
-
-        def swap(t):
-            sent = t[mine]
-            return jnp.stack([sent[0]] + [shift(sent[m], m) for m in range(1, n_dev)])[mine]
 
         def after(values, deps):
             return lax.optimization_barrier((values, deps))[0]
@@ -275,43 +299,55 @@
         cos, sin = rope_tables(pos, long_factor)
         x, dy, r, pair_a, pair_b = norm_call(both, norm_gain[None, :])
 
+        def own(ab):
+            a, b = ab
+            return [a, b, shift(a, 1), shift(b, 1)]
+
         def near(ab):
             a, b = ab
-            return [a, b, shift(a, 2), shift(b, 2), shift(a, 4), shift(b, 4)]
-
-        def far(pieces, deps=()):
-            pieces = after(pieces, deps)
-            diag = [shift(pieces[2], 4), shift(pieces[5], 2)]
-            return pieces + [shift(t, 1) for t in pieces], diag + [shift(t, 1) for t in diag]
-
-        pair_part = near((pair_a, pair_b))
-        out = block_call(x, r, dy, norm_gain[None, :], w_qkv, w_out, cos, sin, scale)
-        y, dx, gg = out[:3]
-        pair_near, pair_far = far(pair_part, (gg,))
-        o_part = near(out[3:5])
-        q_part = near(out[5:7])
-        k_part = near(after(out[7:9], o_part))
-        o_near, o_far = far(o_part)
+            return [shift(a, 2), shift(b, 2), shift(a, 4), shift(b, 4)]
+
+        def far(part, deps=()):
+            part = after(part, deps)
+            diag = [shift(part[0], 4), shift(part[3], 2)]
+            every = list(part) + diag
+            return every + [shift(t, 1) for t in every]
+
+        p_ab = (pair_a, pair_b)
+        p_part, p_own = near(p_ab), own(p_ab)
+        out = block_call(me, x, r, dy, norm_gain[None, :], w_qkv, w_out, cos, sin, scale, n_dev)
+        gg = out[0]
+        o_ab, q_ab, k_ab, v_ab = (tuple(out[i:i + 2]) for i in (1, 3, 5, 7))
+        back = out[9:]
         gg1 = shift(gg, 1)
-        g_wout = grad_call(pair_near + pair_far, o_near + o_far, 1, hidden, 0, flip=True)
-        y_out = swap(after(y, g_wout).reshape(n_dev, piece, hidden))
-        gg, gg1 = after((gg, gg1), g_wout)
+        p_rest = far(p_part, (gg,))
+        o_part = near(o_ab)
+        cols = 3 * width
+        g_wout = grad_call(p_own, own(o_ab), 1, hidden, 0, flip=True)
+        g_wqkv = grad_call(p_own, own(q_ab), 0, cols, 0)
+        g_wqkv = grad_call(p_own, own(k_ab), 0, cols, width, g_wqkv)
+        g_wqkv = grad_call(p_own, own(v_ab), 0, cols, 2 * width, g_wqkv)
+        gg, gg1 = after((gg, gg1), g_wqkv)
         gg = gg + gg1
+        o_rest = far(o_part, (g_wqkv, g_wout))
         gg2 = shift(gg, 2)
-        v_part = near(after(out[9:11], q_part))
-        q_near, q_far = far(q_part, (g_wout,))
-        g_wqkv = grad_call(pair_near + pair_far, q_near + q_far, 0, 3 * width, 0)
-        grad_x = swap(after(dx, g_wqkv).reshape(n_dev, piece, hidden))
-        gg, gg2 = after((gg, gg2), g_wqkv)
+        q_part = near(after(q_ab, o_part))
+        k_part = near(after(k_ab, o_part))
+        g_wout = grad_call(p_rest, o_rest, 1, hidden, 0, g_wout, flip=True, add=True)
+        gg, gg2 = after((gg, gg2), g_wout)
         gg = gg + gg2
+        q_rest = far(q_part, (g_wout,))
         gg4 = shift(gg, 4)
-        k_near, k_far = far(k_part, (g_wqkv,))
-        g_wqkv = grad_call(pair_near + pair_far, k_near + k_far, 0, 3 * width, width, g_wqkv)
+        v_part = near(after(v_ab, q_part))
+        k_rest = far(k_part, (g_wout,))
+        g_wqkv = grad_call(p_rest, q_rest, 0, cols, 0, g_wqkv, add=True)
         gg, gg4 = after((gg, gg4), g_wqkv)
         g_gain = (gg + gg4)[0]
-        v_near, v_far = far(v_part, (g_wqkv,))
-        g_wqkv = grad_call(pair_near, v_near, 0, 3 * width, 2 * width, g_wqkv)
-        g_wqkv = grad_call(pair_far, v_far, 0, 3 * width, 2 * width, g_wqkv, add=True)
+        v_rest = far(v_part, (g_wqkv,))
+        back = [back[0]] + [shift(t, m + 1) for m, t in enumerate(after(back[1:], g_wqkv))]
+        g_wqkv = grad_call(p_rest, k_rest, 0, cols, width, g_wqkv, add=True)
+        g_wqkv = grad_call(p_rest, v_rest, 0, cols, 2 * width, g_wqkv, add=True)
+        y_out, grad_x = join_call(*after((me, back), g_wqkv))
         return y_out, grad_x, g_gain, g_wqkv, g_wout
 
     seq_spec = P('dp', 'cp', None)

time: 769 us -> 781 us (1.016)
  Pallas kernels: 311 us -> 342 us
  local copies, waits for them, and re-layouts: 27.5 us -> 9.99 us
  starting transfers between devices: 56.2 us -> 44.9 us
  waiting for transfers between devices: 314 us -> 323 us
    pallas_call x5 -> x8, Pallas kernels: 210 us -> 238 us  [grad_call(): pl.pallas_call(functools.partial(grad_kernel, count, flip, add), grid=(ro...]
    ppermute x87 -> x80, starting transfers between devices: 50.7 us -> 39.3 us  [shift(): return lax.ppermute(t, 'cp', [(i, i ^ bit) for i in range(n_dev)])]
    gather x4 -> x0, local copies, waits for them, and re-layouts: 10.3 us -> none  [the longest x2 5.74 us: swap(): jnp.stack([sent[0]] + [shift(sent[m], m) for m in range(1, n_dev)])[mine]]
    ppermute x87 -> x80, waiting for transfers between devices: 314 us -> 323 us  [shift(): return lax.ppermute(t, 'cp', [(i, i ^ bit) for i in range(n_dev)])]
  transfers between devices with their start and end apart: 88 -> 81, of which waited for: 33 -> 34; matrix products, arithmetic and copies ran while one was open for 3% -> 0% of each run, Pallas kernels for 24% -> 31%
where the time goes in v4:
time: 781 us; the launch traced here: 780 us
  Pallas kernels  342 us (44%)
  waiting for transfers between devices  323 us (41%)
  blocking collectives  49.8 us (6%)
  starting transfers between devices  44.9 us (6%)
  local copies, waits for them, and re-layouts  9.99 us (1%)
    ppermute x80, waiting for transfers between devices, shift(): return lax.ppermute(t, 'cp', [(i, i ^ bit) for i in range(n_dev)])  323 us
    pallas_call x8, Pallas kernels, grad_call(): pl.pallas_call(functools.partial(grad_kernel, count, flip, add), grid=(ro...  238 us
    pallas_call x1, Pallas kernels, block_call(): pl.pallas_call(functools.partial(block_kernel, scale), grid=(steps,), in_...  95.5 us
    unnamed x1, blocking collectives  49.8 us
    ppermute x80, starting transfers between devices, shift(): return lax.ppermute(t, 'cp', [(i, i ^ bit) for i in range(n_dev)])  39.3 us
  transfers between devices with their start and end apart: 81, of which 34 were waited for; matrix products, arithmetic and copies ran while one was open for 0% of the time, Pallas kernels for 31%

profile of v4, /device:TPU:0, one launch (start us, length us, event | category | flops | bytes accessed | tf_op | source)
XLA Modules:
  0.0 779.6 jit_solution(14754886404631362008)
XLA Ops:
  12.6 49.8 %all-reduce = s32[512]{0:T(512)S(1)} all-reduce(s32[512]{0:T(512)S(1)} %dynamic-update-slice), channel_id=1, replica_groups=mesh['dp'=2,'cp'=8] {'cp'}, use_global_device_ids=true, to_apply=%add | all-reduce | flops 512 | bytes 4096
  64.7 6.2 norm.1
  73.5 95.5 %block.1 = (f32[1,2048]{1,0:T(1,128)}, bf16[256,2048]{1,0:T(8,128)(2,1)}, bf16[256,2048]{1,0:T(8,128)(2,1)}, bf16[256,2048]{1,0:T(8,128)(2,1)}, bf16[256,2048]{1...) custom-call(s32[1]{0:T(128)} %bitcast.me_ref, ...), custom_call_target="tpu_custom_call" | custom-call | flops 60000002048 | bytes 60000000 | tf_op jit(solution)/shard_map/block/pallas_call | solution.py:155
  183.2 19.4 %collective-permute-done.12.refs_12_ = bf16[256,2048]{1,0:T(8,128)(2,1)S(1)} collective-permute-done((bf16[256,2048]{1,0:T(8,128)(2,1)}, bf16[256,2048]{1,0:T(8,128)(2,1)S(1)}, u32[]{:S(2)}, u32[]{:S(2)}) %collective-permute-start.12) | collective-permute-done | bytes 1048608 | tf_op jit(solution)/shard_map/ppermute | solution.py:292
  203.2 21.9 %collective-permute-done.13.refs_13_ = bf16[256,2048]{1,0:T(8,128)(2,1)S(1)} collective-permute-done((bf16[256,2048]{1,0:T(8,128)(2,1)}, bf16[256,2048]{1,0:T(8,128)(2,1)S(1)}, u32[]{:S(2)}, u32[]{:S(2)}) %collective-permute-start.13) | collective-permute-done | bytes 1048608 | tf_op jit(solution)/shard_map/ppermute | solution.py:292
  227.1 21.8 %collective-permute-done.15.refs_15_ = bf16[256,2048]{1,0:T(8,128)(2,1)S(1)} collective-permute-done((bf16[256,2048]{1,0:T(8,128)(2,1)}, bf16[256,2048]{1,0:T(8,128)(2,1)S(1)}, u32[]{:S(2)}, u32[]{:S(2)}) %collective-permute-start.15) | collective-permute-done | bytes 1048608 | tf_op jit(solution)/shard_map/ppermute | solution.py:292
  251.6 18.5 %collective-permute-done.refs_0_ = bf16[2,2048,256]{2,1,0:T(8,128)(2,1)S(1)} collective-permute-done((bf16[2,2048,256]{2,1,0:T(8,128)(2,1)}, bf16[2,2048,256]{2,1,0:T(8,128)(2,1)S(1)}, u32[]{:S(2)}, u32[]{:S(2)}) %collective-permute-start) | collective-permute-done | bytes 2097184 | tf_op jit(solution)/shard_map/ppermute | solution.py:292
  270.8 18.1 %wgrad.8.refs_8_ = f32[2048,6144]{1,0:T(8,128)} custom-call(bf16[2,2048,256]{2,1,0:T(8,128)(2,1)} %get-tuple-element.88.refs_0_, bf16[2,2048,256]{2,1,0:T(8,128)(2,1)} %get-tuple-element.89.refs_1_, bf16[2,2048,256]{2,1,0:T(8,128)(2,1)} %copy-done.14, bf16[2,2048,256]{2,1,0:T(8,128)(2,1)} %copy-done.15, bf16[256,2048]{1,0:T(8,128)(2,1)} %get-tuple-element.99.refs_4_, ...), custom_call_target="tpu_custom_call" | custom-call | flops 8589934592 | bytes 80000000 | tf_op jit(solution)/shard_map/wgrad/pallas_call | solution.py:269
  288.9 19.9 %wgrad.11.refs_24_ = f32[2048,2048]{1,0:T(8,128)} custom-call(bf16[2,2048,256]{2,1,0:T(8,128)(2,1)} %get-tuple-element.88.refs_0_, bf16[2,2048,256]{2,1,0:T(8,128)(2,1)} %get-tuple-element.89.refs_1_, bf16[2,2048,256]{2,1,0:T(8,128)(2,1)} %copy-done.14, bf16[2,2048,256]{2,1,0:T(8,128)(2,1)} %copy-done.15, bf16[256,2048]{1,0:T(8,128)(2,1)} %get-tuple-element.97.refs_4_, ...), custom_call_target="tpu_custom_call" | custom-call | flops 8589934592 | bytes 80000000 | tf_op jit(solution)/shard_map/wgrad/pallas_call | solution.py:269
  308.8 6.2 collective-permute-done.1.refs_1_
  317.1 25.6 %collective-permute-done.3.refs_3_ = bf16[2,2048,256]{2,1,0:T(8,128)(2,1)} collective-permute-done((bf16[2,2048,256]{2,1,0:T(8,128)(2,1)}, bf16[2,2048,256]{2,1,0:T(8,128)(2,1)}, u32[]{:S(2)}, u32[]{:S(2)}) %collective-permute-start.3) | collective-permute-done | bytes 2097184 | tf_op jit(solution)/shard_map/ppermute | solution.py:292
  343.7 16.3 %collective-permute-done.17.refs_13_ = bf16[256,2048]{1,0:T(8,128)(2,1)S(1)} collective-permute-done((bf16[256,2048]{1,0:T(8,128)(2,1)}, bf16[256,2048]{1,0:T(8,128)(2,1)S(1)}, u32[]{:S(2)}, u32[]{:S(2)}) %collective-permute-start.17) | collective-permute-done | bytes 1048608 | tf_op jit(solution)/shard_map/ppermute | solution.py:292
  361.0 18.1 %wgrad.9.refs_8_ = f32[2048,6144]{1,0:T(8,128)} custom-call(bf16[2,2048,256]{2,1,0:T(8,128)(2,1)} %get-tuple-element.88.refs_0_, bf16[2,2048,256]{2,1,0:T(8,128)(2,1)} %get-tuple-element.89.refs_1_, bf16[2,2048,256]{2,1,0:T(8,128)(2,1)} %copy-done.14, bf16[2,2048,256]{2,1,0:T(8,128)(2,1)} %copy-done.15, ...), custom_call_target="tpu_custom_call", output_to_operand_aliasing={{}: (8, {})} | custom-call | flops 8589934592 | bytes 80000000 | tf_op jit(solution)/shard_map/wgrad/pallas_call | solution.py:269
  379.1 18.2 %wgrad.10.refs_24_ = f32[2048,6144]{1,0:T(8,128)} custom-call(bf16[2,2048,256]{2,1,0:T(8,128)(2,1)} %get-tuple-element.88.refs_0_, bf16[2,2048,256]{2,1,0:T(8,128)(2,1)} %get-tuple-element.89.refs_1_, bf16[2,2048,256]{2,1,0:T(8,128)(2,1)} %copy-done.14, bf16[2,2048,256]{2,1,0:T(8,128)(2,1)} %copy-done.15, ...), custom_call_target="tpu_custom_call", output_to_operand_aliasing={{}: (8, {})} | custom-call | flops 8589934592 | bytes 80000000 | tf_op jit(solution)/shard_map/wgrad/pallas_call | solution.py:269
  410.0 22.5 %collective-permute-done.68.refs_15_ = bf16[256,2048]{1,0:T(8,128)(2,1)S(1)} collective-permute-done((bf16[256,2048]{1,0:T(8,128)(2,1)}, bf16[256,2048]{1,0:T(8,128)(2,1)S(1)}, u32[]{:S(2)}, u32[]{:S(2)}) %collective-permute-start.68) | collective-permute-done | bytes 1048608 | tf_op jit(solution)/shard_map/ppermute | solution.py:292
  432.4 19.1 %collective-permute-done.30.refs_16_ = bf16[256,2048]{1,0:T(8,128)(2,1)S(1)} collective-permute-done((bf16[256,2048]{1,0:T(8,128)(2,1)}, bf16[256,2048]{1,0:T(8,128)(2,1)S(1)}, u32[]{:S(2)}, u32[]{:S(2)}) %collective-permute-start.30) | collective-permute-done | bytes 1048608 | tf_op jit(solution)/shard_map/ppermute | solution.py:292
  460.7 38.9 %collective-permute-done.4.refs_4_ = bf16[2,2048,256]{2,1,0:T(8,128)(2,1)S(1)} collective-permute-done((bf16[2,2048,256]{2,1,0:T(8,128)(2,1)S(1)}, bf16[2,2048,256]{2,1,0:T(8,128)(2,1)S(1)}, u32[]{:S(2)}, u32[]{:S(2)}) %collective-permute-start.4) | collective-permute-done | bytes 2097184 | tf_op jit(solution)/shard_map/ppermute | solution.py:292
  511.3 42.7 %wgrad.12 = f32[2048,2048]{1,0:T(8,128)} custom-call(bf16[2,2048,256]{2,1,0:T(8,128)(2,1)} %copy-done.4, bf16[2,2048,256]{2,1,0:T(8,128)(2,1)} %copy-done.5, bf16[2,2048,256]{2,1,0:T(8,128)(2,1)} %collective-permute-done.2.refs_2_, bf16[2,2048,256]{2,1,0:T(8,128)(2,1)} %collective-permute-done.3.refs_3_, ...), custom_call_target="tpu_custom_call", output_to_operand_aliasing={{}: (24, {})} | custom-call | flops 25769803776 | bytes 80000000 | tf_op jit(solution)/shard_map/wgrad/pallas_call | solution.py:269
  557.4 22.2 %collective-permute-done.79 = f32[1,2048]{1,0:T(1,128)S(1)} collective-permute-done((f32[1,2048]{1,0:T(1,128)S(1)}, f32[1,2048]{1,0:T(1,128)S(1)}, u32[]{:S(2)}, u32[]{:S(2)}) %collective-permute-start.79) | collective-permute-done | bytes 8224 | tf_op jit(solution)/shard_map/ppermute | solution.py:292
  584.2 21.1 %collective-permute-done.69.refs_16_ = bf16[256,2048]{1,0:T(8,128)(2,1)S(1)} collective-permute-done((bf16[256,2048]{1,0:T(8,128)(2,1)S(1)}, bf16[256,2048]{1,0:T(8,128)(2,1)S(1)}, u32[]{:S(2)}, u32[]{:S(2)}) %collective-permute-start.69) | collective-permute-done | bytes 1048608 | tf_op jit(solution)/shard_map/ppermute | solution.py:292
  608.4 40.4 %wgrad.13.refs_24_ = f32[2048,6144]{1,0:T(8,128)} custom-call(bf16[2,2048,256]{2,1,0:T(8,128)(2,1)} %copy-done.4, bf16[2,2048,256]{2,1,0:T(8,128)(2,1)} %copy-done.5, bf16[2,2048,256]{2,1,0:T(8,128)(2,1)} %collective-permute-done.2.refs_2_, bf16[2,2048,256]{2,1,0:T(8,128)(2,1)} %collective-permute-done.3.refs_3_, ...), custom_call_target="tpu_custom_call", output_to_operand_aliasing={{}: (24, {})} | custom-call | flops 25769803776 | bytes 80000000 | tf_op jit(solution)/shard_map/wgrad/pallas_call | solution.py:269
  655.2 31.9 %collective-permute-done.47.refs_2_ = bf16[2,64,2048]{2,1,0:T(8,128)(2,1)S(1)} collective-permute-done((bf16[2,64,2048]{2,1,0:T(8,128)(2,1)}, bf16[2,64,2048]{2,1,0:T(8,128)(2,1)S(1)}, u32[]{:S(2)}, u32[]{:S(2)}) %collective-permute-start.47) | collective-permute-done | bytes 524320 | tf_op jit(solution)/shard_map/ppermute | solution.py:292
  688.2 40.6 %wgrad.14.refs_24_ = f32[2048,6144]{1,0:T(8,128)} custom-call(bf16[2,2048,256]{2,1,0:T(8,128)(2,1)} %copy-done.4, bf16[2,2048,256]{2,1,0:T(8,128)(2,1)} %copy-done.5, bf16[2,2048,256]{2,1,0:T(8,128)(2,1)} %collective-permute-done.2.refs_2_, bf16[2,2048,256]{2,1,0:T(8,128)(2,1)} %collective-permute-done.3.refs_3_, ...), custom_call_target="tpu_custom_call", output_to_operand_aliasing={{}: (24, {})} | custom-call | flops 25769803776 | bytes 80000000 | tf_op jit(solution)/shard_map/wgrad/pallas_call | solution.py:269
  734.8 40.4 %wgrad.15 = f32[2048,6144]{1,0:T(8,128)} custom-call(bf16[2,2048,256]{2,1,0:T(8,128)(2,1)} %copy-done.4, bf16[2,2048,256]{2,1,0:T(8,128)(2,1)} %copy-done.5, bf16[2,2048,256]{2,1,0:T(8,128)(2,1)} %collective-permute-done.2.refs_2_, bf16[2,2048,256]{2,1,0:T(8,128)(2,1)} %collective-permute-done.3.refs_3_, ...), custom_call_target="tpu_custom_call", output_to_operand_aliasing={{}: (24, {})} | custom-call | flops 25769803776 | bytes 80000000 | tf_op jit(solution)/shard_map/wgrad/pallas_call | solution.py:269
  (283 shorter events, 102.6 us)
Async XLA Ops:
  5.5 59.2 %all-to-all-start = ((bf16[8,128,2048]{2,1,0:T(8,128)(2,1)}), bf16[8,128,2048]{2,1,0:T(8,128)(2,1)}, u32[]{:S(2)}, u32[]{:S(2)}) async-start(bf16[8,128,2048]{2,1,0:T(8,128)(2,1)} %pad_maximum_fusion), calls=%async_computation | async-start | bytes 8388608 | tf_op jit(solution)/shard_map/all_to_all | solution.py:297
  177.9 47.2 %collective-permute-start.13 = (bf16[256,2048]{1,0:T(8,128)(2,1)}, bf16[256,2048]{1,0:T(8,128)(2,1)S(1)}, u32[]{:S(2)}, u32[]{:S(2)}) collective-permute-start(bf16[256,2048]{1,0:T(8,128)(2,1)} %get-tuple-element.98.refs_5_), channel_id=1, source_target_pairs={{0,2},{1,3},{2,0},{3,1},{4,6},{5,7},{6,4},{7,5},{8,10},{9,11},{10,... | collective-permute-start | bytes 3145736 | tf_op jit(solution)/shard_map/ppermute | solution.py:292
  179.4 70.0 %collective-permute-start.20 = (bf16[2,2048,256]{2,1,0:T(8,128)(2,1)}, bf16[2,2048,256]{2,1,0:T(8,128)(2,1)S(1)}, u32[]{:S(2)}, u32[]{:S(2)}) collective-permute-start(bf16[2,2048,256]{2,1,0:T(8,128)(2,1)} %get-tuple-element.88.refs_0_), channel_id=1, source_target_pairs={{0,1},{1,0},{2,3},{3,2},{4,5},{5,4},{6,7},{7,6},{8,9},{9,8},{10,11... | collective-permute-start | bytes 6291464 | tf_op jit(solution)/shard_map/ppermute | solution.py:292
  180.9 70.0 %collective-permute-start.21 = (bf16[2,2048,256]{2,1,0:T(8,128)(2,1)}, bf16[2,2048,256]{2,1,0:T(8,128)(2,1)S(1)}, u32[]{:S(2)}, u32[]{:S(2)}) collective-permute-start(bf16[2,2048,256]{2,1,0:T(8,128)(2,1)} %get-tuple-element.89.refs_1_), channel_id=1, source_target_pairs={{0,1},{1,0},{2,3},{3,2},{4,5},{5,4},{6,7},{7,6},{8,9},{9,8},{10,11... | collective-permute-start | bytes 6291464 | tf_op jit(solution)/shard_map/ppermute | solution.py:292
  182.6 87.5 %collective-permute-start = (bf16[2,2048,256]{2,1,0:T(8,128)(2,1)}, bf16[2,2048,256]{2,1,0:T(8,128)(2,1)S(1)}, u32[]{:S(2)}, u32[]{:S(2)}) collective-permute-start(bf16[2,2048,256]{2,1,0:T(8,128)(2,1)} %get-tuple-element.88.refs_0_), channel_id=1, source_target_pairs={{0,2},{1,3},{2,0},{3,1},{4,6},{5,7},{6,4},{7,5},{8,10},{9,11},{10,... | collective-permute-start | bytes 6291464 | tf_op jit(solution)/shard_map/ppermute | solution.py:292
  226.4 88.6 %collective-permute-start.1 = (bf16[2,2048,256]{2,1,0:T(8,128)(2,1)}, bf16[2,2048,256]{2,1,0:T(8,128)(2,1)S(1)}, u32[]{:S(2)}, u32[]{:S(2)}) collective-permute-start(bf16[2,2048,256]{2,1,0:T(8,128)(2,1)} %get-tuple-element.89.refs_1_), channel_id=1, source_target_pairs={{0,2},{1,3},{2,0},{3,1},{4,6},{5,7},{6,4},{7,5},{8,10},{9,11},{10,... | collective-permute-start | bytes 6291464 | tf_op jit(solution)/shard_map/ppermute | solution.py:292
  248.9 66.7 %collective-permute-start.2 = (bf16[2,2048,256]{2,1,0:T(8,128)(2,1)}, bf16[2,2048,256]{2,1,0:T(8,128)(2,1)}, u32[]{:S(2)}, u32[]{:S(2)}) collective-permute-start(bf16[2,2048,256]{2,1,0:T(8,128)(2,1)} %get-tuple-element.88.refs_0_), channel_id=1, source_target_pairs={{0,4},{1,5},{2,6},{3,7},{4,0},{5,1},{6,2},{7,3},{8,12},{9,13},{10,... | collective-permute-start | bytes 6291464 | tf_op jit(solution)/shard_map/ppermute | solution.py:292
  249.5 93.2 %collective-permute-start.3 = (bf16[2,2048,256]{2,1,0:T(8,128)(2,1)}, bf16[2,2048,256]{2,1,0:T(8,128)(2,1)}, u32[]{:S(2)}, u32[]{:S(2)}) collective-permute-start(bf16[2,2048,256]{2,1,0:T(8,128)(2,1)} %get-tuple-element.89.refs_1_), channel_id=1, source_target_pairs={{0,4},{1,5},{2,6},{3,7},{4,0},{5,1},{6,2},{7,3},{8,12},{9,13},{10,... | collective-permute-start | bytes 6291464 | tf_op jit(solution)/shard_map/ppermute | solution.py:292
  250.9 92.4 %collective-permute-start.16 = (bf16[256,2048]{1,0:T(8,128)(2,1)}, bf16[256,2048]{1,0:T(8,128)(2,1)}, u32[]{:S(2)}, u32[]{:S(2)}) collective-permute-start(bf16[256,2048]{1,0:T(8,128)(2,1)} %get-tuple-element.99.refs_4_), channel_id=1, source_target_pairs={{0,2},{1,3},{2,0},{3,1},{4,6},{5,7},{6,4},{7,5},{8,10},{9,11},{10,... | collective-permute-start | bytes 3145736 | tf_op jit(solution)/shard_map/ppermute | solution.py:292
  270.1 89.9 %collective-permute-start.17 = (bf16[256,2048]{1,0:T(8,128)(2,1)}, bf16[256,2048]{1,0:T(8,128)(2,1)S(1)}, u32[]{:S(2)}, u32[]{:S(2)}) collective-permute-start(bf16[256,2048]{1,0:T(8,128)(2,1)} %get-tuple-element.100.refs_5_), channel_id=1, source_target_pairs={{0,2},{1,3},{2,0},{3,1},{4,6},{5,7},{6,4},{7,5},{8,10},{9,11},{10,... | collective-permute-start | bytes 3145736 | tf_op jit(solution)/shard_map/ppermute | solution.py:292
  315.0 82.3 %collective-permute-start.18 = (bf16[256,2048]{1,0:T(8,128)(2,1)}, bf16[256,2048]{1,0:T(8,128)(2,1)}, u32[]{:S(2)}, u32[]{:S(2)}) collective-permute-start(bf16[256,2048]{1,0:T(8,128)(2,1)} %get-tuple-element.99.refs_4_), channel_id=1, source_target_pairs={{0,4},{1,5},{2,6},{3,7},{4,0},{5,1},{6,2},{7,3},{8,12},{9,13},{10,... | collective-permute-start | bytes 3145736 | tf_op jit(solution)/shard_map/ppermute | solution.py:292
  315.6 82.3 %collective-permute-start.19 = (bf16[256,2048]{1,0:T(8,128)(2,1)}, bf16[256,2048]{1,0:T(8,128)(2,1)}, u32[]{:S(2)}, u32[]{:S(2)}) collective-permute-start(bf16[256,2048]{1,0:T(8,128)(2,1)} %get-tuple-element.100.refs_5_), channel_id=1, source_target_pairs={{0,4},{1,5},{2,6},{3,7},{4,0},{5,1},{6,2},{7,3},{8,12},{9,13},{10,... | collective-permute-start | bytes 3145736 | tf_op jit(solution)/shard_map/ppermute | solution.py:292
  342.6 56.7 %collective-permute-start.65 = (bf16[256,2048]{1,0:T(8,128)(2,1)}, bf16[256,2048]{1,0:T(8,128)(2,1)S(1)}, u32[]{:S(2)}, u32[]{:S(2)}) collective-permute-start(bf16[256,2048]{1,0:T(8,128)(2,1)} %get-tuple-element.126.refs_4_), channel_id=1, source_target_pairs={{0,2},{1,3},{2,0},{3,1},{4,6},{5,7},{6,4},{7,5},{8,10},{9,11},{10,... | collective-permute-start | bytes 3145736 | tf_op jit(solution)/shard_map/ppermute | solution.py:292
  343.3 66.6 %collective-permute-start.67 = (bf16[256,2048]{1,0:T(8,128)(2,1)}, bf16[256,2048]{1,0:T(8,128)(2,1)S(1)}, u32[]{:S(2)}, u32[]{:S(2)}) collective-permute-start(bf16[256,2048]{1,0:T(8,128)(2,1)} %get-tuple-element.126.refs_4_), channel_id=1, source_target_pairs={{0,4},{1,5},{2,6},{3,7},{4,0},{5,1},{6,2},{7,3},{8,12},{9,13},{10,... | collective-permute-start | bytes 3145736 | tf_op jit(solution)/shard_map/ppermute | solution.py:292
  397.9 53.6 %collective-permute-start.30 = (bf16[256,2048]{1,0:T(8,128)(2,1)}, bf16[256,2048]{1,0:T(8,128)(2,1)S(1)}, u32[]{:S(2)}, u32[]{:S(2)}) collective-permute-start(bf16[256,2048]{1,0:T(8,128)(2,1)} %copy-done.45), channel_id=1, source_target_pairs={{0,4},{1,5},{2,6},{3,7},{4,0},{5,1},{6,2},{7,3},{8,12},{9,13},{10,... | collective-permute-start | bytes 3145736 | tf_op jit(solution)/shard_map/ppermute | solution.py:292
  399.4 52.2 %collective-permute-start.31 = (bf16[256,2048]{1,0:T(8,128)(2,1)}, bf16[256,2048]{1,0:T(8,128)(2,1)S(1)}, u32[]{:S(2)}, u32[]{:S(2)}) collective-permute-start(bf16[256,2048]{1,0:T(8,128)(2,1)} %copy-done.48), channel_id=1, source_target_pairs={{0,2},{1,3},{2,0},{3,1},{4,6},{5,7},{6,4},{7,5},{8,10},{9,11},{10,... | collective-permute-start | bytes 3145736 | tf_op jit(solution)/shard_map/ppermute | solution.py:292
  405.0 47.1 %collective-permute-start.32 = (bf16[256,2048]{1,0:T(8,128)(2,1)}, bf16[256,2048]{1,0:T(8,128)(2,1)S(1)}, u32[]{:S(2)}, u32[]{:S(2)}) collective-permute-start(bf16[256,2048]{1,0:T(8,128)(2,1)} %copy-done.45), channel_id=1, source_target_pairs={{0,1},{1,0},{2,3},{3,2},{4,5},{5,4},{6,7},{7,6},{8,9},{9,8},{10,11... | collective-permute-start | bytes 3145736 | tf_op jit(solution)/shard_map/ppermute | solution.py:292
  451.5 48.0 %collective-permute-start.4 = (bf16[2,2048,256]{2,1,0:T(8,128)(2,1)S(1)}, bf16[2,2048,256]{2,1,0:T(8,128)(2,1)S(1)}, u32[]{:S(2)}, u32[]{:S(2)}) collective-permute-start(bf16[2,2048,256]{2,1,0:T(8,128)(2,1)S(1)} %collective-permute-done.refs_0_), channel_id=1, source_target_pairs={{0,4},{1,5},{2,6},{3,7},{4,0},{5,1},{6,2},{7,3},{8,12},{9,13},{10,... | collective-permute-start | bytes 6291464 | tf_op jit(solution)/shard_map/ppermute | solution.py:292
  452.1 47.9 %collective-permute-start.5 = (bf16[2,2048,256]{2,1,0:T(8,128)(2,1)}, bf16[2,2048,256]{2,1,0:T(8,128)(2,1)S(1)}, u32[]{:S(2)}, u32[]{:S(2)}) collective-permute-start(bf16[2,2048,256]{2,1,0:T(8,128)(2,1)} %collective-permute-done.3.refs_3_), channel_id=1, source_target_pairs={{0,2},{1,3},{2,0},{3,1},{4,6},{5,7},{6,4},{7,5},{8,10},{9,11},{10,... | collective-permute-start | bytes 6291464 | tf_op jit(solution)/shard_map/ppermute | solution.py:292
  502.1 52.5 %collective-permute-start.53 = (bf16[256,2048]{1,0:T(8,128)(2,1)}, bf16[256,2048]{1,0:T(8,128)(2,1)}, u32[]{:S(2)}, u32[]{:S(2)}) collective-permute-start(bf16[256,2048]{1,0:T(8,128)(2,1)} %get-tuple-element.120.refs_4_), channel_id=1, source_target_pairs={{0,2},{1,3},{2,0},{3,1},{4,6},{5,7},{6,4},{7,5},{8,10},{9,11},{10,... | collective-permute-start | bytes 3145736 | tf_op jit(solution)/shard_map/ppermute | solution.py:292
  502.8 54.1 %collective-permute-start.55 = (bf16[256,2048]{1,0:T(8,128)(2,1)}, bf16[256,2048]{1,0:T(8,128)(2,1)S(1)}, u32[]{:S(2)}, u32[]{:S(2)}) collective-permute-start(bf16[256,2048]{1,0:T(8,128)(2,1)} %get-tuple-element.120.refs_4_), channel_id=1, source_target_pairs={{0,4},{1,5},{2,6},{3,7},{4,0},{5,1},{6,2},{7,3},{8,12},{9,13},{10,... | collective-permute-start | bytes 3145736 | tf_op jit(solution)/shard_map/ppermute | solution.py:292
  504.2 52.0 %collective-permute-start.54 = (bf16[256,2048]{1,0:T(8,128)(2,1)S(1)}, bf16[256,2048]{1,0:T(8,128)(2,1)S(1)}, u32[]{:S(2)}, u32[]{:S(2)}) collective-permute-start(bf16[256,2048]{1,0:T(8,128)(2,1)S(1)} %copy-done.17), channel_id=1, source_target_pairs={{0,2},{1,3},{2,0},{3,1},{4,6},{5,7},{6,4},{7,5},{8,10},{9,11},{10,... | collective-permute-start | bytes 3145736 | tf_op jit(solution)/shard_map/ppermute | solution.py:292
  507.0 50.0 %collective-permute-start.56 = (bf16[256,2048]{1,0:T(8,128)(2,1)S(1)}, bf16[256,2048]{1,0:T(8,128)(2,1)}, u32[]{:S(2)}, u32[]{:S(2)}) collective-permute-start(bf16[256,2048]{1,0:T(8,128)(2,1)S(1)} %copy-done.17), channel_id=1, source_target_pairs={{0,4},{1,5},{2,6},{3,7},{4,0},{5,1},{6,2},{7,3},{8,12},{9,13},{10,... | collective-permute-start | bytes 3145736 | tf_op jit(solution)/shard_map/ppermute | solution.py:292
  654.9 76.1 %collective-permute-start.62 = (bf16[256,2048]{1,0:T(8,128)(2,1)}, bf16[256,2048]{1,0:T(8,128)(2,1)}, u32[]{:S(2)}, u32[]{:S(2)}) collective-permute-start(bf16[256,2048]{1,0:T(8,128)(2,1)} %collective-permute-done.56.refs_15_), channel_id=1, source_target_pairs={{0,1},{1,0},{2,3},{3,2},{4,5},{5,4},{6,7},{7,6},{8,9},{9,8},{10,11... | collective-permute-start | bytes 3145736 | tf_op jit(solution)/shard_map/ppermute | solution.py:292
  (118 other events, 3967.9 us)

commit v5 on v4

--- a/solution.py
+++ b/solution.py
@@ -310,8 +310,9 @@
         def far(part, deps=()):
             part = after(part, deps)
             diag = [shift(part[0], 4), shift(part[3], 2)]
-            every = list(part) + diag
-            return every + [shift(t, 1) for t in every]
+            across = [shift(t, 1) for t in part]
+            across += [shift(t, 1) for t in diag]
+            return list(part) + diag + across
 
         p_ab = (pair_a, pair_b)
         p_part, p_own = near(p_ab), own(p_ab)
@@ -332,21 +333,28 @@
         o_rest = far(o_part, (g_wqkv, g_wout))
         gg2 = shift(gg, 2)
         q_part = near(after(q_ab, o_part))
-        k_part = near(after(k_ab, o_part))
+        back = list(back)
+        early = (2, 4)
+        for m in early:
+            back[m] = shift(after(back[m], o_part), m)
         g_wout = grad_call(p_rest, o_rest, 1, hidden, 0, g_wout, flip=True, add=True)
         gg, gg2 = after((gg, gg2), g_wout)
         gg = gg + gg2
         q_rest = far(q_part, (g_wout,))
         gg4 = shift(gg, 4)
-        v_part = near(after(v_ab, q_part))
-        k_rest = far(k_part, (g_wout,))
+        k_part = near(after(k_ab, g_wout))
+        v_part = near(after(v_ab, k_part))
         g_wqkv = grad_call(p_rest, q_rest, 0, cols, 0, g_wqkv, add=True)
         gg, gg4 = after((gg, gg4), g_wqkv)
         g_gain = (gg + gg4)[0]
+        k_rest = far(k_part, (g_wqkv,))
+        g_wqkv = grad_call(p_rest, k_rest, 0, cols, width, g_wqkv, add=True)
         v_rest = far(v_part, (g_wqkv,))
-        back = [back[0]] + [shift(t, m + 1) for m, t in enumerate(after(back[1:], g_wqkv))]
-        g_wqkv = grad_call(p_rest, k_rest, 0, cols, width, g_wqkv, add=True)
-        g_wqkv = grad_call(p_rest, v_rest, 0, cols, 2 * width, g_wqkv, add=True)
+        for m in range(1, n_dev):
+            if m not in early:
+                back[m] = shift(after(back[m], g_wqkv), m)
+        g_wqkv = grad_call(p_rest[:4], v_part, 0, cols, 2 * width, g_wqkv, add=True)
+        g_wqkv = grad_call(p_rest[4:], v_rest[4:], 0, cols, 2 * width, g_wqkv, add=True)
         y_out, grad_x = join_call(*after((me, back), g_wqkv))
         return y_out, grad_x, g_gain, g_wqkv, g_wout
 

time: 781 us -> 705 us (0.903)
  waiting for transfers between devices: 323 us -> 232 us
  Pallas kernels: 342 us -> 354 us
    ppermute x80, waiting for transfers between devices: 323 us -> 232 us  [shift(): return lax.ppermute(t, 'cp', [(i, i ^ bit) for i in range(n_dev)])]
    pallas_call x8 -> x9, Pallas kernels: 238 us -> 250 us  [grad_call(): pl.pallas_call(functools.partial(grad_kernel, count, flip, add), grid=(ro...]
  transfers between devices with their start and end apart: 81 -> 81, of which waited for: 34 -> 33; matrix products, arithmetic and copies ran while one was open for 0% -> 1% of each run, Pallas kernels for 31% -> 36%
where the time goes in v5:
time: 705 us; the launch traced here: 704 us
  Pallas kernels  354 us (50%)
  waiting for transfers between devices  232 us (33%)
  starting transfers between devices  51.7 us (7%)
  blocking collectives  49.8 us (7%)
  other arithmetic  8.07 us (1%)
    pallas_call x9, Pallas kernels, grad_call(): pl.pallas_call(functools.partial(grad_kernel, count, flip, add), grid=(ro...  250 us
    ppermute x80, waiting for transfers between devices, shift(): return lax.ppermute(t, 'cp', [(i, i ^ bit) for i in range(n_dev)])  232 us
    pallas_call x1, Pallas kernels, block_call(): pl.pallas_call(functools.partial(block_kernel, scale), grid=(steps,), in_...  95.5 us
    unnamed x1, blocking collectives  49.8 us
    ppermute x80, starting transfers between devices, shift(): return lax.ppermute(t, 'cp', [(i, i ^ bit) for i in range(n_dev)])  46.1 us
  transfers between devices with their start and end apart: 81, of which 33 were waited for; matrix products, arithmetic and copies ran while one was open for 1% of the time, Pallas kernels for 36%

profile of v5, /device:TPU:0, one launch (start us, length us, event | category | flops | bytes accessed | tf_op | source)
XLA Modules:
  0.0 703.6 jit_solution(18108173085168282349)
XLA Ops:
  0.6 4.8 pad_maximum_fusion
  5.5 5.6 all-to-all-start
  12.5 49.8 %all-reduce = s32[512]{0:T(512)S(1)} all-reduce(s32[512]{0:T(512)S(1)} %dynamic-update-slice), channel_id=1, replica_groups=mesh['dp'=2,'cp'=8] {'cp'}, use_global_device_ids=true, to_apply=%add | all-reduce | flops 512 | bytes 4096
  64.7 6.1 norm.1
  73.5 95.5 %block.1 = (f32[1,2048]{1,0:T(1,128)}, bf16[256,2048]{1,0:T(8,128)(2,1)}, bf16[256,2048]{1,0:T(8,128)(2,1)}, bf16[256,2048]{1,0:T(8,128)(2,1)}, bf16[256,2048]{1...) custom-call(s32[1]{0:T(128)} %bitcast.me_ref, ...), custom_call_target="tpu_custom_call" | custom-call | flops 60000002048 | bytes 60000000 | tf_op jit(solution)/shard_map/block/pallas_call | solution.py:155
  175.1 7.4 %collective-permute-done.21.refs_7_ = bf16[256,2048]{1,0:T(8,128)(2,1)S(1)} collective-permute-done((bf16[256,2048]{1,0:T(8,128)(2,1)}, bf16[256,2048]{1,0:T(8,128)(2,1)S(1)}, u32[]{:S(2)}, u32[]{:S(2)}) %collective-permute-start.21) | collective-permute-done | bytes 1048608 | tf_op jit(solution)/shard_map/ppermute | solution.py:292
  187.8 18.1 %wgrad.9.refs_8_ = f32[2048,6144]{1,0:T(8,128)} custom-call(bf16[2,2048,256]{2,1,0:T(8,128)(2,1)} %get-tuple-element.82.refs_0_, bf16[2,2048,256]{2,1,0:T(8,128)(2,1)} %get-tuple-element.83.refs_1_, bf16[2,2048,256]{2,1,0:T(8,128)(2,1)} %copy-done.14, bf16[2,2048,256]{2,1,0:T(8,128)(2,1)} %copy-done.15, bf16[256,2048]{1,0:T(8,128)(2,1)} %get-tuple-element.103.refs_4_, ...), custom_call_target="tpu_custom_call" | custom-call | flops 8589934592 | bytes 80000000 | tf_op jit(solution)/shard_map/wgrad/pallas_call | solution.py:269
  205.9 2.9 collective-permute-done.12.refs_12_
  211.4 19.9 %wgrad.12.refs_24_ = f32[2048,2048]{1,0:T(8,128)} custom-call(bf16[2,2048,256]{2,1,0:T(8,128)(2,1)} %get-tuple-element.82.refs_0_, bf16[2,2048,256]{2,1,0:T(8,128)(2,1)} %get-tuple-element.83.refs_1_, bf16[2,2048,256]{2,1,0:T(8,128)(2,1)} %copy-done.14, bf16[2,2048,256]{2,1,0:T(8,128)(2,1)} %copy-done.15, bf16[256,2048]{1,0:T(8,128)(2,1)} %get-tuple-element.91.refs_4_, ...), custom_call_target="tpu_custom_call" | custom-call | flops 8589934592 | bytes 80000000 | tf_op jit(solution)/shard_map/wgrad/pallas_call | solution.py:269
  233.3 18.1 %wgrad.10.refs_8_ = f32[2048,6144]{1,0:T(8,128)} custom-call(bf16[2,2048,256]{2,1,0:T(8,128)(2,1)} %get-tuple-element.82.refs_0_, bf16[2,2048,256]{2,1,0:T(8,128)(2,1)} %get-tuple-element.83.refs_1_, bf16[2,2048,256]{2,1,0:T(8,128)(2,1)} %copy-done.14, bf16[2,2048,256]{2,1,0:T(8,128)(2,1)} %copy-done.15, ...), custom_call_target="tpu_custom_call", output_to_operand_aliasing={{}: (8, {})} | custom-call | flops 8589934592 | bytes 80000000 | tf_op jit(solution)/shard_map/wgrad/pallas_call | solution.py:269
  251.4 18.1 %wgrad.11.refs_24_ = f32[2048,6144]{1,0:T(8,128)} custom-call(bf16[2,2048,256]{2,1,0:T(8,128)(2,1)} %get-tuple-element.82.refs_0_, bf16[2,2048,256]{2,1,0:T(8,128)(2,1)} %get-tuple-element.83.refs_1_, bf16[2,2048,256]{2,1,0:T(8,128)(2,1)} %copy-done.14, bf16[2,2048,256]{2,1,0:T(8,128)(2,1)} %copy-done.15, ...), custom_call_target="tpu_custom_call", output_to_operand_aliasing={{}: (8, {})} | custom-call | flops 8589934592 | bytes 80000000 | tf_op jit(solution)/shard_map/wgrad/pallas_call | solution.py:269
  269.5 54.6 %collective-permute-done.15.refs_15_ = bf16[256,2048]{1,0:T(8,128)(2,1)} collective-permute-done((bf16[256,2048]{1,0:T(8,128)(2,1)S(1)}, bf16[256,2048]{1,0:T(8,128)(2,1)}, u32[]{:S(2)}, u32[]{:S(2)}) %collective-permute-start.15) | collective-permute-done | bytes 1048608 | tf_op jit(solution)/shard_map/ppermute | solution.py:292
  326.6 20.0 %collective-permute-done.26.refs_16_ = bf16[256,2048]{1,0:T(8,128)(2,1)S(1)} collective-permute-done((bf16[256,2048]{1,0:T(8,128)(2,1)}, bf16[256,2048]{1,0:T(8,128)(2,1)S(1)}, u32[]{:S(2)}, u32[]{:S(2)}) %collective-permute-start.26) | collective-permute-done | bytes 1048608 | tf_op jit(solution)/shard_map/ppermute | solution.py:292
  350.7 5.1 collective-permute-done.32.refs_22_
  357.4 37.3 %collective-permute-done.4.refs_4_.refs_0_ = bf16[2,2048,256]{2,1,0:T(8,128)(2,1)S(1)} collective-permute-done((bf16[2,2048,256]{2,1,0:T(8,128)(2,1)S(1)}, bf16[2,2048,256]{2,1,0:T(8,128)(2,1)S(1)}, u32[]{:S(2)}, u32[]{:S(2)}) %collective-permute-start.4) | collective-permute-done | bytes 2097184 | tf_op jit(solution)/shard_map/ppermute | solution.py:292
  405.2 42.7 %wgrad.13 = f32[2048,2048]{1,0:T(8,128)} custom-call(bf16[2,2048,256]{2,1,0:T(8,128)(2,1)} %copy-done.4, bf16[2,2048,256]{2,1,0:T(8,128)(2,1)} %copy-done.5, bf16[2,2048,256]{2,1,0:T(8,128)(2,1)} %copy-done.6, bf16[2,2048,256]{2,1,0:T(8,128)(2,1)} %collective-permute-done.3.refs_3_, ...), custom_call_target="tpu_custom_call", output_to_operand_aliasing={{}: (24, {})} | custom-call | flops 25769803776 | bytes 80000000 | tf_op jit(solution)/shard_map/wgrad/pallas_call | solution.py:269
  453.4 20.1 %collective-permute-done.42.refs_16_ = bf16[256,2048]{1,0:T(8,128)(2,1)S(1)} collective-permute-done((bf16[256,2048]{1,0:T(8,128)(2,1)}, bf16[256,2048]{1,0:T(8,128)(2,1)S(1)}, u32[]{:S(2)}, u32[]{:S(2)}) %collective-permute-start.42) | collective-permute-done | bytes 1048608 | tf_op jit(solution)/shard_map/ppermute | solution.py:292
  479.5 40.4 %wgrad.14.refs_24_ = f32[2048,6144]{1,0:T(8,128)} custom-call(bf16[2,2048,256]{2,1,0:T(8,128)(2,1)} %copy-done.4, bf16[2,2048,256]{2,1,0:T(8,128)(2,1)} %copy-done.5, bf16[2,2048,256]{2,1,0:T(8,128)(2,1)} %copy-done.6, bf16[2,2048,256]{2,1,0:T(8,128)(2,1)} %collective-permute-done.3.refs_3_, ...), custom_call_target="tpu_custom_call", output_to_operand_aliasing={{}: (24, {})} | custom-call | flops 25769803776 | bytes 80000000 | tf_op jit(solution)/shard_map/wgrad/pallas_call | solution.py:269
  527.1 21.8 %collective-permute-done.78 = f32[1,2048]{1,0:T(1,128)S(1)} collective-permute-done((f32[1,2048]{1,0:T(1,128)S(1)}, f32[1,2048]{1,0:T(1,128)S(1)}, u32[]{:S(2)}, u32[]{:S(2)}) %collective-permute-start.78) | collective-permute-done | bytes 8224 | tf_op jit(solution)/shard_map/ppermute | solution.py:292
  559.9 40.4 %wgrad.15.refs_8_ = f32[2048,6144]{1,0:T(8,128)} custom-call(bf16[2,2048,256]{2,1,0:T(8,128)(2,1)} %copy-done.4, bf16[2,2048,256]{2,1,0:T(8,128)(2,1)} %copy-done.5, bf16[2,2048,256]{2,1,0:T(8,128)(2,1)} %copy-done.6, bf16[2,2048,256]{2,1,0:T(8,128)(2,1)} %collective-permute-done.3.refs_3_, ...), custom_call_target="tpu_custom_call", output_to_operand_aliasing={{}: (24, {})} | custom-call | flops 25769803776 | bytes 80000000 | tf_op jit(solution)/shard_map/wgrad/pallas_call | solution.py:269
  607.1 32.4 %collective-permute-done.59.refs_2_ = bf16[2,64,2048]{2,1,0:T(8,128)(2,1)S(1)} collective-permute-done((bf16[2,64,2048]{2,1,0:T(8,128)(2,1)}, bf16[2,64,2048]{2,1,0:T(8,128)(2,1)S(1)}, u32[]{:S(2)}, u32[]{:S(2)}) %collective-permute-start.59) | collective-permute-done | bytes 524320 | tf_op jit(solution)/shard_map/ppermute | solution.py:292
  641.4 22.3 %wgrad.16.refs_16_ = f32[2048,6144]{1,0:T(8,128)} custom-call(bf16[2,2048,256]{2,1,0:T(8,128)(2,1)} %copy-done.4, bf16[2,2048,256]{2,1,0:T(8,128)(2,1)} %copy-done.5, bf16[2,2048,256]{2,1,0:T(8,128)(2,1)} %copy-done.6, bf16[2,2048,256]{2,1,0:T(8,128)(2,1)} %collective-permute-done.3.refs_3_, ...), custom_call_target="tpu_custom_call", output_to_operand_aliasing={{}: (8, {})} | custom-call | flops 8589934592 | bytes 80000000 | tf_op jit(solution)/shard_map/wgrad/pallas_call | solution.py:269
  668.0 30.4 %wgrad.17 = f32[2048,6144]{1,0:T(8,128)} custom-call(bf16[2,2048,256]{2,1,0:T(8,128)(2,1)} %copy-done.7, bf16[2,2048,256]{2,1,0:T(8,128)(2,1)} %copy-done.8, bf16[2,2048,256]{2,1,0:T(8,128)(2,1)} %copy-done.9, bf16[2,2048,256]{2,1,0:T(8,128)(2,1)} %copy-done.10, bf16[2,2048,256]{2,1,0:T(8,128)(2,1)} %copy-done.11, ...), custom_call_target="tpu_custom_call", output_to_operand_aliasing={{}: (16, {})} | custom-call | flops 17179869184 | bytes 80000000 | tf_op jit(solution)/shard_map/wgrad/pallas_call | solution.py:269
  698.4 2.8 collective-permute-done.64.refs_7_
  (288 shorter events, 85.4 us)
Async XLA Ops:
  5.5 59.3 %all-to-all-start = ((bf16[8,128,2048]{2,1,0:T(8,128)(2,1)}), bf16[8,128,2048]{2,1,0:T(8,128)(2,1)}, u32[]{:S(2)}, u32[]{:S(2)}) async-start(bf16[8,128,2048]{2,1,0:T(8,128)(2,1)} %pad_maximum_fusion), calls=%async_computation | async-start | bytes 8388608 | tf_op jit(solution)/shard_map/all_to_all | solution.py:297
  185.6 45.7 %collective-permute-start.13 = (bf16[256,2048]{1,0:T(8,128)(2,1)}, bf16[256,2048]{1,0:T(8,128)(2,1)}, u32[]{:S(2)}, u32[]{:S(2)}) collective-permute-start(bf16[256,2048]{1,0:T(8,128)(2,1)} %get-tuple-element.92.refs_5_), channel_id=1, source_target_pairs={{0,2},{1,3},{2,0},{3,1},{4,6},{5,7},{6,4},{7,5},{8,10},{9,11},{10,... | collective-permute-start | bytes 3145736 | tf_op jit(solution)/shard_map/ppermute | solution.py:292
  186.3 46.5 %collective-permute-start.14 = (bf16[256,2048]{1,0:T(8,128)(2,1)}, bf16[256,2048]{1,0:T(8,128)(2,1)}, u32[]{:S(2)}, u32[]{:S(2)}) collective-permute-start(bf16[256,2048]{1,0:T(8,128)(2,1)} %get-tuple-element.91.refs_4_), channel_id=1, source_target_pairs={{0,4},{1,5},{2,6},{3,7},{4,0},{5,1},{6,2},{7,3},{8,12},{9,13},{10,... | collective-permute-start | bytes 3145736 | tf_op jit(solution)/shard_map/ppermute | solution.py:292
  208.8 115.8 %collective-permute-start = (bf16[2,2048,256]{2,1,0:T(8,128)(2,1)}, bf16[2,2048,256]{2,1,0:T(8,128)(2,1)S(1)}, u32[]{:S(2)}, u32[]{:S(2)}) collective-permute-start(bf16[2,2048,256]{2,1,0:T(8,128)(2,1)} %get-tuple-element.82.refs_0_), channel_id=1, source_target_pairs={{0,2},{1,3},{2,0},{3,1},{4,6},{5,7},{6,4},{7,5},{8,10},{9,11},{10,... | collective-permute-start | bytes 6291464 | tf_op jit(solution)/shard_map/ppermute | solution.py:292
  209.4 116.6 %collective-permute-start.1 = (bf16[2,2048,256]{2,1,0:T(8,128)(2,1)}, bf16[2,2048,256]{2,1,0:T(8,128)(2,1)S(1)}, u32[]{:S(2)}, u32[]{:S(2)}) collective-permute-start(bf16[2,2048,256]{2,1,0:T(8,128)(2,1)} %get-tuple-element.83.refs_1_), channel_id=1, source_target_pairs={{0,2},{1,3},{2,0},{3,1},{4,6},{5,7},{6,4},{7,5},{8,10},{9,11},{10,... | collective-permute-start | bytes 6291464 | tf_op jit(solution)/shard_map/ppermute | solution.py:292
  210.8 115.3 %collective-permute-start.2 = (bf16[2,2048,256]{2,1,0:T(8,128)(2,1)}, bf16[2,2048,256]{2,1,0:T(8,128)(2,1)S(1)}, u32[]{:S(2)}, u32[]{:S(2)}) collective-permute-start(bf16[2,2048,256]{2,1,0:T(8,128)(2,1)} %get-tuple-element.82.refs_0_), channel_id=1, source_target_pairs={{0,4},{1,5},{2,6},{3,7},{4,0},{5,1},{6,2},{7,3},{8,12},{9,13},{10,... | collective-permute-start | bytes 6291464 | tf_op jit(solution)/shard_map/ppermute | solution.py:292
  231.3 95.3 %collective-permute-start.3 = (bf16[2,2048,256]{2,1,0:T(8,128)(2,1)}, bf16[2,2048,256]{2,1,0:T(8,128)(2,1)}, u32[]{:S(2)}, u32[]{:S(2)}) collective-permute-start(bf16[2,2048,256]{2,1,0:T(8,128)(2,1)} %get-tuple-element.83.refs_1_), channel_id=1, source_target_pairs={{0,4},{1,5},{2,6},{3,7},{4,0},{5,1},{6,2},{7,3},{8,12},{9,13},{10,... | collective-permute-start | bytes 6291464 | tf_op jit(solution)/shard_map/ppermute | solution.py:292
  232.8 91.4 %collective-permute-start.15 = (bf16[256,2048]{1,0:T(8,128)(2,1)S(1)}, bf16[256,2048]{1,0:T(8,128)(2,1)}, u32[]{:S(2)}, u32[]{:S(2)}) collective-permute-start(bf16[256,2048]{1,0:T(8,128)(2,1)S(1)} %copy-done.49), channel_id=1, source_target_pairs={{0,4},{1,5},{2,6},{3,7},{4,0},{5,1},{6,2},{7,3},{8,12},{9,13},{10,... | collective-permute-start | bytes 3145736 | tf_op jit(solution)/shard_map/ppermute | solution.py:292
  346.9 47.8 %collective-permute-start.4 = (bf16[2,2048,256]{2,1,0:T(8,128)(2,1)S(1)}, bf16[2,2048,256]{2,1,0:T(8,128)(2,1)S(1)}, u32[]{:S(2)}, u32[]{:S(2)}) collective-permute-start(bf16[2,2048,256]{2,1,0:T(8,128)(2,1)S(1)} %collective-permute-done.refs_0_), channel_id=1, source_target_pairs={{0,4},{1,5},{2,6},{3,7},{4,0},{5,1},{6,2},{7,3},{8,12},{9,13},{10,... | collective-permute-start | bytes 6291464 | tf_op jit(solution)/shard_map/ppermute | solution.py:292
  348.4 46.8 %collective-permute-start.5 = (bf16[2,2048,256]{2,1,0:T(8,128)(2,1)}, bf16[2,2048,256]{2,1,0:T(8,128)(2,1)S(1)}, u32[]{:S(2)}, u32[]{:S(2)}) collective-permute-start(bf16[2,2048,256]{2,1,0:T(8,128)(2,1)} %collective-permute-done.3.refs_3_), channel_id=1, source_target_pairs={{0,2},{1,3},{2,0},{3,1},{4,6},{5,7},{6,4},{7,5},{8,10},{9,11},{10,... | collective-permute-start | bytes 6291464 | tf_op jit(solution)/shard_map/ppermute | solution.py:292
  350.1 45.2 %collective-permute-start.6 = (bf16[2,2048,256]{2,1,0:T(8,128)(2,1)S(1)}, bf16[2,2048,256]{2,1,0:T(8,128)(2,1)S(1)}, u32[]{:S(2)}, u32[]{:S(2)}) collective-permute-start(bf16[2,2048,256]{2,1,0:T(8,128)(2,1)S(1)} %collective-permute-done.refs_0_), channel_id=1, source_target_pairs={{0,1},{1,0},{2,3},{3,2},{4,5},{5,4},{6,7},{7,6},{8,9},{9,8},{10,11... | collective-permute-start | bytes 6291464 | tf_op jit(solution)/shard_map/ppermute | solution.py:292
  357.3 40.2 %collective-permute-start.8 = (bf16[2,2048,256]{2,1,0:T(8,128)(2,1)S(1)}, bf16[2,2048,256]{2,1,0:T(8,128)(2,1)S(1)}, u32[]{:S(2)}, u32[]{:S(2)}) collective-permute-start(bf16[2,2048,256]{2,1,0:T(8,128)(2,1)S(1)} %collective-permute-done.2.refs_2_), channel_id=1, source_target_pairs={{0,1},{1,0},{2,3},{3,2},{4,5},{5,4},{6,7},{7,6},{8,9},{9,8},{10,11... | collective-permute-start | bytes 6291464 | tf_op jit(solution)/shard_map/ppermute | solution.py:292
  395.7 52.3 %collective-permute-start.38 = (bf16[256,2048]{1,0:T(8,128)(2,1)}, bf16[256,2048]{1,0:T(8,128)(2,1)}, u32[]{:S(2)}, u32[]{:S(2)}) collective-permute-start(bf16[256,2048]{1,0:T(8,128)(2,1)} %get-tuple-element.103.refs_4_), channel_id=1, source_target_pairs={{0,2},{1,3},{2,0},{3,1},{4,6},{5,7},{6,4},{7,5},{8,10},{9,11},{10,... | collective-permute-start | bytes 3145736 | tf_op jit(solution)/shard_map/ppermute | solution.py:292
  397.5 50.6 %collective-permute-start.40 = (bf16[256,2048]{1,0:T(8,128)(2,1)}, bf16[256,2048]{1,0:T(8,128)(2,1)}, u32[]{:S(2)}, u32[]{:S(2)}) collective-permute-start(bf16[256,2048]{1,0:T(8,128)(2,1)} %get-tuple-element.103.refs_4_), channel_id=1, source_target_pairs={{0,4},{1,5},{2,6},{3,7},{4,0},{5,1},{6,2},{7,3},{8,12},{9,13},{10,... | collective-permute-start | bytes 3145736 | tf_op jit(solution)/shard_map/ppermute | solution.py:292
  399.1 48.9 %collective-permute-start.39 = (bf16[256,2048]{1,0:T(8,128)(2,1)}, bf16[256,2048]{1,0:T(8,128)(2,1)}, u32[]{:S(2)}, u32[]{:S(2)}) collective-permute-start(bf16[256,2048]{1,0:T(8,128)(2,1)} %get-tuple-element.104.refs_5_), channel_id=1, source_target_pairs={{0,2},{1,3},{2,0},{3,1},{4,6},{5,7},{6,4},{7,5},{8,10},{9,11},{10,... | collective-permute-start | bytes 3145736 | tf_op jit(solution)/shard_map/ppermute | solution.py:292
  402.1 45.9 %collective-permute-start.41 = (bf16[256,2048]{1,0:T(8,128)(2,1)}, bf16[256,2048]{1,0:T(8,128)(2,1)}, u32[]{:S(2)}, u32[]{:S(2)}) collective-permute-start(bf16[256,2048]{1,0:T(8,128)(2,1)} %get-tuple-element.104.refs_5_), channel_id=1, source_target_pairs={{0,4},{1,5},{2,6},{3,7},{4,0},{5,1},{6,2},{7,3},{8,12},{9,13},{10,... | collective-permute-start | bytes 3145736 | tf_op jit(solution)/shard_map/ppermute | solution.py:292
  474.2 45.6 %collective-permute-start.34 = (bf16[256,2048]{1,0:T(8,128)(2,1)}, bf16[256,2048]{1,0:T(8,128)(2,1)S(1)}, u32[]{:S(2)}, u32[]{:S(2)}) collective-permute-start(bf16[256,2048]{1,0:T(8,128)(2,1)} %get-tuple-element.101.refs_4_), channel_id=1, source_target_pairs={{0,2},{1,3},{2,0},{3,1},{4,6},{5,7},{6,4},{7,5},{8,10},{9,11},{10,... | collective-permute-start | bytes 3145736 | tf_op jit(solution)/shard_map/ppermute | solution.py:292
  476.0 46.3 %collective-permute-start.36 = (bf16[256,2048]{1,0:T(8,128)(2,1)}, bf16[256,2048]{1,0:T(8,128)(2,1)S(1)}, u32[]{:S(2)}, u32[]{:S(2)}) collective-permute-start(bf16[256,2048]{1,0:T(8,128)(2,1)} %get-tuple-element.101.refs_4_), channel_id=1, source_target_pairs={{0,4},{1,5},{2,6},{3,7},{4,0},{5,1},{6,2},{7,3},{8,12},{9,13},{10,... | collective-permute-start | bytes 3145736 | tf_op jit(solution)/shard_map/ppermute | solution.py:292
  477.5 44.8 %collective-permute-start.35 = (bf16[256,2048]{1,0:T(8,128)(2,1)S(1)}, bf16[256,2048]{1,0:T(8,128)(2,1)S(1)}, u32[]{:S(2)}, u32[]{:S(2)}) collective-permute-start(bf16[256,2048]{1,0:T(8,128)(2,1)S(1)} %copy-done.18), channel_id=1, source_target_pairs={{0,2},{1,3},{2,0},{3,1},{4,6},{5,7},{6,4},{7,5},{8,10},{9,11},{10,... | collective-permute-start | bytes 3145736 | tf_op jit(solution)/shard_map/ppermute | solution.py:292
  478.1 45.6 %collective-permute-start.37 = (bf16[256,2048]{1,0:T(8,128)(2,1)S(1)}, bf16[256,2048]{1,0:T(8,128)(2,1)S(1)}, u32[]{:S(2)}, u32[]{:S(2)}) collective-permute-start(bf16[256,2048]{1,0:T(8,128)(2,1)S(1)} %copy-done.18), channel_id=1, source_target_pairs={{0,4},{1,5},{2,6},{3,7},{4,0},{5,1},{6,2},{7,3},{8,12},{9,13},{10,... | collective-permute-start | bytes 3145736 | tf_op jit(solution)/shard_map/ppermute | solution.py:292
  553.6 46.7 %collective-permute-start.65 = (bf16[256,2048]{1,0:T(8,128)(2,1)S(1)}, bf16[256,2048]{1,0:T(8,128)(2,1)}, u32[]{:S(2)}, u32[]{:S(2)}) collective-permute-start(bf16[256,2048]{1,0:T(8,128)(2,1)S(1)} %copy-done.17), channel_id=1, source_target_pairs={{0,2},{1,3},{2,0},{3,1},{4,6},{5,7},{6,4},{7,5},{8,10},{9,11},{10,... | collective-permute-start | bytes 3145736 | tf_op jit(solution)/shard_map/ppermute | solution.py:292
  555.2 46.1 %collective-permute-start.67 = (bf16[256,2048]{1,0:T(8,128)(2,1)S(1)}, bf16[256,2048]{1,0:T(8,128)(2,1)S(1)}, u32[]{:S(2)}, u32[]{:S(2)}) collective-permute-start(bf16[256,2048]{1,0:T(8,128)(2,1)S(1)} %copy-done.17), channel_id=1, source_target_pairs={{0,4},{1,5},{2,6},{3,7},{4,0},{5,1},{6,2},{7,3},{8,12},{9,13},{10,... | collective-permute-start | bytes 3145736 | tf_op jit(solution)/shard_map/ppermute | solution.py:292
  556.7 44.6 %collective-permute-start.66 = (bf16[256,2048]{1,0:T(8,128)(2,1)S(1)}, bf16[256,2048]{1,0:T(8,128)(2,1)}, u32[]{:S(2)}, u32[]{:S(2)}) collective-permute-start(bf16[256,2048]{1,0:T(8,128)(2,1)S(1)} %copy-done.16), channel_id=1, source_target_pairs={{0,2},{1,3},{2,0},{3,1},{4,6},{5,7},{6,4},{7,5},{8,10},{9,11},{10,... | collective-permute-start | bytes 3145736 | tf_op jit(solution)/shard_map/ppermute | solution.py:292
  558.2 44.8 %collective-permute-start.68 = (bf16[256,2048]{1,0:T(8,128)(2,1)S(1)}, bf16[256,2048]{1,0:T(8,128)(2,1)}, u32[]{:S(2)}, u32[]{:S(2)}) collective-permute-start(bf16[256,2048]{1,0:T(8,128)(2,1)S(1)} %copy-done.16), channel_id=1, source_target_pairs={{0,4},{1,5},{2,6},{3,7},{4,0},{5,1},{6,2},{7,3},{8,12},{9,13},{10,... | collective-permute-start | bytes 3145736 | tf_op jit(solution)/shard_map/ppermute | solution.py:292
  (120 other events, 2516.9 us)
